TPU v7x, 32 devices: a whole 2x2x4 slice. The times are simulated.
32 devices in a mesh: grp: 2 (over y), seq: 4 (over z), head: 4 (over x, core).
Axes of the slice: x: 2, y: 2, z: 4, core: 2. Of those that a mesh axis runs over, the one named last changes fastest.
Arguments:
- queries: bfloat16 [1024, 32, 128], P(('grp', 'seq'), 'head'), parts along dimension 0, may hold values from -26 to 26
- keys: bfloat16 [1024, 8, 128], P(('grp', 'seq'), 'head'), parts along dimension 0, may hold values from -13 to 13
- values: bfloat16 [1024, 8, 128], P(('grp', 'seq'), 'head'), parts along dimension 0, may hold values from -6 to 6
- block_order: int32 [16], P('grp'), parts along dimension 0, may hold values from 0 to 7, as said below
Outputs:
- attended: bfloat16 [1024, 32, 128], P(('grp', 'seq'), 'head'), parts along dimension 0
There are 2 independent parts, one for each index of `grp`. A program takes and returns all parts, laid end to end along the dimension named above; each array names one. Nothing has to cross between parts.
Inputs may be any that keep to these rules, and one draw needn't show every extreme that they name: `block_order`: slots 2 i and 2 i + 1 hold blocks c and 7 - c for some c, in either order; every block stands in one slot.
All inputs are finite; a program needn't handle non-finite values.
Results may differ from a plain program's by a relative error of at most 0.0055.
Values may be sent and summed in bfloat16 or wider, within the bound.
No kernel may reach another device: no remote copies, remote signals or barrier semaphores. Data moves between devices by JAX's collectives and lax.ppermute only.
A program may use at most 128 MiB of HBM per device.

v0:
```python
import jax
import jax.numpy as jnp
from jax import lax
from jax.sharding import PartitionSpec as P


def partner(value, axis, stride):
    mask = 2**stride
    pairs = [(source, source ^ mask) for source in range(lax.axis_size(axis))]
    return lax.ppermute(value, axis, pairs)


def from_behind(value, axis, by):
    devices = lax.axis_size(axis)
    return lax.ppermute(value, axis, [(i, (i + by) % devices) for i in range(devices)])


def locate(table, start, count, half_rows):
    index = start + jnp.arange(count, dtype=jnp.int32)
    slot = index // half_rows
    match = slot[:, None] == jnp.arange(table.shape[0], dtype=jnp.int32)[None, :]
    block_id = jnp.sum(jnp.where(match, table[None, :], 0), axis=1)
    return block_id * half_rows + index % half_rows


def attend(state, query_rows, query_pos, key_rows, value_rows, key_pos, score_scale):
    running_max, running_sum, running_acc = state
    scores = (
        jnp.einsum("cghd,pgd->ghcp", query_rows, key_rows, preferred_element_type=jnp.float32)
        * score_scale
    )
    visible = (key_pos[None, :] <= query_pos[:, None])[None, None]
    new_max = jnp.maximum(running_max, jnp.max(jnp.where(visible, scores, -1e30), axis=-1))
    weights = jnp.where(visible, jnp.exp(scores - new_max[..., None]), 0.0)
    factor = jnp.exp(running_max - new_max)
    new_sum = running_sum * factor + jnp.sum(weights, axis=-1)
    product = jnp.einsum(
        "ghcp,pgd->ghcd",
        weights.astype(jnp.bfloat16),
        value_rows,
        preferred_element_type=jnp.float32,
    )
    new_acc = running_acc * factor[..., None] + product
    return (new_max, new_sum, new_acc)


def finish(state, half_rows):
    running_max, running_sum, running_acc = state
    result = running_acc / running_sum[..., None]
    groups = result.shape[0] * result.shape[1]
    return (
        jnp.transpose(result, (2, 0, 1, 3))
        .reshape(half_rows, groups, result.shape[3])
        .astype(jnp.bfloat16)
    )


def fresh_state(groups, per_group, half_rows, head_width):
    return (
        jnp.full((groups, per_group, half_rows), -1e30, jnp.float32),
        jnp.zeros((groups, per_group, half_rows), jnp.float32),
        jnp.zeros((groups, per_group, half_rows, head_width), jnp.float32),
    )


def on_device(queries, keys, values, block_order):
    tokens = queries.shape[0]
    half_rows = tokens // 2
    groups = keys.shape[1]
    per_group = queries.shape[1] // groups
    head_width = queries.shape[2]
    score_scale = head_width ** (-0.5)
    seq_index = lax.axis_index("seq")
    half_groups = groups // 2
    half_heads = half_groups * per_group
    parity = seq_index % 2
    pair_index = seq_index // 2
    pair_total = lax.axis_size("seq") // 2
    own_q = lax.dynamic_slice_in_dim(queries, parity * half_heads, half_heads, 1)
    own_k = lax.dynamic_slice_in_dim(keys, parity * half_groups, half_groups, 1)
    own_v = lax.dynamic_slice_in_dim(values, parity * half_groups, half_groups, 1)
    other_q = lax.dynamic_slice_in_dim(queries, (1 - parity) * half_heads, half_heads, 1)
    other_k = lax.dynamic_slice_in_dim(keys, (1 - parity) * half_groups, half_groups, 1)
    other_v = lax.dynamic_slice_in_dim(values, (1 - parity) * half_groups, half_groups, 1)
    got_q, got_k, got_v = partner((other_q, other_k, other_v), "seq", 0)
    lower = parity == 0
    pair_q = jnp.where(
        lower, jnp.concatenate([own_q, got_q], 0), jnp.concatenate([got_q, own_q], 0)
    )
    pair_k = jnp.where(
        lower, jnp.concatenate([own_k, got_k], 0), jnp.concatenate([got_k, own_k], 0)
    )
    pair_v = jnp.where(
        lower, jnp.concatenate([own_v, got_v], 0), jnp.concatenate([got_v, own_v], 0)
    )
    pair_rows = 2 * tokens
    split_q = pair_q.reshape(4, half_rows, half_groups, per_group, head_width)
    pair_pos = locate(block_order, pair_index * pair_rows, pair_rows, half_rows)
    query_blocks = [pair_pos[which * half_rows : (which + 1) * half_rows] for which in range(4)]

    def consume(states, key_rows, value_rows, source):
        key_pos = locate(block_order, source * pair_rows, pair_rows, half_rows)
        result = []
        for which in range(4):
            state = states[which]
            for piece in range(4):
                low = piece * half_rows
                state = attend(
                    state,
                    split_q[which],
                    query_blocks[which],
                    key_rows[low : low + half_rows],
                    value_rows[low : low + half_rows],
                    key_pos[low : low + half_rows],
                    score_scale,
                )
            result.append(state)
        return tuple(result)

    states = tuple(
        (fresh_state(half_groups, per_group, half_rows, head_width) for which in range(4))
    )
    states = consume(states, pair_k, pair_v, pair_index)

    def pass_step(step, carry):
        states, key_rows, value_rows = carry
        key_rows, value_rows = from_behind((key_rows, value_rows), "seq", 2)
        source = (pair_index - step) % pair_total
        return (consume(states, key_rows, value_rows, source), key_rows, value_rows)

    states, ignored_k, ignored_v = lax.fori_loop(1, pair_total, pass_step, (states, pair_k, pair_v))
    outputs = jnp.concatenate([finish(states[which], half_rows) for which in range(4)], axis=0)
    first_rows = outputs[:tokens]
    second_rows = outputs[tokens:]
    mine = jnp.where(lower, first_rows, second_rows)
    theirs = jnp.where(lower, second_rows, first_rows)
    returned = partner(theirs, "seq", 0)
    return jnp.where(
        lower, jnp.concatenate([mine, returned], 1), jnp.concatenate([returned, mine], 1)
    )


def solution(mesh):
    placed = (
        P(("grp", "seq"), "head", None),
        P(("grp", "seq"), "head", None),
        P(("grp", "seq"), "head", None),
        P("grp"),
    )
    return jax.shard_map(
        on_device,
        mesh=mesh,
        in_specs=placed,
        out_specs=P(("grp", "seq"), "head", None),
        check_vma=False,
    )
```

profile of v0, /device:TPU:0, one launch (start us, length us, event | category | flops | bytes accessed | tf_op | source)
XLA Modules:
  0.0 33.9 jit_solution(1314867537099419183)
XLA Ops:
  0.0 1.2 %constant_dynamic-slice_fusion.3 = (bf16[128,4,128]{2,1,0:T(4,128)(2,1)S(1)}, bf16[128,4,128]{2,1,0:T(4,128)(2,1)S(1)}) fusion(bf16[128,8,128]{2,1,0:T(8,128)(2,1)} %param.4, s32[]{:T(128)S(6)} %select_n.365, s32[]{:T(128)S(6)} %select_n.366), kind=kLoop, calls=%fused_computation.545 | loop fusion | bytes 524296 | tf_op jit(solution)/shard_map/dynamic_slice | solution.py:79
  1.2 3.1 %collective-permute-start.1 = (bf16[128,4,128]{2,0,1:T(8,128)(2,1)S(1)}, bf16[128,4,128]{2,0,1:T(8,128)(2,1)S(1)}, u32[]{:S(2)}, u32[]{:S(2)}) collective-permute-start(bf16[128,4,128]{2,0,1:T(8,128)(2,1)S(1)} %copy.118), channel_id=1, source_target_pairs={{0,4},{4,0},{8,12},{12,8},{1,5},{5,1},{9,13},{13,9},{2,6},{6,2},{1... | collective-permute-start | bytes 393224 | tf_op jit(solution)/shard_map/ppermute | solution.py:10
  4.5 0.8 %collective-permute-start = (bf16[128,1,128]{2,0,1:T(8,128)(2,1)S(1)}, bf16[128,1,128]{2,0,1:T(8,128)(2,1)S(1)}, u32[]{:S(2)}, u32[]{:S(2)}) collective-permute-start(bf16[128,1,128]{2,0,1:T(8,128)(2,1)S(1)} %copy.116), channel_id=1, source_target_pairs={{0,4},{4,0},{8,12},{12,8},{1,5},{5,1},{9,13},{13,9},{2,6},{6,2},{1... | collective-permute-start | bytes 98312 | tf_op jit(solution)/shard_map/ppermute | solution.py:10
  5.5 1.3 %collective-permute-start.2 = (bf16[128,1,128]{2,0,1:T(8,128)(2,1)S(1)}, bf16[128,1,128]{2,0,1:T(8,128)(2,1)S(1)}, u32[]{:S(2)}, u32[]{:S(2)}) collective-permute-start(bf16[128,1,128]{2,0,1:T(8,128)(2,1)S(1)} %copy.120), channel_id=1, source_target_pairs={{0,4},{4,0},{8,12},{12,8},{1,5},{5,1},{9,13},{13,9},{2,6},{6,2},{1... | collective-permute-start | bytes 98312 | tf_op jit(solution)/shard_map/ppermute | solution.py:10
  6.8 0.6 %copy-done.2 = s32[8]{0:T(128)S(1)} copy-done((s32[8]{0:T(128)S(1)}, s32[8]{0:T(128)}, u32[]{:S(2)}) %copy-start.2) | copy-done | bytes 56
  7.8 0.2 broadcast_compare_fusion.30
  8.0 0.8 %collective-permute-done = bf16[128,1,128]{2,0,1:T(8,128)(2,1)S(1)} collective-permute-done((bf16[128,1,128]{2,0,1:T(8,128)(2,1)S(1)}, bf16[128,1,128]{2,0,1:T(8,128)(2,1)S(1)}, u32[]{:S(2)}, u32[]{:S(2)}) %collective-permute-start) | collective-permute-done | bytes 32800 | tf_op jit(solution)/shard_map/ppermute | solution.py:10
  8.9 2.8 %collective-permute-start.3 = (bf16[256,1,128]{2,0,1:T(8,128)(2,1)S(1)}, bf16[256,1,128]{2,0,1:T(8,128)(2,1)S(1)}, u32[]{:S(2)}, u32[]{:S(2)}) collective-permute-start(bf16[256,1,128]{2,0,1:T(8,128)(2,1)S(1)} %maximum_select_fusion.2), channel_id=1, source_target_pairs={{0,8},{4,12},{8,0},{12,4},{1,9},{5,13},{9,1},{13,5},{2,10},{6,14},... | collective-permute-start | bytes 196616 | tf_op jit(solution)/shard_map/while/body/eval_jaxpr/ppermute | solution.py:15
  11.7 0.4 %collective-permute-start.4 = (bf16[256,1,128]{2,0,1:T(8,128)(2,1)S(1)}, bf16[256,1,128]{2,0,1:T(8,128)(2,1)S(1)}, u32[]{:S(2)}, u32[]{:S(2)}) collective-permute-start(bf16[256,1,128]{2,0,1:T(8,128)(2,1)S(1)} %maximum_select_fusion.3), channel_id=1, source_target_pairs={{0,8},{4,12},{8,0},{12,4},{1,9},{5,13},{9,1},{13,5},{2,10},{6,14},... | collective-permute-start | bytes 196616 | tf_op jit(solution)/shard_map/while/body/eval_jaxpr/ppermute | solution.py:15
  17.1 0.2 fusion.72
  17.3 0.2 fusion.70
  19.3 0.2 fusion.53
  19.5 0.2 fusion.51
  21.7 0.2 fusion.32
  21.9 0.2 fusion.30
  23.6 0.2 fusion.15
  23.8 0.2 fusion.13
  26.8 0.3 fusion.83
  27.1 0.3 fusion.82
  27.3 0.3 fusion.81
  27.6 0.3 fusion.80
  28.0 1.7 %collective-permute-start.5 = (bf16[128,4,128]{2,0,1:T(8,128)(2,1)S(1)}, bf16[128,4,128]{2,0,1:T(8,128)(2,1)S(1)}, u32[]{:S(2)}, u32[]{:S(2)}) collective-permute-start(bf16[128,4,128]{2,0,1:T(8,128)(2,1)S(1)} %get-tuple-element.137), channel_id=1, source_target_pairs={{0,4},{4,0},{8,12},{12,8},{1,5},{5,1},{9,13},{13,9},{2,6},{6,2},{1... | collective-permute-start | bytes 393224 | tf_op jit(solution)/shard_map/ppermute | solution.py:10
  29.6 3.4 %collective-permute-done.5 = bf16[128,4,128]{2,0,1:T(8,128)(2,1)S(1)} collective-permute-done((bf16[128,4,128]{2,0,1:T(8,128)(2,1)S(1)}, bf16[128,4,128]{2,0,1:T(8,128)(2,1)S(1)}, u32[]{:S(2)}, u32[]{:S(2)}) %collective-permute-start.5) | collective-permute-done | bytes 131104 | tf_op jit(solution)/shard_map/ppermute | solution.py:10
  33.0 0.9 %copy.82 = bf16[128,8,128]{2,1,0:T(8,128)(2,1)} copy(bf16[128,8,128]{2,0,1:T(8,128)(2,1)S(1)} %maximum_select_fusion.1) | data formatting | bytes 524288 | tf_op jit(solution)/shard_map/jit(_where)/select_n | solution.py:138
  (120 shorter events, 13.5 us)
Async XLA Ops:
  1.2 3.2 %copy-start = (bf16[128,2,128]{2,1,0:T(2,128)(2,1)S(1)}, bf16[128,2,128]{2,1,0:T(2,128)(2,1)}, u32[]{:S(2)}) copy-start(bf16[128,2,128]{2,1,0:T(2,128)(2,1)} %param.5) | copy-start | bytes 196612
  1.2 10.9 %collective-permute-start.1 = (bf16[128,4,128]{2,0,1:T(8,128)(2,1)S(1)}, bf16[128,4,128]{2,0,1:T(8,128)(2,1)S(1)}, u32[]{:S(2)}, u32[]{:S(2)}) collective-permute-start(bf16[128,4,128]{2,0,1:T(8,128)(2,1)S(1)} %copy.118), channel_id=1, source_target_pairs={{0,4},{4,0},{8,12},{12,8},{1,5},{5,1},{9,13},{13,9},{2,6},{6,2},{1... | collective-permute-start | bytes 393224 | tf_op jit(solution)/shard_map/ppermute | solution.py:10
  4.5 0.8 %copy-start.1 = (bf16[128,2,128]{2,1,0:T(2,128)(2,1)S(1)}, bf16[128,2,128]{2,1,0:T(2,128)(2,1)}, u32[]{:S(2)}) copy-start(bf16[128,2,128]{2,1,0:T(2,128)(2,1)} %param.6) | copy-start | bytes 196612
  4.5 4.4 %collective-permute-start = (bf16[128,1,128]{2,0,1:T(8,128)(2,1)S(1)}, bf16[128,1,128]{2,0,1:T(8,128)(2,1)S(1)}, u32[]{:S(2)}, u32[]{:S(2)}) collective-permute-start(bf16[128,1,128]{2,0,1:T(8,128)(2,1)S(1)} %copy.116), channel_id=1, source_target_pairs={{0,4},{4,0},{8,12},{12,8},{1,5},{5,1},{9,13},{13,9},{2,6},{6,2},{1... | collective-permute-start | bytes 98312 | tf_op jit(solution)/shard_map/ppermute | solution.py:10
  5.5 6.2 %collective-permute-start.2 = (bf16[128,1,128]{2,0,1:T(8,128)(2,1)S(1)}, bf16[128,1,128]{2,0,1:T(8,128)(2,1)S(1)}, u32[]{:S(2)}, u32[]{:S(2)}) collective-permute-start(bf16[128,1,128]{2,0,1:T(8,128)(2,1)S(1)} %copy.120), channel_id=1, source_target_pairs={{0,4},{4,0},{8,12},{12,8},{1,5},{5,1},{9,13},{13,9},{2,6},{6,2},{1... | collective-permute-start | bytes 98312 | tf_op jit(solution)/shard_map/ppermute | solution.py:10
  6.8 0.7 %copy-start.2 = (s32[8]{0:T(128)S(1)}, s32[8]{0:T(128)}, u32[]{:S(2)}) copy-start(s32[8]{0:T(128)} %param.7) | copy-start | bytes 100
  8.9 6.7 %collective-permute-start.3 = (bf16[256,1,128]{2,0,1:T(8,128)(2,1)S(1)}, bf16[256,1,128]{2,0,1:T(8,128)(2,1)S(1)}, u32[]{:S(2)}, u32[]{:S(2)}) collective-permute-start(bf16[256,1,128]{2,0,1:T(8,128)(2,1)S(1)} %maximum_select_fusion.2), channel_id=1, source_target_pairs={{0,8},{4,12},{8,0},{12,4},{1,9},{5,13},{9,1},{13,5},{2,10},{6,14},... | collective-permute-start | bytes 196616 | tf_op jit(solution)/shard_map/while/body/eval_jaxpr/ppermute | solution.py:15
  11.7 12.5 %collective-permute-start.4 = (bf16[256,1,128]{2,0,1:T(8,128)(2,1)S(1)}, bf16[256,1,128]{2,0,1:T(8,128)(2,1)S(1)}, u32[]{:S(2)}, u32[]{:S(2)}) collective-permute-start(bf16[256,1,128]{2,0,1:T(8,128)(2,1)S(1)} %maximum_select_fusion.3), channel_id=1, source_target_pairs={{0,8},{4,12},{8,0},{12,4},{1,9},{5,13},{9,1},{13,5},{2,10},{6,14},... | collective-permute-start | bytes 196616 | tf_op jit(solution)/shard_map/while/body/eval_jaxpr/ppermute | solution.py:15
  28.0 5.0 %collective-permute-start.5 = (bf16[128,4,128]{2,0,1:T(8,128)(2,1)S(1)}, bf16[128,4,128]{2,0,1:T(8,128)(2,1)S(1)}, u32[]{:S(2)}, u32[]{:S(2)}) collective-permute-start(bf16[128,4,128]{2,0,1:T(8,128)(2,1)S(1)} %get-tuple-element.137), channel_id=1, source_target_pairs={{0,4},{4,0},{8,12},{12,8},{1,5},{5,1},{9,13},{13,9},{2,6},{6,2},{1... | collective-permute-start | bytes 393224 | tf_op jit(solution)/shard_map/ppermute | solution.py:10
where the time goes:
time: 34.1 us; the launch traced here: 33.9 us
  matrix products  13.6 us (40%)
  starting transfers between devices  10.1 us (30%)
  waiting for transfers between devices  4.23 us (12%)
  local copies, waits for them, and re-layouts  3.22 us (9%)
  other arithmetic  2.32 us (7%)
  between operations  0.38 us (1%)
    dot_general x32, matrix products, attend(): jnp.einsum('ghcp,pgd->ghcd', weights.astype(jnp.bfloat16), value_rows, pr...  6.99 us
    ppermute x4, starting transfers between devices, partner(): return lax.ppermute(value, axis, pairs)  6.91 us
    dot_general x32, matrix products, attend(): jnp.einsum('cghd,pgd->ghcp', query_rows, key_rows, preferred_element_type...  6.64 us
    ppermute x4, waiting for transfers between devices, partner(): return lax.ppermute(value, axis, pairs)  4.22 us
    ppermute x2, starting transfers between devices, from_behind(): lax.ppermute(value, axis, [(i, (i + by) % devices) for i in range(devices)])  3.21 us
    reduce_sum x32, other arithmetic, attend(): new_sum = running_sum * factor + jnp.sum(weights, axis=-1)  1.57 us
    dynamic_slice x1, local copies, waits for them, and re-layouts, on_device(): lax.dynamic_slice_in_dim(queries, parity * half_heads, half_heads, 1)  1.17 us
    select_n x1, local copies, waits for them, and re-layouts, on_device(): jnp.where(lower, jnp.concatenate([mine, returned], 1), jnp.concatenate([r...  0.88 us
  transfers between devices with their start and end apart: 6, of which 2 were waited for; matrix products, arithmetic and copies ran while one was open for 38% of the time, Pallas kernels for 0%

commit v1 on v0

v1 whole, which is shorter than its diff:
```python
import functools

import jax
import jax.numpy as jnp
from jax import lax
from jax.experimental import pallas as pl
from jax.experimental.pallas import tpu as pltpu
from jax.sharding import PartitionSpec as P

LOW = -1e30
LOG2E = 1.4426950408889634


def pick(table, index):
    value = jnp.int32(table[0])
    for place in range(1, len(table)):
        value = jnp.where(index == place, jnp.int32(table[place]), value)
    return value


def attend(query, key, value, lanes, scale, state, diagonal):
    groups, per_token = lanes
    rows = query.shape[0]
    keys = key.shape[0] // groups
    lane = lax.broadcasted_iota(jnp.int32, (keys, rows), 1)
    group = (lane % per_token) // (per_token // groups)
    both = lax.dot_general(
        key, query, (((1,), (1,)), ((), ())), preferred_element_type=jnp.float32
    )
    scores = both[:keys]
    for g in range(1, groups):
        scores = jnp.where(group == g, both[g * keys : (g + 1) * keys], scores)
    scores = scores * scale
    if diagonal:
        place = lax.broadcasted_iota(jnp.int32, (keys, rows), 0)
        scores = jnp.where(place <= lane // per_token, scores, LOW)
    top = jnp.max(scores, axis=0, keepdims=True)
    if state is not None:
        top = jnp.maximum(top, state[0])
    weights = jnp.exp2(scores - top)
    total = jnp.sum(weights, axis=0, keepdims=True)
    rounded = weights.astype(jnp.bfloat16)
    nothing = jnp.zeros_like(rounded)
    spread = jnp.concatenate(
        [jnp.where(group == g, rounded, nothing) for g in range(groups)], axis=0
    )
    product = lax.dot_general(
        value, spread, (((0,), (0,)), ((), ())), preferred_element_type=jnp.float32
    )
    if state is None:
        return top, total, product
    factor = jnp.exp2(state[0] - top)
    return top, state[1] * factor + total, state[2] * factor + product


def load(refs, slot):
    return tuple(ref[slot] for ref in refs)


def store(refs, slot, state):
    for ref, part in zip(refs, state, strict=True):
        ref[slot] = part


def rows_of(ref, slot):
    half = ref.shape[0] // 2
    return ref[pl.ds(pl.multiple_of(slot * half, half), half), :]


def own_kernel(lanes, scale, order, query, packed, top, total, acc):
    me = lax.axis_index("seq")
    refs = (top, total, acc)
    for slot in range(2):
        state = attend(
            rows_of(query, slot), packed[slot, 0], packed[slot, 1], lanes, scale, None, True
        )
        store(refs, slot, state)
    late = jnp.where(order[2 * me] < order[2 * me + 1], 1, 0)
    early = 1 - late
    state = attend(
        rows_of(query, late), packed[early, 0], packed[early, 1], lanes, scale, load(refs, late), False
    )
    store(refs, late, state)


def remote(lanes, scale, order, query, packed, refs, me, source):
    late = jnp.where(order[2 * me] < order[2 * me + 1], 1, 0)
    early = 1 - late
    source_late = jnp.where(order[2 * source] < order[2 * source + 1], 1, 0)
    source_early = 1 - source_late
    state = attend(
        rows_of(query, late),
        packed[source_early, 0],
        packed[source_early, 1],
        lanes,
        scale,
        load(refs, late),
        False,
    )
    store(refs, late, state)
    before = order[2 * source + source_early] < order[2 * me + early]
    mine = jnp.where(before, early, late)
    theirs = jnp.where(before, source_early, source_late)
    state = attend(
        rows_of(query, mine),
        packed[theirs, 0],
        packed[theirs, 1],
        lanes,
        scale,
        load(refs, mine),
        False,
    )
    store(refs, mine, state)


def finish(refs, out):
    half = out.shape[0] // 2
    for slot in range(2):
        result = refs[2][slot] / refs[1][slot]
        out[slot * half : (slot + 1) * half, :] = result.T.astype(out.dtype)


def middle_kernel(lanes, scale, sources, order, query, *rest):
    count = len(sources)
    blocks, before, after = rest[:count], rest[count : count + 3], rest[count + 3 :]
    me = lax.axis_index("seq")
    for slot in range(2):
        store(after, slot, load(before, slot))
    for table, packed in zip(sources, blocks, strict=True):
        remote(lanes, scale, order, query, packed, after, me, pick(table, me))


def last_kernel(lanes, scale, sources, choose, order, query, *rest):
    count = len(sources)
    blocks, before, out, after = rest[:count], rest[count : count + 3], rest[count + 3], rest[count + 4 :]
    me = lax.axis_index("seq")
    for slot in range(2):
        store(after, slot, load(before, slot))
    for number, (table, packed) in enumerate(zip(sources, blocks, strict=True)):
        @pl.when(pick(choose, me) == number)
        def _():
            remote(lanes, scale, order, query, packed, after, me, pick(table, me))
    finish(after, out)


def gathered_kernel(lanes, scale, order, query, blocks, *rest):
    before, out, after = rest[:3], rest[3], rest[4:]
    me = lax.axis_index("seq")
    count = blocks.shape[0]
    for slot in range(2):
        store(after, slot, load(before, slot))

    def step(index, carry):
        source = lax.rem(me + index, count)
        remote(lanes, scale, order, query, blocks.at[source], after, me, source)
        return carry

    lax.fori_loop(1, count, step, 0)
    finish(after, out)


def on_device(queries, keys, values, block_order):
    tokens, heads, width = queries.shape
    groups = keys.shape[1]
    half = tokens // 2
    devices = lax.axis_size("seq")
    scale = width ** (-0.5) * LOG2E
    lanes = (groups, heads)
    rows = tokens * heads
    query = queries.reshape(rows, width)

    def pack(array):
        split = array.reshape(2, half, groups, width)
        return jnp.transpose(split, (0, 2, 1, 3)).reshape(2, 1, groups * half, width)

    packed = jnp.concatenate([pack(keys), pack(values)], axis=1)
    shapes = [
        jax.ShapeDtypeStruct((2, 1, rows // 2), jnp.float32),
        jax.ShapeDtypeStruct((2, 1, rows // 2), jnp.float32),
        jax.ShapeDtypeStruct((2, width, rows // 2), jnp.float32),
    ]
    scratch = [pltpu.VMEM(s.shape, s.dtype) for s in shapes]
    result = jax.ShapeDtypeStruct((rows, width), queries.dtype)
    vmem = pl.BlockSpec(memory_space=pltpu.VMEM)
    smem = pl.BlockSpec(memory_space=pltpu.SMEM)

    def call(kernel, blocks, state, out_shape, tasks, scratch_shapes=()):
        inputs = [block_order, query, *blocks, *state]
        flops = 4 * tasks * groups * half * rows // 2 * width
        return pl.pallas_call(
            kernel,
            out_shape=out_shape,
            in_specs=[smem] + [vmem] * (len(inputs) - 1),
            out_specs=jax.tree.map(lambda _: vmem, out_shape),
            scratch_shapes=scratch_shapes,
            cost_estimate=pl.CostEstimate(
                flops=flops, bytes_accessed=rows * width * 2, transcendentals=tasks * half * rows
            ),
        )(*inputs)

    def permute(value, pairs):
        return lax.ppermute(value, "seq", pairs)

    if devices == 4:
        first = permute(packed, [(0, 2), (3, 1), (1, 0), (2, 3)])
        second = permute(packed, [(1, 3), (2, 0), (0, 1), (3, 2)])
        inner = permute(packed, [(1, 2), (2, 1), (0, 0), (3, 3)])
        state = call(functools.partial(own_kernel, lanes, scale), [packed], [], shapes, 3)
        outer = permute(first, [(2, 3), (1, 0), (0, 1), (3, 2)])
        state = call(
            functools.partial(middle_kernel, lanes, scale, [(1, 3, 0, 2), (2, 0, 3, 1)]),
            [first, second],
            state,
            shapes,
            4,
        )
        out = call(
            functools.partial(
                last_kernel, lanes, scale, [(0, 2, 1, 3), (3, 0, 3, 0)], (1, 0, 0, 1)
            ),
            [inner, outer],
            state,
            result,
            2,
            scratch,
        )
    else:
        blocks = lax.all_gather(packed, "seq", axis=0, tiled=False)
        state = call(functools.partial(own_kernel, lanes, scale), [packed], [], shapes, 3)
        out = call(
            functools.partial(gathered_kernel, lanes, scale), [blocks], state, result, 2 * devices, scratch
        )
    return out.reshape(tokens, heads, width)


def solution(mesh):
    placed = (
        P(("grp", "seq"), "head", None),
        P(("grp", "seq"), "head", None),
        P(("grp", "seq"), "head", None),
        P("grp"),
    )
    return jax.shard_map(
        on_device,
        mesh=mesh,
        in_specs=placed,
        out_specs=P(("grp", "seq"), "head", None),
        check_vma=False,
    )
```

time: 34.1 us -> 21.6 us (0.63)
  matrix products: 13.6 us -> 0 us
  Pallas kernels: 0 us -> 8.64 us
  starting transfers between devices: 10.1 us -> 7.14 us
  other arithmetic: 2.32 us -> 0.02 us
  waiting for transfers between devices: 4.23 us -> 3.23 us
  local copies, waits for them, and re-layouts: 3.22 us -> 2.22 us
    dot_general x64 -> x0, matrix products: 13.6 us -> none  [the longest x32 6.99 us: attend(): jnp.einsum('ghcp,pgd->ghcd', weights.astype(jnp.bfloat16), value_rows, pr...]
    pallas_call x0 -> x3, Pallas kernels: none -> 8.64 us  [call(): pl.pallas_call(kernel, out_shape=out_shape, in_specs=[smem] + [vmem] * (l...]
    ppermute x6 -> x4, starting transfers between devices: 10.1 us -> 7.14 us  [permute(): return lax.ppermute(value, 'seq', pairs)]
    reduce_sum x33 -> x0, other arithmetic: 1.65 us -> none  [the longest x32 1.57 us: attend(): new_sum = running_sum * factor + jnp.sum(weights, axis=-1)]
    dynamic_slice x3 -> x0, local copies, waits for them, and re-layouts: 1.45 us -> none  [the longest x1 1.17 us: on_device(): lax.dynamic_slice_in_dim(queries, parity * half_heads, half_heads, 1)]
    ppermute x6 -> x4, waiting for transfers between devices: 4.23 us -> 3.23 us  [permute(): return lax.ppermute(value, 'seq', pairs)]
    reshape x0 -> x2, local copies, waits for them, and re-layouts: none -> 0.89 us  [pack(): split = array.reshape(2, half, groups, width)]
    select_n x1 -> x0, local copies, waits for them, and re-layouts: 0.88 us -> none  [on_device(): jnp.where(lower, jnp.concatenate([mine, returned], 1), jnp.concatenate([r...]
  transfers between devices with their start and end apart: 6 -> 4, of which waited for: 2 -> 1; matrix products, arithmetic and copies ran while one was open for 38% -> 0% of each run, Pallas kernels for 0% -> 27%
where the time goes in v1:
time: 21.6 us; the launch traced here: 21.3 us
  Pallas kernels  8.64 us (40%)
  starting transfers between devices  7.14 us (33%)
  waiting for transfers between devices  3.23 us (15%)
  local copies, waits for them, and re-layouts  2.22 us (10%)
    pallas_call x3, Pallas kernels, call(): pl.pallas_call(kernel, out_shape=out_shape, in_specs=[smem] + [vmem] * (l...  8.64 us
    ppermute x4, starting transfers between devices, permute(): return lax.ppermute(value, 'seq', pairs)  7.14 us
    ppermute x4, waiting for transfers between devices, permute(): return lax.ppermute(value, 'seq', pairs)  3.23 us
    unnamed x12, local copies, waits for them, and re-layouts  1.32 us
    reshape x2, local copies, waits for them, and re-layouts, pack(): split = array.reshape(2, half, groups, width)  0.89 us
  transfers between devices with their start and end apart: 4, of which 1 were waited for; matrix products, arithmetic and copies ran while one was open for 0% of the time, Pallas kernels for 27%

profile of v1, /device:TPU:0, one launch (start us, length us, event | category | flops | bytes accessed | tf_op | source)
XLA Modules:
  0.0 21.3 jit_solution(13076362116524194730)
XLA Ops:
  0.0 0.0 copy-start.5
  0.0 0.9 %copy.5 = bf16[2,64,2,128]{3,1,2,0:T(8,128)(2,1)S(1)} copy(bf16[2,64,2,128]{3,2,1,0:T(2,128)(2,1)} %bitcast.15) | data formatting | bytes 131072 | tf_op jit(solution)/shard_map/reshape | solution.py:173
  0.9 0.0 copy-done.5
  0.9 0.0 copy-start
  0.9 4.1 %collective-permute-start.1 = (bf16[2,2,128,128]{3,2,1,0:T(8,128)(2,1)S(1)}, bf16[2,2,128,128]{3,2,1,0:T(8,128)(2,1)S(1)}, u32[]{:S(2)}, u32[]{:S(2)}) collective-permute-start(bf16[2,2,128,128]{3,2,1,0:T(8,128)(2,1)S(1)} %pad_maximum_fusion.packed), channel_id=1, source_target_pairs={{0,8},{12,4},{4,0},{8,12},{1,9},{13,5},{5,1},{9,13},{2,10},{14,6},... | collective-permute-start | bytes 393224 | tf_op jit(solution)/shard_map/ppermute | solution.py:202
  5.1 0.0 collective-permute-start.3
  5.1 0.7 %collective-permute-start = (bf16[2,2,128,128]{3,2,1,0:T(8,128)(2,1)S(1)}, bf16[2,2,128,128]{3,2,1,0:T(8,128)(2,1)S(1)}, u32[]{:S(2)}, u32[]{:S(2)}) collective-permute-start(bf16[2,2,128,128]{3,2,1,0:T(8,128)(2,1)S(1)} %pad_maximum_fusion.packed), channel_id=1, source_target_pairs={{4,8},{8,4},{0,0},{12,12},{5,9},{9,5},{1,1},{13,13},{6,10},{10,6},... | collective-permute-start | bytes 393224 | tf_op jit(solution)/shard_map/ppermute | solution.py:202
  5.7 3.2 %collective-permute-done.1.rest_0_ = bf16[2,2,128,128]{3,2,1,0:T(8,128)(2,1)S(1)} collective-permute-done((bf16[2,2,128,128]{3,2,1,0:T(8,128)(2,1)S(1)}, bf16[2,2,128,128]{3,2,1,0:T(8,128)(2,1)S(1)}, u32[]{:S(2)}, u32[]{:S(2)}) %collective-permute-start.1) | collective-permute-done | bytes 131104 | tf_op jit(solution)/shard_map/ppermute | solution.py:202
  9.0 0.0 copy-start.3
  9.0 2.4 %collective-permute-start.2 = (bf16[2,2,128,128]{3,2,1,0:T(8,128)(2,1)S(1)}, bf16[2,2,128,128]{3,2,1,0:T(8,128)(2,1)S(1)}, u32[]{:S(2)}, u32[]{:S(2)}) collective-permute-start(bf16[2,2,128,128]{3,2,1,0:T(8,128)(2,1)S(1)} %collective-permute-done.1.rest_0_), channel_id=1, source_target_pairs={{8,12},{4,0},{0,4},{12,8},{9,13},{5,1},{1,5},{13,9},{10,14},{6,2},... | collective-permute-start | bytes 393224 | tf_op jit(solution)/shard_map/ppermute | solution.py:202
  11.3 0.0 copy-done
  11.3 2.6 %shard_map.46 = (f32[2,1,512]{2,1,0:T(1,128)}, f32[2,1,512]{2,1,0:T(1,128)}, f32[2,128,512]{2,1,0:T(8,128)}) custom-call(s32[8]{0:T(128)} %order.5, bf16[1024,128]{1,0:T(8,128)(2,1)} %bitcast.10, bf16[2,2,128,128]{3,2,1,0:T(8,128)(2,1)} %copy-done), custom_call_target="tpu_custom_call" | custom-call | flops 100663296 | bytes 262144 | tf_op jit(solution)/shard_map/pallas_call | solution.py:190
  14.0 0.0 copy-done.3
  14.0 0.0 collective-permute-done.3.rest_1_
  14.0 0.0 copy-start.4
  14.0 0.6 %copy-done.4 = bf16[2,2,128,128]{3,2,1,0:T(8,128)(2,1)} copy-done((bf16[2,2,128,128]{3,2,1,0:T(8,128)(2,1)}, bf16[2,2,128,128]{3,2,1,0:T(8,128)(2,1)S(1)}, u32[]{:S(2)}) %copy-start.4) | copy-done | bytes 131096
  14.6 3.2 %shard_map.47 = (f32[2,1,512]{2,1,0:T(1,128)}, f32[2,1,512]{2,1,0:T(1,128)}, f32[2,128,512]{2,1,0:T(8,128)}) custom-call(s32[8]{0:T(128)} %order.5, bf16[1024,128]{1,0:T(8,128)(2,1)} %bitcast.11, bf16[2,2,128,128]{3,2,1,0:T(8,128)(2,1)} %copy-done.3, bf16[2,2,128,128]{3,2,1,0:T(8,128)(2,1)} %copy-done.4, f32[2,1,512]{2,1,0:T(1,128)} %get-tuple-element.11.rest_2_, ...), custom_call_target="tpu_custom_call" | custom-call | flops 134217728 | bytes 262144 | tf_op jit(solution)/shard_map/pallas_call | solution.py:190
  17.8 0.0 collective-permute-done.rest_0_
  17.8 0.0 copy-start.1
  17.8 0.0 collective-permute-done.2.rest_1_
  17.8 0.0 copy-start.2
  17.8 0.6 %copy-done.1 = bf16[2,2,128,128]{3,2,1,0:T(8,128)(2,1)} copy-done((bf16[2,2,128,128]{3,2,1,0:T(8,128)(2,1)}, bf16[2,2,128,128]{3,2,1,0:T(8,128)(2,1)S(1)}, u32[]{:S(2)}) %copy-start.1) | copy-done | bytes 131096
  18.5 0.1 copy-done.2
  18.5 2.8 %shard_map.48 = bf16[1024,128]{1,0:T(8,128)(2,1)} custom-call(s32[8]{0:T(128)} %order.5, bf16[1024,128]{1,0:T(8,128)(2,1)} %bitcast.12, bf16[2,2,128,128]{3,2,1,0:T(8,128)(2,1)} %copy-done.1, bf16[2,2,128,128]{3,2,1,0:T(8,128)(2,1)} %copy-done.2, f32[2,1,512]{2,1,0:T(1,128)} %get-tuple-element.14.rest_2_, f32[2,1,512]{2,1,0:T(1,128)} %get-tuple-element.15.rest_3_, ...), custom_call_target="tpu_custom_call" | custom-call | flops 67108864 | bytes 262144 | tf_op jit(solution)/shard_map/pallas_call | solution.py:190
  (2 shorter events, 0.0 us)
Async XLA Ops:
  0.0 0.9 %copy-start.5 = (bf16[128,2,128]{2,1,0:T(2,128)(2,1)S(1)}, bf16[128,2,128]{2,1,0:T(2,128)(2,1)}, u32[]{:S(2)}) copy-start(bf16[128,2,128]{2,1,0:T(2,128)(2,1)} %param.6) | copy-start | bytes 196612
  0.9 10.4 %copy-start = (bf16[2,2,128,128]{3,2,1,0:T(8,128)(2,1)}, bf16[2,2,128,128]{3,2,1,0:T(8,128)(2,1)S(1)}, u32[]{:S(2)}) copy-start(bf16[2,2,128,128]{3,2,1,0:T(8,128)(2,1)S(1)} %pad_maximum_fusion.packed) | copy-start | bytes 393220
  0.9 8.0 %collective-permute-start.1 = (bf16[2,2,128,128]{3,2,1,0:T(8,128)(2,1)S(1)}, bf16[2,2,128,128]{3,2,1,0:T(8,128)(2,1)S(1)}, u32[]{:S(2)}, u32[]{:S(2)}) collective-permute-start(bf16[2,2,128,128]{3,2,1,0:T(8,128)(2,1)S(1)} %pad_maximum_fusion.packed), channel_id=1, source_target_pairs={{0,8},{12,4},{4,0},{8,12},{1,9},{13,5},{5,1},{9,13},{2,10},{14,6},... | collective-permute-start | bytes 393224 | tf_op jit(solution)/shard_map/ppermute | solution.py:202
  5.1 8.9 %collective-permute-start.3 = (bf16[2,2,128,128]{3,2,1,0:T(8,128)(2,1)S(1)}, bf16[2,2,128,128]{3,2,1,0:T(8,128)(2,1)S(1)}, u32[]{:S(2)}, u32[]{:S(2)}) collective-permute-start(bf16[2,2,128,128]{3,2,1,0:T(8,128)(2,1)S(1)} %pad_maximum_fusion.packed), channel_id=1, source_target_pairs={{4,12},{8,0},{0,4},{12,8},{5,13},{9,1},{1,5},{13,9},{6,14},{10,2},... | collective-permute-start | bytes 393224 | tf_op jit(solution)/shard_map/ppermute | solution.py:202
  5.1 12.7 %collective-permute-start = (bf16[2,2,128,128]{3,2,1,0:T(8,128)(2,1)S(1)}, bf16[2,2,128,128]{3,2,1,0:T(8,128)(2,1)S(1)}, u32[]{:S(2)}, u32[]{:S(2)}) collective-permute-start(bf16[2,2,128,128]{3,2,1,0:T(8,128)(2,1)S(1)} %pad_maximum_fusion.packed), channel_id=1, source_target_pairs={{4,8},{8,4},{0,0},{12,12},{5,9},{9,5},{1,1},{13,13},{6,10},{10,6},... | collective-permute-start | bytes 393224 | tf_op jit(solution)/shard_map/ppermute | solution.py:202
  9.0 5.0 %copy-start.3 = (bf16[2,2,128,128]{3,2,1,0:T(8,128)(2,1)}, bf16[2,2,128,128]{3,2,1,0:T(8,128)(2,1)S(1)}, u32[]{:S(2)}) copy-start(bf16[2,2,128,128]{3,2,1,0:T(8,128)(2,1)S(1)} %collective-permute-done.1.rest_0_) | copy-start | bytes 393220
  9.0 8.9 %collective-permute-start.2 = (bf16[2,2,128,128]{3,2,1,0:T(8,128)(2,1)S(1)}, bf16[2,2,128,128]{3,2,1,0:T(8,128)(2,1)S(1)}, u32[]{:S(2)}, u32[]{:S(2)}) collective-permute-start(bf16[2,2,128,128]{3,2,1,0:T(8,128)(2,1)S(1)} %collective-permute-done.1.rest_0_), channel_id=1, source_target_pairs={{8,12},{4,0},{0,4},{12,8},{9,13},{5,1},{1,5},{13,9},{10,14},{6,2},... | collective-permute-start | bytes 393224 | tf_op jit(solution)/shard_map/ppermute | solution.py:202
  14.0 0.6 %copy-start.4 = (bf16[2,2,128,128]{3,2,1,0:T(8,128)(2,1)}, bf16[2,2,128,128]{3,2,1,0:T(8,128)(2,1)S(1)}, u32[]{:S(2)}) copy-start(bf16[2,2,128,128]{3,2,1,0:T(8,128)(2,1)S(1)} %collective-permute-done.3.rest_1_) | copy-start | bytes 393220
  17.8 0.6 %copy-start.1 = (bf16[2,2,128,128]{3,2,1,0:T(8,128)(2,1)}, bf16[2,2,128,128]{3,2,1,0:T(8,128)(2,1)S(1)}, u32[]{:S(2)}) copy-start(bf16[2,2,128,128]{3,2,1,0:T(8,128)(2,1)S(1)} %collective-permute-done.rest_0_) | copy-start | bytes 393220
  17.8 0.7 %copy-start.2 = (bf16[2,2,128,128]{3,2,1,0:T(8,128)(2,1)}, bf16[2,2,128,128]{3,2,1,0:T(8,128)(2,1)S(1)}, u32[]{:S(2)}) copy-start(bf16[2,2,128,128]{3,2,1,0:T(8,128)(2,1)S(1)} %collective-permute-done.2.rest_1_) | copy-start | bytes 393220

commit v2 on v1

--- a/solution.py
+++ b/solution.py
@@ -193,6 +193,7 @@
             in_specs=[smem] + [vmem] * (len(inputs) - 1),
             out_specs=jax.tree.map(lambda _: vmem, out_shape),
             scratch_shapes=scratch_shapes,
+            compiler_params=pltpu.CompilerParams(vmem_limit_bytes=16 * 2**20),
             cost_estimate=pl.CostEstimate(
                 flops=flops, bytes_accessed=rows * width * 2, transcendentals=tasks * half * rows
             ),

time: 21.6 us -> 17.3 us (0.80)
  Pallas kernels: 8.64 us -> 5.14 us
  local copies, waits for them, and re-layouts: 2.22 us -> 0.92 us
  waiting for transfers between devices: 3.23 us -> 3.86 us
    pallas_call x3, Pallas kernels: 8.64 us -> 5.14 us  [call(): pl.pallas_call(kernel, out_shape=out_shape, in_specs=[smem] + [vmem] * (l...]
    unnamed x12 -> x6, local copies, waits for them, and re-layouts: 1.32 us -> 0.01 us
    ppermute x4, waiting for transfers between devices: 3.23 us -> 3.86 us  [permute(): return lax.ppermute(value, 'seq', pairs)]
  transfers between devices with their start and end apart: 4 -> 4, of which waited for: 1 -> 3; matrix products, arithmetic and copies ran while one was open for 0% -> 0% of each run, Pallas kernels for 27% -> 18%
where the time goes in v2:
time: 17.3 us; the launch traced here: 17.2 us
  starting transfers between devices  7.14 us (41%)
  Pallas kernels  5.14 us (30%)
  waiting for transfers between devices  3.86 us (22%)
  local copies, waits for them, and re-layouts  0.92 us (5%)
    ppermute x4, starting transfers between devices, permute(): return lax.ppermute(value, 'seq', pairs)  7.14 us
    pallas_call x3, Pallas kernels, call(): pl.pallas_call(kernel, out_shape=out_shape, in_specs=[smem] + [vmem] * (l...  5.14 us
    ppermute x4, waiting for transfers between devices, permute(): return lax.ppermute(value, 'seq', pairs)  3.86 us
    reshape x2, local copies, waits for them, and re-layouts, pack(): split = array.reshape(2, half, groups, width)  0.91 us
  transfers between devices with their start and end apart: 4, of which 3 were waited for; matrix products, arithmetic and copies ran while one was open for 0% of the time, Pallas kernels for 18%

profile of v2, /device:TPU:0, one launch (start us, length us, event | category | flops | bytes accessed | tf_op | source)
XLA Modules:
  0.0 17.2 jit_solution(1496411372362421471)
XLA Ops:
  0.0 0.0 copy-start.2
  0.0 0.0 copy-start
  0.0 0.9 %copy.5 = bf16[2,64,2,128]{3,1,2,0:T(8,128)(2,1)S(1)} copy(bf16[2,64,2,128]{3,2,1,0:T(2,128)(2,1)} %bitcast.15) | data formatting | bytes 131072 | tf_op jit(solution)/shard_map/reshape | solution.py:173
  0.9 0.0 copy-done.2
  1.0 0.0 copy-start.1
  1.0 4.1 %collective-permute-start.1 = (bf16[2,2,128,128]{3,2,1,0:T(8,128)(2,1)S(1)}, bf16[2,2,128,128]{3,2,1,0:T(8,128)(2,1)S(1)}, u32[]{:S(2)}, u32[]{:S(2)}) collective-permute-start(bf16[2,2,128,128]{3,2,1,0:T(8,128)(2,1)S(1)} %pad_maximum_fusion.packed), channel_id=1, source_target_pairs={{0,8},{12,4},{4,0},{8,12},{1,9},{13,5},{5,1},{9,13},{2,10},{14,6},... | collective-permute-start | bytes 393224 | tf_op jit(solution)/shard_map/ppermute | solution.py:203
  5.1 0.0 collective-permute-start.3
  5.1 0.7 %collective-permute-start = (bf16[2,2,128,128]{3,2,1,0:T(8,128)(2,1)S(1)}, bf16[2,2,128,128]{3,2,1,0:T(8,128)(2,1)S(1)}, u32[]{:S(2)}, u32[]{:S(2)}) collective-permute-start(bf16[2,2,128,128]{3,2,1,0:T(8,128)(2,1)S(1)} %pad_maximum_fusion.packed), channel_id=1, source_target_pairs={{4,8},{8,4},{0,0},{12,12},{5,9},{9,5},{1,1},{13,13},{6,10},{10,6},... | collective-permute-start | bytes 393224 | tf_op jit(solution)/shard_map/ppermute | solution.py:203
  5.8 3.2 %collective-permute-done.1.rest_0_ = bf16[2,2,128,128]{3,2,1,0:T(8,128)(2,1)S(1)} collective-permute-done((bf16[2,2,128,128]{3,2,1,0:T(8,128)(2,1)S(1)}, bf16[2,2,128,128]{3,2,1,0:T(8,128)(2,1)S(1)}, u32[]{:S(2)}, u32[]{:S(2)}) %collective-permute-start.1) | collective-permute-done | bytes 131104 | tf_op jit(solution)/shard_map/ppermute | solution.py:203
  9.0 2.4 %collective-permute-start.2 = (bf16[2,2,128,128]{3,2,1,0:T(8,128)(2,1)S(1)}, bf16[2,2,128,128]{3,2,1,0:T(8,128)(2,1)S(1)}, u32[]{:S(2)}, u32[]{:S(2)}) collective-permute-start(bf16[2,2,128,128]{3,2,1,0:T(8,128)(2,1)S(1)} %collective-permute-done.1.rest_0_), channel_id=1, source_target_pairs={{8,12},{4,0},{0,4},{12,8},{9,13},{5,1},{1,5},{13,9},{10,14},{6,2},... | collective-permute-start | bytes 393224 | tf_op jit(solution)/shard_map/ppermute | solution.py:203
  11.3 0.0 copy-done
  11.3 0.0 copy-done.1
  11.3 1.4 %shard_map.46 = (f32[2,1,512]{2,1,0:T(1,128)S(1)}, f32[2,1,512]{2,1,0:T(1,128)S(1)}, f32[2,128,512]{2,1,0:T(8,128)S(1)}) custom-call(s32[8]{0:T(128)S(1)} %copy-done.1, bf16[1024,128]{1,0:T(8,128)(2,1)S(1)} %bitcast.10, bf16[2,2,128,128]{3,2,1,0:T(8,128)(2,1)S(1)} %pad_maximum_fusion.packed), custom_call_target="tpu_custom_call" | custom-call | flops 100663296 | bytes 262144 | tf_op jit(solution)/shard_map/pallas_call | solution.py:190
  12.7 0.3 %collective-permute-done.3.rest_1_ = bf16[2,2,128,128]{3,2,1,0:T(8,128)(2,1)S(1)} collective-permute-done((bf16[2,2,128,128]{3,2,1,0:T(8,128)(2,1)S(1)}, bf16[2,2,128,128]{3,2,1,0:T(8,128)(2,1)S(1)}, u32[]{:S(2)}, u32[]{:S(2)}) %collective-permute-start.3) | collective-permute-done | bytes 131104 | tf_op jit(solution)/shard_map/ppermute | solution.py:203
  13.0 1.7 %shard_map.47 = (f32[2,1,512]{2,1,0:T(1,128)S(1)}, f32[2,1,512]{2,1,0:T(1,128)S(1)}, f32[2,128,512]{2,1,0:T(8,128)S(1)}) custom-call(s32[8]{0:T(128)S(1)} %copy-done.1, bf16[1024,128]{1,0:T(8,128)(2,1)S(1)} %bitcast.11, bf16[2,2,128,128]{3,2,1,0:T(8,128)(2,1)S(1)} %collective-permute-done.1.rest_0_, ...), custom_call_target="tpu_custom_call" | custom-call | flops 134217728 | bytes 262144 | tf_op jit(solution)/shard_map/pallas_call | solution.py:190
  14.7 0.0 collective-permute-done.rest_0_
  14.7 0.4 %collective-permute-done.2.rest_1_ = bf16[2,2,128,128]{3,2,1,0:T(8,128)(2,1)S(1)} collective-permute-done((bf16[2,2,128,128]{3,2,1,0:T(8,128)(2,1)S(1)}, bf16[2,2,128,128]{3,2,1,0:T(8,128)(2,1)S(1)}, u32[]{:S(2)}, u32[]{:S(2)}) %collective-permute-start.2) | collective-permute-done | bytes 131104 | tf_op jit(solution)/shard_map/ppermute | solution.py:203
  15.1 2.1 %shard_map.48 = bf16[1024,128]{1,0:T(8,128)(2,1)} custom-call(s32[8]{0:T(128)S(1)} %copy-done.1, bf16[1024,128]{1,0:T(8,128)(2,1)S(1)} %bitcast.12, bf16[2,2,128,128]{3,2,1,0:T(8,128)(2,1)S(1)} %collective-permute-done.rest_0_, bf16[2,2,128,128]{3,2,1,0:T(8,128)(2,1)S(1)} %collective-permute-done.2.rest_1_, f32[2,1,512]{2,1,0:T(1,128)S(1)} %get-tuple-element.14.rest_2_, ...), custom_call_target="tpu_custom_call" | custom-call | flops 67108864 | bytes 262144 | tf_op jit(solution)/shard_map/pallas_call | solution.py:190
  (2 shorter events, 0.0 us)
Async XLA Ops:
  0.0 0.9 %copy-start.2 = (bf16[128,2,128]{2,1,0:T(2,128)(2,1)S(1)}, bf16[128,2,128]{2,1,0:T(2,128)(2,1)}, u32[]{:S(2)}) copy-start(bf16[128,2,128]{2,1,0:T(2,128)(2,1)} %param.6) | copy-start | bytes 196612
  0.0 11.3 %copy-start = (bf16[128,8,128]{2,1,0:T(8,128)(2,1)S(1)}, bf16[128,8,128]{2,1,0:T(8,128)(2,1)}, u32[]{:S(2)}) copy-start(bf16[128,8,128]{2,1,0:T(8,128)(2,1)} %param.4) | copy-start | bytes 786436
  1.0 10.4 %copy-start.1 = (s32[8]{0:T(128)S(1)}, s32[8]{0:T(128)}, u32[]{:S(2)}) copy-start(s32[8]{0:T(128)} %order.5) | copy-start | bytes 100
  1.0 8.0 %collective-permute-start.1 = (bf16[2,2,128,128]{3,2,1,0:T(8,128)(2,1)S(1)}, bf16[2,2,128,128]{3,2,1,0:T(8,128)(2,1)S(1)}, u32[]{:S(2)}, u32[]{:S(2)}) collective-permute-start(bf16[2,2,128,128]{3,2,1,0:T(8,128)(2,1)S(1)} %pad_maximum_fusion.packed), channel_id=1, source_target_pairs={{0,8},{12,4},{4,0},{8,12},{1,9},{13,5},{5,1},{9,13},{2,10},{14,6},... | collective-permute-start | bytes 393224 | tf_op jit(solution)/shard_map/ppermute | solution.py:203
  5.1 7.9 %collective-permute-start.3 = (bf16[2,2,128,128]{3,2,1,0:T(8,128)(2,1)S(1)}, bf16[2,2,128,128]{3,2,1,0:T(8,128)(2,1)S(1)}, u32[]{:S(2)}, u32[]{:S(2)}) collective-permute-start(bf16[2,2,128,128]{3,2,1,0:T(8,128)(2,1)S(1)} %pad_maximum_fusion.packed), channel_id=1, source_target_pairs={{4,12},{8,0},{0,4},{12,8},{5,13},{9,1},{1,5},{13,9},{6,14},{10,2},... | collective-permute-start | bytes 393224 | tf_op jit(solution)/shard_map/ppermute | solution.py:203
  5.1 9.6 %collective-permute-start = (bf16[2,2,128,128]{3,2,1,0:T(8,128)(2,1)S(1)}, bf16[2,2,128,128]{3,2,1,0:T(8,128)(2,1)S(1)}, u32[]{:S(2)}, u32[]{:S(2)}) collective-permute-start(bf16[2,2,128,128]{3,2,1,0:T(8,128)(2,1)S(1)} %pad_maximum_fusion.packed), channel_id=1, source_target_pairs={{4,8},{8,4},{0,0},{12,12},{5,9},{9,5},{1,1},{13,13},{6,10},{10,6},... | collective-permute-start | bytes 393224 | tf_op jit(solution)/shard_map/ppermute | solution.py:203
  9.0 6.1 %collective-permute-start.2 = (bf16[2,2,128,128]{3,2,1,0:T(8,128)(2,1)S(1)}, bf16[2,2,128,128]{3,2,1,0:T(8,128)(2,1)S(1)}, u32[]{:S(2)}, u32[]{:S(2)}) collective-permute-start(bf16[2,2,128,128]{3,2,1,0:T(8,128)(2,1)S(1)} %collective-permute-done.1.rest_0_), channel_id=1, source_target_pairs={{8,12},{4,0},{0,4},{12,8},{9,13},{5,1},{1,5},{13,9},{10,14},{6,2},... | collective-permute-start | bytes 393224 | tf_op jit(solution)/shard_map/ppermute | solution.py:203

commit v3 on v2

v3 whole, which is shorter than its diff:
```python
import functools

import jax
import jax.numpy as jnp
from jax import lax
from jax.experimental import pallas as pl
from jax.experimental.pallas import tpu as pltpu
from jax.sharding import PartitionSpec as P

LOW = -1e30
LOG2E = 1.4426950408889634


def pick(table, index):
    value = jnp.int32(table[0])
    for place in range(1, len(table)):
        value = jnp.where(index == place, jnp.int32(table[place]), value)
    return value


def attend(query, blocks, lanes, scale, state, diagonal):
    groups, per_token = lanes
    rows = query.shape[0]
    keys = blocks[0][0].shape[0] // groups
    lane = lax.broadcasted_iota(jnp.int32, (keys, rows), 1)
    group = (lane % per_token) // (per_token // groups)
    parts = []
    for key, _ in blocks:
        both = lax.dot_general(
            key, query, (((1,), (1,)), ((), ())), preferred_element_type=jnp.float32
        )
        part = both[:keys]
        for g in range(1, groups):
            part = jnp.where(group == g, both[g * keys : (g + 1) * keys], part)
        part = part * scale
        if diagonal:
            place = lax.broadcasted_iota(jnp.int32, (keys, rows), 0)
            part = jnp.where(place <= lane // per_token, part, LOW)
        parts.append(part)
    top = functools.reduce(jnp.maximum, [jnp.max(part, axis=0, keepdims=True) for part in parts])
    if state is not None:
        top = jnp.maximum(top, state[0])
    total = 0.0
    spread = []
    for part in parts:
        weights = jnp.exp2(part - top)
        total = total + jnp.sum(weights, axis=0, keepdims=True)
        rounded = weights.astype(jnp.bfloat16)
        nothing = jnp.zeros_like(rounded)
        spread += [jnp.where(group == g, rounded, nothing) for g in range(groups)]
    product = lax.dot_general(
        jnp.concatenate([value for _, value in blocks], axis=0),
        jnp.concatenate(spread, axis=0),
        (((0,), (0,)), ((), ())),
        preferred_element_type=jnp.float32,
    )
    if state is None:
        return top, total, product
    factor = jnp.exp2(state[0] - top)
    return top, state[1] * factor + total, state[2] * factor + product


def load(refs, slot):
    return tuple(ref[slot] for ref in refs)


def store(refs, slot, state):
    for ref, part in zip(refs, state, strict=True):
        ref[slot] = part


def rows_of(ref, slot):
    half = ref.shape[0] // 2
    return ref[pl.ds(pl.multiple_of(slot * half, half), half), :]


def order_of(order, me, source):
    mine, theirs = order[2 * me], order[2 * source]
    mine_too, theirs_too = order[2 * me + 1], order[2 * source + 1]
    late = jnp.where(mine < mine_too, 1, 0)
    source_late = jnp.where(theirs < theirs_too, 1, 0)
    before = jnp.where(jnp.minimum(theirs, theirs_too) < jnp.minimum(mine, mine_too), 1, 0)
    return late + 2 * source_late + 4 * before


def own_kernel(lanes, scale, sources, order, query, packed, top, total, acc, codes):
    me = lax.axis_index("seq")
    refs = (top, total, acc)
    row = lax.broadcasted_iota(jnp.int32, codes.shape, 0)
    value = jnp.zeros(codes.shape, jnp.int32)
    for number, table in enumerate(sources):
        value = jnp.where(row == number, order_of(order, me, pick(table, me)), value)
    codes[...] = value
    late = jnp.where(order[2 * me] < order[2 * me + 1], 1, 0)
    for slot in range(2):
        block = (packed[slot, 0], packed[slot, 1])
        store(refs, slot, attend(rows_of(query, slot), [block], lanes, scale, None, True))
    block = (packed[1 - late, 0], packed[1 - late, 1])
    store(
        refs, late, attend(rows_of(query, late), [block], lanes, scale, load(refs, late), False)
    )


def split(code):
    return code % 2, (code // 2) % 2, code // 4


def code_of(codes, number):
    return codes[number : number + 1, 0:1][0, 0]


def remote(lanes, scale, code, query, packed, refs):
    late, source_late, before = split(code)
    mine = jnp.where(before == 1, 1 - late, late)
    theirs = jnp.where(before == 1, 1 - source_late, source_late)
    for slot, source_slot in ((mine, theirs), (late, 1 - source_late)):
        block = (packed[source_slot, 0], packed[source_slot, 1])
        state = attend(rows_of(query, slot), [block], lanes, scale, load(refs, slot), False)
        store(refs, slot, state)


def finish(state, staged, out, slot, done):
    result = state[2] * (1.0 / state[1])
    staged[slot] = result.astype(staged.dtype).T
    half = staged.shape[1]
    rows = pl.ds(pl.multiple_of(slot * half, half), half)
    pltpu.make_async_copy(staged.at[slot], out.at[rows], done.at[slot]).start()


def settle(staged, out, done):
    half = staged.shape[1]
    for slot in range(2):
        rows = pl.ds(slot * half, half)
        pltpu.make_async_copy(staged.at[slot], out.at[rows], done.at[slot]).wait()


def middle_kernel(lanes, scale, numbers, codes, query, *rest):
    blocks, before, refs = rest[: len(numbers)], rest[-6:-3], rest[-3:]
    for slot in range(2):
        store(refs, slot, load(before, slot))
    for number, packed in zip(numbers, blocks, strict=True):
        remote(lanes, scale, code_of(codes, number), query, packed, refs)


def last_kernel(lanes, scale, numbers, choose, codes, query, *rest):
    blocks = rest[: len(numbers)]
    refs, out, staged, done = rest[-6:-3], rest[-3], rest[-2], rest[-1]
    chosen = pick(choose, lax.axis_index("seq"))
    code = code_of(codes, numbers[0])
    for place in range(1, len(numbers)):
        code = jnp.where(chosen == place, code_of(codes, numbers[place]), code)

    def take(slot):
        parts = []
        for which in range(2):
            value = blocks[0][slot, which]
            for place in range(1, len(numbers)):
                value = jnp.where(chosen == place, blocks[place][slot, which], value)
            parts.append(value)
        return tuple(parts)

    late, source_late, before = split(code)
    early = 1 - late

    @pl.when(before == 1)
    def _():
        block = take(1 - source_late)
        for slot in (early, late):
            state = attend(rows_of(query, slot), [block], lanes, scale, load(refs, slot), False)
            finish(state, staged, out, slot, done)

    @pl.when(before == 0)
    def _():
        finish(load(refs, early), staged, out, early, done)
        pair = [take(0), take(1)]
        state = attend(rows_of(query, late), pair, lanes, scale, load(refs, late), False)
        finish(state, staged, out, late, done)

    settle(staged, out, done)


def gathered_kernel(lanes, scale, order, query, blocks, *rest):
    before, out, staged, done, refs = rest[:3], rest[3], rest[4], rest[5], rest[6:]
    me = lax.axis_index("seq")
    count = blocks.shape[0]
    for slot in range(2):
        store(refs, slot, load(before, slot))

    def step(index, carry):
        source = lax.rem(me + index, count)
        code = order_of(order, me, source)
        remote(lanes, scale, code, query, blocks.at[source], refs)
        return carry

    lax.fori_loop(1, count, step, 0)
    for slot in range(2):
        finish(load(refs, slot), staged, out, slot, done)
    settle(staged, out, done)


def on_device(queries, keys, values, block_order):
    tokens, heads, width = queries.shape
    groups = keys.shape[1]
    half = tokens // 2
    devices = lax.axis_size("seq")
    scale = width ** (-0.5) * LOG2E
    lanes = (groups, heads)
    rows = tokens * heads
    query = queries.reshape(rows, width)

    def pack(array):
        split = array.reshape(2, half, groups, width)
        return jnp.transpose(split, (0, 2, 1, 3)).reshape(2, 1, groups * half, width)

    packed = jnp.concatenate([pack(keys), pack(values)], axis=1)
    shapes = [
        jax.ShapeDtypeStruct((2, 1, rows // 2), jnp.float32),
        jax.ShapeDtypeStruct((2, 1, rows // 2), jnp.float32),
        jax.ShapeDtypeStruct((2, width, rows // 2), jnp.float32),
    ]
    result = jax.ShapeDtypeStruct((rows, width), queries.dtype)
    staging = [
        pltpu.VMEM((2, rows // 2, width), queries.dtype),
        pltpu.SemaphoreType.DMA((2,)),
    ]
    vmem = pl.BlockSpec(memory_space=pltpu.VMEM)
    smem = pl.BlockSpec(memory_space=pltpu.SMEM)
    anywhere = pl.BlockSpec(memory_space=pl.ANY)

    def call(kernel, tasks, first, blocks, state, out_shape, out_specs, scratch=(), first_spec=vmem):
        inputs = [first, query, *blocks, *state]
        return pl.pallas_call(
            functools.partial(kernel, lanes, scale),
            out_shape=out_shape,
            in_specs=[first_spec] + [vmem] * (len(inputs) - 1),
            out_specs=out_specs,
            scratch_shapes=scratch,
            compiler_params=pltpu.CompilerParams(vmem_limit_bytes=16 * 2**20),
            cost_estimate=pl.CostEstimate(
                flops=4 * tasks * groups * half * rows // 2 * width,
                bytes_accessed=rows * width * 2,
                transcendentals=tasks * half * rows,
            ),
        )(*inputs)

    def own(sources):
        codes = jax.ShapeDtypeStruct((8, 128), jnp.int32)

        def kernel(lanes, scale, *refs):
            own_kernel(lanes, scale, sources, *refs)

        return call(
            kernel, 3, block_order, [packed], [], [*shapes, codes], [vmem] * 4, first_spec=smem
        )

    def permute(value, pairs):
        return lax.ppermute(value, "seq", pairs)

    if devices == 4:
        first = permute(packed, [(0, 2), (3, 1), (1, 0), (2, 3)])
        second = permute(packed, [(1, 3), (2, 0), (0, 1), (3, 2)])
        inner = permute(packed, [(1, 2), (2, 1), (0, 0), (3, 3)])
        *state, codes = own([(1, 3, 0, 2), (2, 0, 3, 1), (0, 2, 1, 3), (3, 0, 3, 0)])
        outer = permute(first, [(2, 3), (1, 0), (0, 1), (3, 2)])

        def middle(lanes, scale, *refs):
            middle_kernel(lanes, scale, (0, 1), *refs)

        state = call(middle, 4, codes, [first, second], state, shapes, [vmem] * 3)

        def last(lanes, scale, *refs):
            last_kernel(lanes, scale, (2, 3), (1, 0, 0, 1), *refs)

        out = call(last, 2, codes, [inner, outer], state, result, anywhere, staging)
    else:
        blocks = lax.all_gather(packed, "seq", axis=0, tiled=False)
        *state, codes = own([])
        out = call(
            gathered_kernel,
            2 * devices,
            block_order,
            [blocks],
            state,
            result,
            anywhere,
            staging + [pltpu.VMEM(s.shape, s.dtype) for s in shapes],
            first_spec=smem,
        )
    return out.reshape(tokens, heads, width)


def solution(mesh):
    placed = (
        P(("grp", "seq"), "head", None),
        P(("grp", "seq"), "head", None),
        P(("grp", "seq"), "head", None),
        P("grp"),
    )
    return jax.shard_map(
        on_device,
        mesh=mesh,
        in_specs=placed,
        out_specs=P(("grp", "seq"), "head", None),
        check_vma=False,
    )
```

time: 17.3 us -> 16.5 us (0.954)
  Pallas kernels: 5.14 us -> 4 us
  waiting for transfers between devices: 3.86 us -> 4.36 us
    pallas_call x3, Pallas kernels: 5.14 us -> 4 us  [call(): pl.pallas_call(functools.partial(kernel, lanes, scale), out_shape=out_sha...]
    ppermute x4, waiting for transfers between devices: 3.86 us -> 4.36 us  [permute(): return lax.ppermute(value, 'seq', pairs)]
  transfers between devices with their start and end apart: 4 -> 4, of which waited for: 3 -> 3; matrix products, arithmetic and copies ran while one was open for 0% -> 0% of each run, Pallas kernels for 18% -> 16%
where the time goes in v3:
time: 16.5 us
  starting transfers between devices  7.14 us (43%)
  waiting for transfers between devices  4.36 us (26%)
  Pallas kernels  4 us (24%)
  local copies, waits for them, and re-layouts  0.92 us (6%)
    ppermute x4, starting transfers between devices, permute(): return lax.ppermute(value, 'seq', pairs)  7.14 us
    ppermute x4, waiting for transfers between devices, permute(): return lax.ppermute(value, 'seq', pairs)  4.36 us
    pallas_call x3, Pallas kernels, call(): pl.pallas_call(functools.partial(kernel, lanes, scale), out_shape=out_sha...  4 us
    reshape x2, local copies, waits for them, and re-layouts, pack(): split = array.reshape(2, half, groups, width)  0.91 us
  transfers between devices with their start and end apart: 4, of which 3 were waited for; matrix products, arithmetic and copies ran while one was open for 0% of the time, Pallas kernels for 16%

profile of v3, /device:TPU:0, one launch (start us, length us, event | category | flops | bytes accessed | tf_op | source)
XLA Modules:
  0.0 16.5 jit_solution(1212285387727984180)
XLA Ops:
  0.0 0.0 copy-start.2
  0.0 0.0 copy-start
  0.0 0.9 %copy.5 = bf16[2,64,2,128]{3,1,2,0:T(8,128)(2,1)S(1)} copy(bf16[2,64,2,128]{3,2,1,0:T(2,128)(2,1)} %bitcast.15) | data formatting | bytes 131072 | tf_op jit(solution)/shard_map/reshape | solution.py:212
  0.9 0.0 copy-done.2
  1.0 0.0 copy-start.1
  1.0 4.1 %collective-permute-start.1 = (bf16[2,2,128,128]{3,2,1,0:T(8,128)(2,1)S(1)}, bf16[2,2,128,128]{3,2,1,0:T(8,128)(2,1)S(1)}, u32[]{:S(2)}, u32[]{:S(2)}) collective-permute-start(bf16[2,2,128,128]{3,2,1,0:T(8,128)(2,1)S(1)} %pad_maximum_fusion.refs_2_), channel_id=1, source_target_pairs={{0,8},{12,4},{4,0},{8,12},{1,9},{13,5},{5,1},{9,13},{2,10},{14,6},... | collective-permute-start | bytes 393224 | tf_op jit(solution)/shard_map/ppermute | solution.py:257
  5.1 0.0 collective-permute-start.3
  5.1 0.7 %collective-permute-start = (bf16[2,2,128,128]{3,2,1,0:T(8,128)(2,1)S(1)}, bf16[2,2,128,128]{3,2,1,0:T(8,128)(2,1)S(1)}, u32[]{:S(2)}, u32[]{:S(2)}) collective-permute-start(bf16[2,2,128,128]{3,2,1,0:T(8,128)(2,1)S(1)} %pad_maximum_fusion.refs_2_), channel_id=1, source_target_pairs={{4,8},{8,4},{0,0},{12,12},{5,9},{9,5},{1,1},{13,13},{6,10},{10,6},... | collective-permute-start | bytes 393224 | tf_op jit(solution)/shard_map/ppermute | solution.py:257
  5.8 3.2 %collective-permute-done.1.refs_2_ = bf16[2,2,128,128]{3,2,1,0:T(8,128)(2,1)S(1)} collective-permute-done((bf16[2,2,128,128]{3,2,1,0:T(8,128)(2,1)S(1)}, bf16[2,2,128,128]{3,2,1,0:T(8,128)(2,1)S(1)}, u32[]{:S(2)}, u32[]{:S(2)}) %collective-permute-start.1) | collective-permute-done | bytes 131104 | tf_op jit(solution)/shard_map/ppermute | solution.py:257
  9.0 2.4 %collective-permute-start.2 = (bf16[2,2,128,128]{3,2,1,0:T(8,128)(2,1)S(1)}, bf16[2,2,128,128]{3,2,1,0:T(8,128)(2,1)S(1)}, u32[]{:S(2)}, u32[]{:S(2)}) collective-permute-start(bf16[2,2,128,128]{3,2,1,0:T(8,128)(2,1)S(1)} %collective-permute-done.1.refs_2_), channel_id=1, source_target_pairs={{8,12},{4,0},{0,4},{12,8},{9,13},{5,1},{1,5},{13,9},{10,14},{6,2},... | collective-permute-start | bytes 393224 | tf_op jit(solution)/shard_map/ppermute | solution.py:257
  11.3 0.0 copy-done
  11.3 0.0 copy-done.1
  11.3 1.4 %shard_map.46 = (f32[2,1,512]{2,1,0:T(1,128)S(1)}, f32[2,1,512]{2,1,0:T(1,128)S(1)}, f32[2,128,512]{2,1,0:T(8,128)S(1)}, s32[8,128]{1,0:T(8,128)S(1)}) custom-call(s32[8]{0:T(128)S(1)} %copy-done.1, bf16[1024,128]{1,0:T(8,128)(2,1)S(1)} %bitcast.10, bf16[2,2,128,128]{3,2,1,0:T(8,128)(2,1)S(1)} %pad_maximum_fusion.refs_2_), custom_call_target="tpu_custom_call" | custom-call | flops 100663296 | bytes 262144 | tf_op jit(solution)/shard_map/pallas_call | solution.py:232
  12.7 0.3 %collective-permute-done.3.refs_3_ = bf16[2,2,128,128]{3,2,1,0:T(8,128)(2,1)S(1)} collective-permute-done((bf16[2,2,128,128]{3,2,1,0:T(8,128)(2,1)S(1)}, bf16[2,2,128,128]{3,2,1,0:T(8,128)(2,1)S(1)}, u32[]{:S(2)}, u32[]{:S(2)}) %collective-permute-start.3) | collective-permute-done | bytes 131104 | tf_op jit(solution)/shard_map/ppermute | solution.py:257
  13.0 1.2 %shard_map.47 = (f32[2,1,512]{2,1,0:T(1,128)S(1)}, f32[2,1,512]{2,1,0:T(1,128)S(1)}, f32[2,128,512]{2,1,0:T(8,128)S(1)}) custom-call(s32[8,128]{1,0:T(8,128)S(1)} %get-tuple-element.12.refs_0_, bf16[1024,128]{1,0:T(8,128)(2,1)S(1)} %bitcast.11, bf16[2,2,128,128]{3,2,1,0:T(8,128)(2,1)S(1)} %collective-permute-done.1.refs_2_, ...), custom_call_target="tpu_custom_call" | custom-call | flops 134217728 | bytes 262144 | tf_op jit(solution)/shard_map/pallas_call | solution.py:232
  14.2 0.0 collective-permute-done.refs_2_
  14.2 0.9 %collective-permute-done.2.refs_3_ = bf16[2,2,128,128]{3,2,1,0:T(8,128)(2,1)S(1)} collective-permute-done((bf16[2,2,128,128]{3,2,1,0:T(8,128)(2,1)S(1)}, bf16[2,2,128,128]{3,2,1,0:T(8,128)(2,1)S(1)}, u32[]{:S(2)}, u32[]{:S(2)}) %collective-permute-start.2) | collective-permute-done | bytes 131104 | tf_op jit(solution)/shard_map/ppermute | solution.py:257
  15.1 1.4 %shard_map.48 = bf16[1024,128]{1,0:T(8,128)(2,1)} custom-call(s32[8,128]{1,0:T(8,128)S(1)} %get-tuple-element.12.refs_0_, bf16[1024,128]{1,0:T(8,128)(2,1)S(1)} %bitcast.12, bf16[2,2,128,128]{3,2,1,0:T(8,128)(2,1)S(1)} %collective-permute-done.refs_2_, bf16[2,2,128,128]{3,2,1,0:T(8,128)(2,1)S(1)} %collective-permute-done.2.refs_3_, ...), custom_call_target="tpu_custom_call" | custom-call | flops 67108864 | bytes 262144 | tf_op jit(solution)/shard_map/pallas_call | solution.py:232
  (2 shorter events, 0.0 us)
Async XLA Ops:
  0.0 0.9 %copy-start.2 = (bf16[128,2,128]{2,1,0:T(2,128)(2,1)S(1)}, bf16[128,2,128]{2,1,0:T(2,128)(2,1)}, u32[]{:S(2)}) copy-start(bf16[128,2,128]{2,1,0:T(2,128)(2,1)} %param.6) | copy-start | bytes 196612
  0.0 11.3 %copy-start = (bf16[128,8,128]{2,1,0:T(8,128)(2,1)S(1)}, bf16[128,8,128]{2,1,0:T(8,128)(2,1)}, u32[]{:S(2)}) copy-start(bf16[128,8,128]{2,1,0:T(8,128)(2,1)} %param.4) | copy-start | bytes 786436
  1.0 10.4 %copy-start.1 = (s32[8]{0:T(128)S(1)}, s32[8]{0:T(128)}, u32[]{:S(2)}) copy-start(s32[8]{0:T(128)} %refs_0_.1) | copy-start | bytes 100
  1.0 8.0 %collective-permute-start.1 = (bf16[2,2,128,128]{3,2,1,0:T(8,128)(2,1)S(1)}, bf16[2,2,128,128]{3,2,1,0:T(8,128)(2,1)S(1)}, u32[]{:S(2)}, u32[]{:S(2)}) collective-permute-start(bf16[2,2,128,128]{3,2,1,0:T(8,128)(2,1)S(1)} %pad_maximum_fusion.refs_2_), channel_id=1, source_target_pairs={{0,8},{12,4},{4,0},{8,12},{1,9},{13,5},{5,1},{9,13},{2,10},{14,6},... | collective-permute-start | bytes 393224 | tf_op jit(solution)/shard_map/ppermute | solution.py:257
  5.1 7.9 %collective-permute-start.3 = (bf16[2,2,128,128]{3,2,1,0:T(8,128)(2,1)S(1)}, bf16[2,2,128,128]{3,2,1,0:T(8,128)(2,1)S(1)}, u32[]{:S(2)}, u32[]{:S(2)}) collective-permute-start(bf16[2,2,128,128]{3,2,1,0:T(8,128)(2,1)S(1)} %pad_maximum_fusion.refs_2_), channel_id=1, source_target_pairs={{4,12},{8,0},{0,4},{12,8},{5,13},{9,1},{1,5},{13,9},{6,14},{10,2},... | collective-permute-start | bytes 393224 | tf_op jit(solution)/shard_map/ppermute | solution.py:257
  5.1 9.1 %collective-permute-start = (bf16[2,2,128,128]{3,2,1,0:T(8,128)(2,1)S(1)}, bf16[2,2,128,128]{3,2,1,0:T(8,128)(2,1)S(1)}, u32[]{:S(2)}, u32[]{:S(2)}) collective-permute-start(bf16[2,2,128,128]{3,2,1,0:T(8,128)(2,1)S(1)} %pad_maximum_fusion.refs_2_), channel_id=1, source_target_pairs={{4,8},{8,4},{0,0},{12,12},{5,9},{9,5},{1,1},{13,13},{6,10},{10,6},... | collective-permute-start | bytes 393224 | tf_op jit(solution)/shard_map/ppermute | solution.py:257
  9.0 6.1 %collective-permute-start.2 = (bf16[2,2,128,128]{3,2,1,0:T(8,128)(2,1)S(1)}, bf16[2,2,128,128]{3,2,1,0:T(8,128)(2,1)S(1)}, u32[]{:S(2)}, u32[]{:S(2)}) collective-permute-start(bf16[2,2,128,128]{3,2,1,0:T(8,128)(2,1)S(1)} %collective-permute-done.1.refs_2_), channel_id=1, source_target_pairs={{8,12},{4,0},{0,4},{12,8},{9,13},{5,1},{1,5},{13,9},{10,14},{6,2},... | collective-permute-start | bytes 393224 | tf_op jit(solution)/shard_map/ppermute | solution.py:257

commit v4 on v3

--- a/solution.py
+++ b/solution.py
@@ -18,7 +18,7 @@
     return value
 
 
-def attend(query, blocks, lanes, scale, state, diagonal):
+def score(query, blocks, lanes, scale, diagonal):
     groups, per_token = lanes
     rows = query.shape[0]
     keys = blocks[0][0].shape[0] // groups
@@ -37,6 +37,13 @@
             place = lax.broadcasted_iota(jnp.int32, (keys, rows), 0)
             part = jnp.where(place <= lane // per_token, part, LOW)
         parts.append(part)
+    return parts
+
+
+def weigh(parts, blocks, lanes, state):
+    groups, per_token = lanes
+    lane = lax.broadcasted_iota(jnp.int32, parts[0].shape, 1)
+    group = (lane % per_token) // (per_token // groups)
     top = functools.reduce(jnp.maximum, [jnp.max(part, axis=0, keepdims=True) for part in parts])
     if state is not None:
         top = jnp.maximum(top, state[0])
@@ -60,6 +67,10 @@
     return top, state[1] * factor + total, state[2] * factor + product
 
 
+def attend(query, blocks, lanes, scale, state, diagonal):
+    return weigh(score(query, blocks, lanes, scale, diagonal), blocks, lanes, state)
+
+
 def load(refs, slot):
     return tuple(ref[slot] for ref in refs)
 
@@ -83,22 +94,21 @@
     return late + 2 * source_late + 4 * before
 
 
-def own_kernel(lanes, scale, sources, order, query, packed, top, total, acc, codes):
-    me = lax.axis_index("seq")
-    refs = (top, total, acc)
-    row = lax.broadcasted_iota(jnp.int32, codes.shape, 0)
-    value = jnp.zeros(codes.shape, jnp.int32)
-    for number, table in enumerate(sources):
-        value = jnp.where(row == number, order_of(order, me, pick(table, me)), value)
-    codes[...] = value
+def diagonal_kernel(lanes, scale, query, packed, *refs):
+    blocks = [(packed[slot, 0], packed[slot, 1]) for slot in range(2)]
+    queries = [rows_of(query, slot) for slot in range(2)]
+    parts = [score(queries[slot], [blocks[slot]], lanes, scale, True) for slot in range(2)]
+    for slot in range(2):
+        store(refs, slot, weigh(parts[slot], [blocks[slot]], lanes, None))
+
+
+def cross(lanes, scale, order, me, query, packed, before, refs):
     late = jnp.where(order[2 * me] < order[2 * me + 1], 1, 0)
-    for slot in range(2):
-        block = (packed[slot, 0], packed[slot, 1])
-        store(refs, slot, attend(rows_of(query, slot), [block], lanes, scale, None, True))
-    block = (packed[1 - late, 0], packed[1 - late, 1])
-    store(
-        refs, late, attend(rows_of(query, late), [block], lanes, scale, load(refs, late), False)
-    )
+    early = 1 - late
+    store(refs, early, load(before, early))
+    block = (packed[early, 0], packed[early, 1])
+    state = attend(rows_of(query, late), [block], lanes, scale, load(before, late), False)
+    store(refs, late, state)
 
 
 def split(code):
@@ -134,12 +144,19 @@
         pltpu.make_async_copy(staged.at[slot], out.at[rows], done.at[slot]).wait()
 
 
-def middle_kernel(lanes, scale, numbers, codes, query, *rest):
-    blocks, before, refs = rest[: len(numbers)], rest[-6:-3], rest[-3:]
-    for slot in range(2):
-        store(refs, slot, load(before, slot))
-    for number, packed in zip(numbers, blocks, strict=True):
-        remote(lanes, scale, code_of(codes, number), query, packed, refs)
+def middle_kernel(lanes, scale, sources, order, query, packed, *rest):
+    count = len(rest) - 7
+    blocks, before, refs, codes = rest[:count], rest[count : count + 3], rest[count + 3 : -1], rest[-1]
+    me = lax.axis_index("seq")
+    row = lax.broadcasted_iota(jnp.int32, codes.shape, 0)
+    value = jnp.zeros(codes.shape, jnp.int32)
+    numbers = [order_of(order, me, pick(table, me)) for table in sources]
+    for place, number in enumerate(numbers):
+        value = jnp.where(row == place, number, value)
+    codes[...] = value
+    cross(lanes, scale, order, me, query, packed, before, refs)
+    for number, block in zip(numbers, blocks):
+        remote(lanes, scale, number, query, block, refs)
 
 
 def last_kernel(lanes, scale, numbers, choose, codes, query, *rest):
@@ -165,9 +182,10 @@
     @pl.when(before == 1)
     def _():
         block = take(1 - source_late)
-        for slot in (early, late):
-            state = attend(rows_of(query, slot), [block], lanes, scale, load(refs, slot), False)
-            finish(state, staged, out, slot, done)
+        parts = [score(rows_of(query, slot), [block], lanes, scale, False) for slot in range(2)]
+        states = [weigh(parts[slot], [block], lanes, load(refs, slot)) for slot in range(2)]
+        for slot in range(2):
+            finish(states[slot], staged, out, slot, done)
 
     @pl.when(before == 0)
     def _():
@@ -179,12 +197,11 @@
     settle(staged, out, done)
 
 
-def gathered_kernel(lanes, scale, order, query, blocks, *rest):
+def gathered_kernel(lanes, scale, order, query, packed, blocks, *rest):
     before, out, staged, done, refs = rest[:3], rest[3], rest[4], rest[5], rest[6:]
     me = lax.axis_index("seq")
     count = blocks.shape[0]
-    for slot in range(2):
-        store(refs, slot, load(before, slot))
+    cross(lanes, scale, order, me, query, packed, before, refs)
 
     def step(index, carry):
         source = lax.rem(me + index, count)
@@ -227,12 +244,11 @@
     smem = pl.BlockSpec(memory_space=pltpu.SMEM)
     anywhere = pl.BlockSpec(memory_space=pl.ANY)
 
-    def call(kernel, tasks, first, blocks, state, out_shape, out_specs, scratch=(), first_spec=vmem):
-        inputs = [first, query, *blocks, *state]
+    def call(kernel, tasks, inputs, out_shape, out_specs, scratch=(), scalars=False):
         return pl.pallas_call(
             functools.partial(kernel, lanes, scale),
             out_shape=out_shape,
-            in_specs=[first_spec] + [vmem] * (len(inputs) - 1),
+            in_specs=[smem if scalars else vmem] + [vmem] * (len(inputs) - 1),
             out_specs=out_specs,
             scratch_shapes=scratch,
             compiler_params=pltpu.CompilerParams(vmem_limit_bytes=16 * 2**20),
@@ -243,49 +259,36 @@
             ),
         )(*inputs)
 
-    def own(sources):
-        codes = jax.ShapeDtypeStruct((8, 128), jnp.int32)
-
-        def kernel(lanes, scale, *refs):
-            own_kernel(lanes, scale, sources, *refs)
-
-        return call(
-            kernel, 3, block_order, [packed], [], [*shapes, codes], [vmem] * 4, first_spec=smem
-        )
-
     def permute(value, pairs):
         return lax.ppermute(value, "seq", pairs)
 
     if devices == 4:
         first = permute(packed, [(0, 2), (3, 1), (1, 0), (2, 3)])
+        state = call(diagonal_kernel, 2, [query, packed], shapes, [vmem] * 3)
+        packed, state = lax.optimization_barrier((packed, state))
         second = permute(packed, [(1, 3), (2, 0), (0, 1), (3, 2)])
         inner = permute(packed, [(1, 2), (2, 1), (0, 0), (3, 3)])
-        *state, codes = own([(1, 3, 0, 2), (2, 0, 3, 1), (0, 2, 1, 3), (3, 0, 3, 0)])
         outer = permute(first, [(2, 3), (1, 0), (0, 1), (3, 2)])
 
         def middle(lanes, scale, *refs):
-            middle_kernel(lanes, scale, (0, 1), *refs)
-
-        state = call(middle, 4, codes, [first, second], state, shapes, [vmem] * 3)
+            sources = [(1, 3, 0, 2), (2, 0, 3, 1), (0, 2, 1, 3), (3, 0, 3, 0)]
+            middle_kernel(lanes, scale, sources, *refs)
+
+        codes = jax.ShapeDtypeStruct((8, 128), jnp.int32)
+        inputs = [block_order, query, packed, first, second, *state]
+        *state, codes = call(middle, 5, inputs, [*shapes, codes], [vmem] * 4, scalars=True)
 
         def last(lanes, scale, *refs):
             last_kernel(lanes, scale, (2, 3), (1, 0, 0, 1), *refs)
 
-        out = call(last, 2, codes, [inner, outer], state, result, anywhere, staging)
+        inputs = [codes, query, inner, outer, *state]
+        out = call(last, 2, inputs, result, anywhere, staging)
     else:
         blocks = lax.all_gather(packed, "seq", axis=0, tiled=False)
-        *state, codes = own([])
-        out = call(
-            gathered_kernel,
-            2 * devices,
-            block_order,
-            [blocks],
-            state,
-            result,
-            anywhere,
-            staging + [pltpu.VMEM(s.shape, s.dtype) for s in shapes],
-            first_spec=smem,
-        )
+        state = call(diagonal_kernel, 2, [query, packed], shapes, [vmem] * 3)
+        inputs = [block_order, query, packed, blocks, *state]
+        scratch = staging + [pltpu.VMEM(s.shape, s.dtype) for s in shapes]
+        out = call(gathered_kernel, 2 * devices, inputs, result, anywhere, scratch, scalars=True)
     return out.reshape(tokens, heads, width)
 
 

time: 16.5 us -> 16.7 us (1.012); the launches traced: 16.5 us -> 16.5 us
  waiting for transfers between devices: 4.36 us -> 4.9 us
  Pallas kernels: 4 us -> 3.66 us
  starting transfers between devices: 7.14 us -> 6.95 us
    ppermute x4, waiting for transfers between devices: 4.36 us -> 4.9 us  [permute(): return lax.ppermute(value, 'seq', pairs)]
    pallas_call x3, Pallas kernels: 4 us -> 3.66 us  [call(): pl.pallas_call(functools.partial(kernel, lanes, scale), out_shape=out_sha...]
    ppermute x4, starting transfers between devices: 7.14 us -> 6.95 us  [permute(): return lax.ppermute(value, 'seq', pairs)]
  transfers between devices with their start and end apart: 4 -> 4, of which waited for: 3 -> 3; matrix products, arithmetic and copies ran while one was open for 0% -> 0% of each run, Pallas kernels for 16% -> 14%
where the time goes in v4:
time: 16.7 us; the launch traced here: 16.5 us
  starting transfers between devices  6.95 us (42%)
  waiting for transfers between devices  4.9 us (29%)
  Pallas kernels  3.66 us (22%)
  local copies, waits for them, and re-layouts  0.92 us (6%)
    ppermute x4, starting transfers between devices, permute(): return lax.ppermute(value, 'seq', pairs)  6.95 us
    ppermute x4, waiting for transfers between devices, permute(): return lax.ppermute(value, 'seq', pairs)  4.9 us
    pallas_call x3, Pallas kernels, call(): pl.pallas_call(functools.partial(kernel, lanes, scale), out_shape=out_sha...  3.66 us
    reshape x2, local copies, waits for them, and re-layouts, pack(): split = array.reshape(2, half, groups, width)  0.91 us
  transfers between devices with their start and end apart: 4, of which 3 were waited for; matrix products, arithmetic and copies ran while one was open for 0% of the time, Pallas kernels for 14%

profile of v4, /device:TPU:0, one launch (start us, length us, event | category | flops | bytes accessed | tf_op | source)
XLA Modules:
  0.0 16.5 jit_solution(5638379319786673085)
XLA Ops:
  0.0 0.0 copy-start.2
  0.0 0.0 copy-start
  0.0 0.9 %copy.5 = bf16[2,64,2,128]{3,1,2,0:T(8,128)(2,1)S(1)} copy(bf16[2,64,2,128]{3,2,1,0:T(2,128)(2,1)} %bitcast.15) | data formatting | bytes 131072 | tf_op jit(solution)/shard_map/reshape | solution.py:229
  0.9 0.0 copy-done.2
  1.0 4.1 %collective-permute-start = (bf16[2,2,128,128]{3,2,1,0:T(8,128)(2,1)S(1)}, bf16[2,2,128,128]{3,2,1,0:T(8,128)(2,1)S(1)}, u32[]{:S(2)}, u32[]{:S(2)}) collective-permute-start(bf16[2,2,128,128]{3,2,1,0:T(8,128)(2,1)S(1)} %pad_maximum_fusion.packed.refs_2_), channel_id=1, source_target_pairs={{0,8},{12,4},{4,0},{8,12},{1,9},{13,5},{5,1},{9,13},{2,10},{14,6},... | collective-permute-start | bytes 393224 | tf_op jit(solution)/shard_map/ppermute | solution.py:263
  5.1 0.0 copy-done
  5.1 0.5 %shard_map.46 = (f32[2,1,512]{2,1,0:T(1,128)S(1)}, f32[2,1,512]{2,1,0:T(1,128)S(1)}, f32[2,128,512]{2,1,0:T(8,128)S(1)}) custom-call(bf16[1024,128]{1,0:T(8,128)(2,1)S(1)} %bitcast.10, bf16[2,2,128,128]{3,2,1,0:T(8,128)(2,1)S(1)} %pad_maximum_fusion.packed.refs_2_), custom_call_target="tpu_custom_call" | custom-call | flops 67108864 | bytes 262144 | tf_op jit(solution)/shard_map/pallas_call | solution.py:248
  5.5 0.0 copy-start.1
  5.5 0.1 collective-permute-start.1
  5.6 0.7 %collective-permute-start.2 = (bf16[2,2,128,128]{3,2,1,0:T(8,128)(2,1)S(1)}, bf16[2,2,128,128]{3,2,1,0:T(8,128)(2,1)S(1)}, u32[]{:S(2)}, u32[]{:S(2)}) collective-permute-start(bf16[2,2,128,128]{3,2,1,0:T(8,128)(2,1)S(1)} %pad_maximum_fusion.packed.refs_2_), channel_id=1, source_target_pairs={{4,8},{8,4},{0,0},{12,12},{5,9},{9,5},{1,1},{13,13},{6,10},{10,6},... | collective-permute-start | bytes 393224 | tf_op jit(solution)/shard_map/ppermute | solution.py:263
  6.3 2.7 %collective-permute-done.refs_3_ = bf16[2,2,128,128]{3,2,1,0:T(8,128)(2,1)S(1)} collective-permute-done((bf16[2,2,128,128]{3,2,1,0:T(8,128)(2,1)S(1)}, bf16[2,2,128,128]{3,2,1,0:T(8,128)(2,1)S(1)}, u32[]{:S(2)}, u32[]{:S(2)}) %collective-permute-start) | collective-permute-done | bytes 131104 | tf_op jit(solution)/shard_map/ppermute | solution.py:263
  9.0 2.1 %collective-permute-start.3 = (bf16[2,2,128,128]{3,2,1,0:T(8,128)(2,1)S(1)}, bf16[2,2,128,128]{3,2,1,0:T(8,128)(2,1)S(1)}, u32[]{:S(2)}, u32[]{:S(2)}) collective-permute-start(bf16[2,2,128,128]{3,2,1,0:T(8,128)(2,1)S(1)} %collective-permute-done.refs_3_), channel_id=1, source_target_pairs={{8,12},{4,0},{0,4},{12,8},{9,13},{5,1},{1,5},{13,9},{10,14},{6,2},... | collective-permute-start | bytes 393224 | tf_op jit(solution)/shard_map/ppermute | solution.py:263
  11.1 2.0 %collective-permute-done.1.refs_4_ = bf16[2,2,128,128]{3,2,1,0:T(8,128)(2,1)S(1)} collective-permute-done((bf16[2,2,128,128]{3,2,1,0:T(8,128)(2,1)S(1)}, bf16[2,2,128,128]{3,2,1,0:T(8,128)(2,1)S(1)}, u32[]{:S(2)}, u32[]{:S(2)}) %collective-permute-start.1) | collective-permute-done | bytes 131104 | tf_op jit(solution)/shard_map/ppermute | solution.py:263
  13.1 0.0 copy-done.1
  13.1 1.9 %shard_map.47 = (f32[2,1,512]{2,1,0:T(1,128)S(1)}, f32[2,1,512]{2,1,0:T(1,128)S(1)}, f32[2,128,512]{2,1,0:T(8,128)S(1)}, s32[8,128]{1,0:T(8,128)S(1)}) custom-call(s32[8]{0:T(128)S(1)} %copy-done.1, bf16[1024,128]{1,0:T(8,128)(2,1)S(1)} %bitcast.11, bf16[2,2,128,128]{3,2,1,0:T(8,128)(2,1)S(1)} %pad_maximum_fusion.packed.refs_2_, ...), custom_call_target="tpu_custom_call" | custom-call | flops 167772160 | bytes 262144 | tf_op jit(solution)/shard_map/pallas_call | solution.py:248
  15.0 0.0 collective-permute-done.2.refs_2_
  15.0 0.2 %collective-permute-done.3.refs_3_ = bf16[2,2,128,128]{3,2,1,0:T(8,128)(2,1)S(1)} collective-permute-done((bf16[2,2,128,128]{3,2,1,0:T(8,128)(2,1)S(1)}, bf16[2,2,128,128]{3,2,1,0:T(8,128)(2,1)S(1)}, u32[]{:S(2)}, u32[]{:S(2)}) %collective-permute-start.3) | collective-permute-done | bytes 131104 | tf_op jit(solution)/shard_map/ppermute | solution.py:263
  15.3 1.3 %shard_map.48 = bf16[1024,128]{1,0:T(8,128)(2,1)} custom-call(s32[8,128]{1,0:T(8,128)S(1)} %get-tuple-element.23.refs_0_, bf16[1024,128]{1,0:T(8,128)(2,1)S(1)} %bitcast.12, bf16[2,2,128,128]{3,2,1,0:T(8,128)(2,1)S(1)} %collective-permute-done.2.refs_2_, bf16[2,2,128,128]{3,2,1,0:T(8,128)(2,1)S(1)} %collective-permute-done.3.refs_3_, ...), custom_call_target="tpu_custom_call" | custom-call | flops 67108864 | bytes 262144 | tf_op jit(solution)/shard_map/pallas_call | solution.py:248
  (2 shorter events, 0.0 us)
Async XLA Ops:
  0.0 0.9 %copy-start.2 = (bf16[128,2,128]{2,1,0:T(2,128)(2,1)S(1)}, bf16[128,2,128]{2,1,0:T(2,128)(2,1)}, u32[]{:S(2)}) copy-start(bf16[128,2,128]{2,1,0:T(2,128)(2,1)} %param.6) | copy-start | bytes 196612
  0.0 5.1 %copy-start = (bf16[128,8,128]{2,1,0:T(8,128)(2,1)S(1)}, bf16[128,8,128]{2,1,0:T(8,128)(2,1)}, u32[]{:S(2)}) copy-start(bf16[128,8,128]{2,1,0:T(8,128)(2,1)} %param.4) | copy-start | bytes 786436
  1.0 8.0 %collective-permute-start = (bf16[2,2,128,128]{3,2,1,0:T(8,128)(2,1)S(1)}, bf16[2,2,128,128]{3,2,1,0:T(8,128)(2,1)S(1)}, u32[]{:S(2)}, u32[]{:S(2)}) collective-permute-start(bf16[2,2,128,128]{3,2,1,0:T(8,128)(2,1)S(1)} %pad_maximum_fusion.packed.refs_2_), channel_id=1, source_target_pairs={{0,8},{12,4},{4,0},{8,12},{1,9},{13,5},{5,1},{9,13},{2,10},{14,6},... | collective-permute-start | bytes 393224 | tf_op jit(solution)/shard_map/ppermute | solution.py:263
  5.5 7.6 %copy-start.1 = (s32[8]{0:T(128)S(1)}, s32[8]{0:T(128)}, u32[]{:S(2)}) copy-start(s32[8]{0:T(128)} %refs_0_.1) | copy-start | bytes 100
  5.5 7.5 %collective-permute-start.1 = (bf16[2,2,128,128]{3,2,1,0:T(8,128)(2,1)S(1)}, bf16[2,2,128,128]{3,2,1,0:T(8,128)(2,1)S(1)}, u32[]{:S(2)}, u32[]{:S(2)}) collective-permute-start(bf16[2,2,128,128]{3,2,1,0:T(8,128)(2,1)S(1)} %pad_maximum_fusion.packed.refs_2_), channel_id=1, source_target_pairs={{4,12},{8,0},{0,4},{12,8},{5,13},{9,1},{1,5},{13,9},{6,14},{10,2},... | collective-permute-start | bytes 393224 | tf_op jit(solution)/shard_map/ppermute | solution.py:263
  5.6 9.4 %collective-permute-start.2 = (bf16[2,2,128,128]{3,2,1,0:T(8,128)(2,1)S(1)}, bf16[2,2,128,128]{3,2,1,0:T(8,128)(2,1)S(1)}, u32[]{:S(2)}, u32[]{:S(2)}) collective-permute-start(bf16[2,2,128,128]{3,2,1,0:T(8,128)(2,1)S(1)} %pad_maximum_fusion.packed.refs_2_), channel_id=1, source_target_pairs={{4,8},{8,4},{0,0},{12,12},{5,9},{9,5},{1,1},{13,13},{6,10},{10,6},... | collective-permute-start | bytes 393224 | tf_op jit(solution)/shard_map/ppermute | solution.py:263
  9.0 6.3 %collective-permute-start.3 = (bf16[2,2,128,128]{3,2,1,0:T(8,128)(2,1)S(1)}, bf16[2,2,128,128]{3,2,1,0:T(8,128)(2,1)S(1)}, u32[]{:S(2)}, u32[]{:S(2)}) collective-permute-start(bf16[2,2,128,128]{3,2,1,0:T(8,128)(2,1)S(1)} %collective-permute-done.refs_3_), channel_id=1, source_target_pairs={{8,12},{4,0},{0,4},{12,8},{9,13},{5,1},{1,5},{13,9},{10,14},{6,2},... | collective-permute-start | bytes 393224 | tf_op jit(solution)/shard_map/ppermute | solution.py:263

commit v5 on v4

v5 whole, which is shorter than its diff:
```python
import functools

import jax
import jax.numpy as jnp
from jax import lax
from jax.experimental import pallas as pl
from jax.experimental.pallas import tpu as pltpu
from jax.sharding import PartitionSpec as P


ROUTE = (
    ("o1", "packed", ((0, 2), (3, 1), (1, 0), (2, 3))),
    ("o2", "packed", ((1, 3), (2, 0), (0, 1), (3, 2))),
    ("x", "packed:0", ((0, 3), (3, 0), (1, 2), (2, 1))),
    ("z", "o1:1", ((0, 1), (1, 0), (2, 3), (3, 2))),
    ("y", "packed:1", ((1, 2), (2, 1), (0, 0), (3, 3))),
)
SOURCES = (
    ((("o1",),), (0, 0, 0, 0)),
    ((("o2",),), (0, 0, 0, 0)),
    ((("x", "z"), ("x", "y")), (0, 1, 1, 0)),
)
LOW = -1e30
LOG2E = 1.4426950408889634


def pick(table, index):
    value = jnp.int32(table[0])
    for place in range(1, len(table)):
        value = jnp.where(index == place, jnp.int32(table[place]), value)
    return value


def score(query, blocks, lanes, scale, diagonal):
    groups, per_token = lanes
    rows = query.shape[0]
    keys = blocks[0][0].shape[0] // groups
    lane = lax.broadcasted_iota(jnp.int32, (keys, rows), 1)
    group = (lane % per_token) // (per_token // groups)
    parts = []
    for key, _ in blocks:
        both = lax.dot_general(
            key, query, (((1,), (1,)), ((), ())), preferred_element_type=jnp.float32
        )
        part = both[:keys]
        for g in range(1, groups):
            part = jnp.where(group == g, both[g * keys : (g + 1) * keys], part)
        part = part * scale
        if diagonal:
            place = lax.broadcasted_iota(jnp.int32, (keys, rows), 0)
            part = jnp.where(place <= lane // per_token, part, LOW)
        parts.append(part)
    return parts


def weigh(parts, blocks, lanes, state):
    groups, per_token = lanes
    lane = lax.broadcasted_iota(jnp.int32, parts[0].shape, 1)
    group = (lane % per_token) // (per_token // groups)
    top = functools.reduce(jnp.maximum, [jnp.max(part, axis=0, keepdims=True) for part in parts])
    if state is not None:
        top = jnp.maximum(top, state[0])
    total = 0.0
    spread = []
    for part in parts:
        weights = jnp.exp2(part - top)
        total = total + jnp.sum(weights, axis=0, keepdims=True)
        rounded = weights.astype(jnp.bfloat16)
        nothing = jnp.zeros_like(rounded)
        spread += [jnp.where(group == g, rounded, nothing) for g in range(groups)]
    product = lax.dot_general(
        jnp.concatenate([value for _, value in blocks], axis=0),
        jnp.concatenate(spread, axis=0),
        (((0,), (0,)), ((), ())),
        preferred_element_type=jnp.float32,
    )
    if state is None:
        return top, total, product
    factor = jnp.exp2(state[0] - top)
    return top, state[1] * factor + total, state[2] * factor + product


def attend(query, blocks, lanes, scale, state, diagonal):
    return weigh(score(query, blocks, lanes, scale, diagonal), blocks, lanes, state)


def load(refs, slot):
    return tuple(ref[slot] for ref in refs)


def store(refs, slot, state):
    for ref, part in zip(refs, state, strict=True):
        ref[slot] = part


def rows_of(ref, slot):
    half = ref.shape[0] // 2
    return ref[pl.ds(pl.multiple_of(slot * half, half), half), :]


def order_of(order, me, source):
    mine, theirs = order[2 * me], order[2 * source]
    mine_too, theirs_too = order[2 * me + 1], order[2 * source + 1]
    late = jnp.where(mine < mine_too, 1, 0)
    source_late = jnp.where(theirs < theirs_too, 1, 0)
    before = jnp.where(jnp.minimum(theirs, theirs_too) < jnp.minimum(mine, mine_too), 1, 0)
    return late + 2 * source_late + 4 * before


def diagonal_kernel(lanes, scale, sources, order, query, packed, top, total, acc, codes, known, arrived):
    copy = pltpu.make_async_copy(order, known, arrived)
    copy.start()
    blocks = [(packed[slot, 0], packed[slot, 1]) for slot in range(2)]
    queries = [rows_of(query, slot) for slot in range(2)]
    parts = [score(queries[slot], [blocks[slot]], lanes, scale, True) for slot in range(2)]
    for slot in range(2):
        store((top, total, acc), slot, weigh(parts[slot], [blocks[slot]], lanes, None))
    copy.wait()
    me = lax.axis_index("seq")
    row = lax.broadcasted_iota(jnp.int32, codes.shape, 0)
    value = jnp.zeros(codes.shape, jnp.int32)
    for place, table in enumerate(sources):
        value = jnp.where(row == place, order_of(known, me, pick(table, me)), value)
    codes[...] = value


def split(code):
    return code % 2, (code // 2) % 2, code // 4


def code_of(codes, number):
    return codes[number : number + 1, 0:1][0, 0]


def fetch(option, slot, which):
    if len(option) == 1:
        return option[0][slot, which]
    if isinstance(slot, int):
        return option[slot][0, which]
    return jnp.where(slot == 0, option[0][0, which], option[1][0, which])


def chooser(options, chosen):
    def take(slot):
        parts = []
        for which in range(2):
            value = fetch(options[0], slot, which)
            for place in range(1, len(options)):
                value = jnp.where(chosen == place, fetch(options[place], slot, which), value)
            parts.append(value)
        return tuple(parts)

    return take


def group(refs, shape):
    options = []
    for length in shape:
        options.append(refs[:length])
        refs = refs[length:]
    return options


def remote(lanes, scale, code, query, take, extra, refs, emit):
    late, source_late, before = split(code)
    early = 1 - late
    more = [extra(early)] if extra else []

    @pl.when(before == 1)
    def _():
        block = take(1 - source_late)
        early_parts = score(rows_of(query, early), [block], lanes, scale, False)
        late_parts = score(rows_of(query, late), [block, *more], lanes, scale, False)
        early_state = weigh(early_parts, [block], lanes, load(refs, early))
        late_state = weigh(late_parts, [block, *more], lanes, load(refs, late))
        emit(early, early_state)
        emit(late, late_state)

    @pl.when(before == 0)
    def _():
        emit(early, load(refs, early))
        blocks = [take(0), take(1), *more]
        emit(late, attend(rows_of(query, late), blocks, lanes, scale, load(refs, late), False))


def finish(state, staged, out, slot, done):
    result = state[2] * (1.0 / state[1])
    staged[slot] = result.astype(staged.dtype).T
    half = staged.shape[1]
    rows = pl.ds(pl.multiple_of(slot * half, half), half)
    pltpu.make_async_copy(staged.at[slot], out.at[rows], done.at[slot]).start()


def settle(staged, out, done):
    half = staged.shape[1]
    for slot in range(2):
        rows = pl.ds(slot * half, half)
        pltpu.make_async_copy(staged.at[slot], out.at[rows], done.at[slot]).wait()


def stage_kernel(lanes, scale, number, shape, choose, first, codes, query, *rest):
    blocks, before, after = rest[:-6], rest[-6:-3], rest[-3:]
    extra = None
    if first:
        own, blocks = blocks[0], blocks[1:]

        def extra(early):
            return own[early, 0], own[early, 1]

    take = chooser(group(blocks, shape), pick(choose, lax.axis_index("seq")))

    def emit(slot, state):
        store(after, slot, state)

    remote(lanes, scale, code_of(codes, number), query, take, extra, before, emit)


def last_kernel(lanes, scale, number, shape, choose, codes, query, *rest):
    blocks, before, out, staged, done = rest[:-6], rest[-6:-3], rest[-3], rest[-2], rest[-1]
    take = chooser(group(blocks, shape), pick(choose, lax.axis_index("seq")))

    def emit(slot, state):
        finish(state, staged, out, slot, done)

    remote(lanes, scale, code_of(codes, number), query, take, None, before, emit)
    settle(staged, out, done)


def gathered_kernel(lanes, scale, order, query, packed, blocks, *rest):
    before, out, staged, done, refs = rest[:3], rest[3], rest[4], rest[5], rest[6:]
    me = lax.axis_index("seq")
    count = blocks.shape[0]
    late = jnp.where(order[2 * me] < order[2 * me + 1], 1, 0)
    early = 1 - late
    store(refs, early, load(before, early))
    own = (packed[early, 0], packed[early, 1])
    store(refs, late, attend(rows_of(query, late), [own], lanes, scale, load(before, late), False))

    def emit(slot, state):
        store(refs, slot, state)

    def step(index, carry):
        source = lax.rem(me + index, count)
        take = chooser([[blocks.at[source]]], 0)
        remote(lanes, scale, order_of(order, me, source), query, take, None, refs, emit)
        return carry

    lax.fori_loop(1, count, step, 0)
    for slot in range(2):
        finish(load(refs, slot), staged, out, slot, done)
    settle(staged, out, done)


def on_device(queries, keys, values, block_order):
    tokens, heads, width = queries.shape
    groups = keys.shape[1]
    half = tokens // 2
    devices = lax.axis_size("seq")
    scale = width ** (-0.5) * LOG2E
    lanes = (groups, heads)
    rows = tokens * heads
    query = queries.reshape(rows, width)

    def pack(array):
        split = array.reshape(2, half, groups, width)
        return jnp.transpose(split, (0, 2, 1, 3)).reshape(2, 1, groups * half, width)

    packed = jnp.concatenate([pack(keys), pack(values)], axis=1)
    shapes = [
        jax.ShapeDtypeStruct((2, 1, rows // 2), jnp.float32),
        jax.ShapeDtypeStruct((2, 1, rows // 2), jnp.float32),
        jax.ShapeDtypeStruct((2, width, rows // 2), jnp.float32),
    ]
    result = jax.ShapeDtypeStruct((rows, width), queries.dtype)
    staging = [
        pltpu.VMEM((2, rows // 2, width), queries.dtype),
        pltpu.SemaphoreType.DMA((2,)),
    ]
    vmem = pl.BlockSpec(memory_space=pltpu.VMEM)
    smem = pl.BlockSpec(memory_space=pltpu.SMEM)
    anywhere = pl.BlockSpec(memory_space=pl.ANY)

    def call(kernel, tasks, inputs, specs, out_shape, out_specs, scratch=()):
        return pl.pallas_call(
            functools.partial(kernel, lanes, scale),
            out_shape=out_shape,
            in_specs=specs + [vmem] * (len(inputs) - len(specs)),
            out_specs=out_specs,
            scratch_shapes=scratch,
            compiler_params=pltpu.CompilerParams(vmem_limit_bytes=16 * 2**20),
            cost_estimate=pl.CostEstimate(
                flops=4 * tasks * groups * half * rows // 2 * width,
                bytes_accessed=rows * width * 2,
                transcendentals=tasks * half * rows,
            ),
        )(*inputs)

    def diagonal(sources):
        def kernel(lanes, scale, *refs):
            diagonal_kernel(lanes, scale, sources, *refs)

        codes = jax.ShapeDtypeStruct((8, 128), jnp.int32)
        scratch = [pltpu.SMEM(block_order.shape, jnp.int32), pltpu.SemaphoreType.DMA]
        inputs = [block_order, query, packed]
        return call(kernel, 2, inputs, [anywhere], [*shapes, codes], [vmem] * 4, scratch)

    if devices == len(ROUTE[0][2]):
        held = {"packed": tuple(range(devices))}
        for name, sent, pairs in ROUTE:
            source = dict((target, origin) for origin, target in pairs)
            held[name] = tuple(held[sent.partition(":")[0]][source[i]] for i in range(devices))
        tables = [
            tuple(held[options[choose[i]][0]][i] for i in range(devices))
            for options, choose in SOURCES
        ]
        got = {"packed": packed}
        for name, sent, pairs in ROUTE:
            base, _, half_of = sent.partition(":")
            value = got[base]
            if half_of:
                value = value[int(half_of) : int(half_of) + 1]
            got[name] = lax.ppermute(value, "seq", pairs)
        *state, codes = diagonal(tables)
        final = len(SOURCES) - 1
        for stage, (options, choose) in enumerate(SOURCES[:final]):
            buffers = [got[name] for option in options for name in option]
            if stage == 0:
                buffers = [packed, *buffers]
            form = (stage, tuple(map(len, options)), choose, stage == 0)

            def kernel(lanes, scale, *refs, form=form):
                stage_kernel(lanes, scale, *form, *refs)

            inputs = [codes, query, *buffers, *state]
            state = call(kernel, 3, inputs, [], shapes, [vmem] * 3)

        options, choose = SOURCES[final]
        form = (final, tuple(map(len, options)), choose)

        def kernel(lanes, scale, *refs):
            last_kernel(lanes, scale, *form, *refs)

        inputs = [codes, query, *[got[name] for option in options for name in option], *state]
        out = call(kernel, 2, inputs, [], result, anywhere, staging)
    else:
        blocks = lax.all_gather(packed, "seq", axis=0, tiled=False)
        *state, _ = diagonal([])
        inputs = [block_order, query, packed, blocks, *state]
        scratch = staging + [pltpu.VMEM(s.shape, s.dtype) for s in shapes]
        out = call(gathered_kernel, 2 * devices, inputs, [smem], result, anywhere, scratch)
    return out.reshape(tokens, heads, width)


def solution(mesh):
    placed = (
        P(("grp", "seq"), "head", None),
        P(("grp", "seq"), "head", None),
        P(("grp", "seq"), "head", None),
        P("grp"),
    )

    return jax.shard_map(
        on_device,
        mesh=mesh,
        in_specs=placed,
        out_specs=P(("grp", "seq"), "head", None),
        check_vma=False,
    )
```

time: 16.7 us -> 16.6 us (level)
  starting transfers between devices: 6.95 us -> 10.3 us
  waiting for transfers between devices: 4.9 us -> 2.14 us
  Pallas kernels: 3.66 us -> 3.01 us
    ppermute x4 -> x5, starting transfers between devices: 6.95 us -> 10.3 us  [on_device(): got[name] = lax.ppermute(value, 'seq', pairs)]
    ppermute x4 -> x5, waiting for transfers between devices: 4.9 us -> 2.14 us  [on_device(): got[name] = lax.ppermute(value, 'seq', pairs)]
    pallas_call x3 -> x4, Pallas kernels: 3.66 us -> 3.01 us  [call(): pl.pallas_call(functools.partial(kernel, lanes, scale), out_shape=out_sha...]
  transfers between devices with their start and end apart: 4 -> 5, of which waited for: 3 -> 4; matrix products, arithmetic and copies ran while one was open for 0% -> 0% of each run, Pallas kernels for 14% -> 11%
where the time goes in v5:
time: 16.6 us; the launch traced here: 16.5 us
  starting transfers between devices  10.3 us (62%)
  Pallas kernels  3.01 us (18%)
  waiting for transfers between devices  2.14 us (13%)
  local copies, waits for them, and re-layouts  0.91 us (5%)
    ppermute x5, starting transfers between devices, on_device(): got[name] = lax.ppermute(value, 'seq', pairs)  10.3 us
    pallas_call x4, Pallas kernels, call(): pl.pallas_call(functools.partial(kernel, lanes, scale), out_shape=out_sha...  3.01 us
    ppermute x5, waiting for transfers between devices, on_device(): got[name] = lax.ppermute(value, 'seq', pairs)  2.14 us
    reshape x2, local copies, waits for them, and re-layouts, pack(): split = array.reshape(2, half, groups, width)  0.89 us
  transfers between devices with their start and end apart: 5, of which 4 were waited for; matrix products, arithmetic and copies ran while one was open for 0% of the time, Pallas kernels for 11%

profile of v5, /device:TPU:0, one launch (start us, length us, event | category | flops | bytes accessed | tf_op | source)
XLA Modules:
  0.0 16.5 jit_solution(16557364971586018352)
XLA Ops:
  0.0 0.0 copy-start.2
  0.0 0.9 %copy.5 = bf16[2,64,2,128]{3,1,2,0:T(8,128)(2,1)S(1)} copy(bf16[2,64,2,128]{3,2,1,0:T(2,128)(2,1)} %bitcast.18) | data formatting | bytes 131072 | tf_op jit(solution)/shard_map/reshape | solution.py:265
  0.9 0.0 copy-done.2
  0.9 0.0 copy-start
  1.0 4.1 %collective-permute-start.1 = (bf16[2,2,128,128]{3,2,1,0:T(8,128)(2,1)S(1)}, bf16[2,2,128,128]{3,2,1,0:T(8,128)(2,1)S(1)}, u32[]{:S(2)}, u32[]{:S(2)}) collective-permute-start(bf16[2,2,128,128]{3,2,1,0:T(8,128)(2,1)S(1)} %pad_maximum_fusion.refs_2_), channel_id=1, source_target_pairs={{0,8},{12,4},{4,0},{8,12},{1,9},{13,5},{5,1},{9,13},{2,10},{14,6},... | collective-permute-start | bytes 393224 | tf_op jit(solution)/shard_map/ppermute | solution.py:322
  5.1 0.0 collective-permute-start.4
  5.1 3.1 %collective-permute-start = (bf16[1,2,128,128]{3,2,1,0:T(8,128)(2,1)S(1)}, bf16[1,2,128,128]{3,2,1,0:T(8,128)(2,1)S(1)}, u32[]{:S(2)}, u32[]{:S(2)}) collective-permute-start(bf16[1,2,128,128]{3,2,1,0:T(8,128)(2,1)S(1)} %get-tuple-element.26), channel_id=1, source_target_pairs={{0,12},{12,0},{4,8},{8,4},{1,13},{13,1},{5,9},{9,5},{2,14},{14,2},... | collective-permute-start | bytes 196616 | tf_op jit(solution)/shard_map/ppermute | solution.py:322
  8.2 0.7 %collective-permute-start.3 = (bf16[1,2,128,128]{3,2,1,0:T(8,128)(2,1)S(1)}, bf16[1,2,128,128]{3,2,1,0:T(8,128)(2,1)S(1)}, u32[]{:S(2)}, u32[]{:S(2)}) collective-permute-start(bf16[1,2,128,128]{3,2,1,0:T(8,128)(2,1)S(1)} %get-tuple-element.25), channel_id=1, source_target_pairs={{4,8},{8,4},{0,0},{12,12},{5,9},{9,5},{1,1},{13,13},{6,10},{10,6},... | collective-permute-start | bytes 196616 | tf_op jit(solution)/shard_map/ppermute | solution.py:322
  8.9 0.1 collective-permute-done.1.refs_3_
  9.0 0.0 copy-start.1
  9.0 2.4 %collective-permute-start.2 = (bf16[1,2,128,128]{3,2,1,0:T(8,128)(2,1)S(1)}, bf16[1,2,128,128]{3,2,1,0:T(8,128)(2,1)S(1)}, u32[]{:S(2)}, u32[]{:S(2)}) collective-permute-start(bf16[1,2,128,128]{3,2,1,0:T(8,128)(2,1)S(1)} %slice.14), channel_id=1, source_target_pairs={{0,4},{4,0},{8,12},{12,8},{1,5},{5,1},{9,13},{13,9},{2,6},{6,2},{1... | collective-permute-start | bytes 196616 | tf_op jit(solution)/shard_map/ppermute | solution.py:322
  11.4 0.0 copy-done
  11.4 0.0 copy-done.1
  11.4 0.6 %shard_map.46 = (f32[2,1,512]{2,1,0:T(1,128)S(1)}, f32[2,1,512]{2,1,0:T(1,128)S(1)}, f32[2,128,512]{2,1,0:T(8,128)S(1)}, s32[8,128]{1,0:T(8,128)S(1)}) custom-call(s32[8]{0:T(128)S(1)} %copy-done.1, bf16[1024,128]{1,0:T(8,128)(2,1)S(1)} %bitcast.10, bf16[2,2,128,128]{3,2,1,0:T(8,128)(2,1)S(1)} %pad_maximum_fusion.refs_2_), custom_call_target="tpu_custom_call" | custom-call | flops 67108864 | bytes 262144 | tf_op jit(solution)/shard_map/pallas_call | solution.py:284
  12.0 0.6 %shard_map.47 = (f32[2,1,512]{2,1,0:T(1,128)S(1)}, f32[2,1,512]{2,1,0:T(1,128)S(1)}, f32[2,128,512]{2,1,0:T(8,128)S(1)}) custom-call(s32[8,128]{1,0:T(8,128)S(1)} %get-tuple-element.15.refs_0_, bf16[1024,128]{1,0:T(8,128)(2,1)S(1)} %bitcast.11, bf16[2,2,128,128]{3,2,1,0:T(8,128)(2,1)S(1)} %pad_maximum_fusion.refs_2_, ...), custom_call_target="tpu_custom_call" | custom-call | flops 100663296 | bytes 262144 | tf_op jit(solution)/shard_map/pallas_call | solution.py:284
  12.6 1.3 %collective-permute-done.4.refs_2_ = bf16[2,2,128,128]{3,2,1,0:T(8,128)(2,1)S(1)} collective-permute-done((bf16[2,2,128,128]{3,2,1,0:T(8,128)(2,1)S(1)}, bf16[2,2,128,128]{3,2,1,0:T(8,128)(2,1)S(1)}, u32[]{:S(2)}, u32[]{:S(2)}) %collective-permute-start.4) | collective-permute-done | bytes 131104 | tf_op jit(solution)/shard_map/ppermute | solution.py:322
  14.0 0.5 %shard_map.48 = (f32[2,1,512]{2,1,0:T(1,128)S(1)}, f32[2,1,512]{2,1,0:T(1,128)S(1)}, f32[2,128,512]{2,1,0:T(8,128)S(1)}) custom-call(s32[8,128]{1,0:T(8,128)S(1)} %get-tuple-element.15.refs_0_, bf16[1024,128]{1,0:T(8,128)(2,1)S(1)} %bitcast.12, bf16[2,2,128,128]{3,2,1,0:T(8,128)(2,1)S(1)} %collective-permute-done.4.refs_2_, ...), custom_call_target="tpu_custom_call" | custom-call | flops 100663296 | bytes 262144 | tf_op jit(solution)/shard_map/pallas_call | solution.py:284
  14.5 0.1 collective-permute-done.refs_2_.refs_4_
  14.6 0.0 collective-permute-done.3.refs_5_
  14.7 0.6 %collective-permute-done.2.refs_3_ = bf16[1,2,128,128]{3,2,1,0:T(8,128)(2,1)S(1)} collective-permute-done((bf16[1,2,128,128]{3,2,1,0:T(8,128)(2,1)S(1)}, bf16[1,2,128,128]{3,2,1,0:T(8,128)(2,1)S(1)}, u32[]{:S(2)}, u32[]{:S(2)}) %collective-permute-start.2) | collective-permute-done | bytes 65568 | tf_op jit(solution)/shard_map/ppermute | solution.py:322
  15.2 1.3 %shard_map.49 = bf16[1024,128]{1,0:T(8,128)(2,1)} custom-call(s32[8,128]{1,0:T(8,128)S(1)} %get-tuple-element.15.refs_0_, bf16[1024,128]{1,0:T(8,128)(2,1)S(1)} %bitcast.13, bf16[1,2,128,128]{3,2,1,0:T(8,128)(2,1)S(1)} %collective-permute-done.refs_2_.refs_4_, bf16[1,2,128,128]{3,2,1,0:T(8,128)(2,1)S(1)} %collective-permute-done.2.refs_3_, ...), custom_call_target="tpu_custom_call" | custom-call | flops 67108864 | bytes 262144 | tf_op jit(solution)/shard_map/pallas_call | solution.py:284
  (4 shorter events, 0.0 us)
Async XLA Ops:
  0.0 0.9 %copy-start.2 = (bf16[128,2,128]{2,1,0:T(2,128)(2,1)S(1)}, bf16[128,2,128]{2,1,0:T(2,128)(2,1)}, u32[]{:S(2)}) copy-start(bf16[128,2,128]{2,1,0:T(2,128)(2,1)} %param.6) | copy-start | bytes 196612
  0.9 10.5 %copy-start = (bf16[128,8,128]{2,1,0:T(8,128)(2,1)S(1)}, bf16[128,8,128]{2,1,0:T(8,128)(2,1)}, u32[]{:S(2)}) copy-start(bf16[128,8,128]{2,1,0:T(8,128)(2,1)} %param.4) | copy-start | bytes 786436
  1.0 8.0 %collective-permute-start.1 = (bf16[2,2,128,128]{3,2,1,0:T(8,128)(2,1)S(1)}, bf16[2,2,128,128]{3,2,1,0:T(8,128)(2,1)S(1)}, u32[]{:S(2)}, u32[]{:S(2)}) collective-permute-start(bf16[2,2,128,128]{3,2,1,0:T(8,128)(2,1)S(1)} %pad_maximum_fusion.refs_2_), channel_id=1, source_target_pairs={{0,8},{12,4},{4,0},{8,12},{1,9},{13,5},{5,1},{9,13},{2,10},{14,6},... | collective-permute-start | bytes 393224 | tf_op jit(solution)/shard_map/ppermute | solution.py:322
  5.1 8.9 %collective-permute-start.4 = (bf16[2,2,128,128]{3,2,1,0:T(8,128)(2,1)S(1)}, bf16[2,2,128,128]{3,2,1,0:T(8,128)(2,1)S(1)}, u32[]{:S(2)}, u32[]{:S(2)}) collective-permute-start(bf16[2,2,128,128]{3,2,1,0:T(8,128)(2,1)S(1)} %pad_maximum_fusion.refs_2_), channel_id=1, source_target_pairs={{4,12},{8,0},{0,4},{12,8},{5,13},{9,1},{1,5},{13,9},{6,14},{10,2},... | collective-permute-start | bytes 393224 | tf_op jit(solution)/shard_map/ppermute | solution.py:322
  5.1 9.6 %collective-permute-start = (bf16[1,2,128,128]{3,2,1,0:T(8,128)(2,1)S(1)}, bf16[1,2,128,128]{3,2,1,0:T(8,128)(2,1)S(1)}, u32[]{:S(2)}, u32[]{:S(2)}) collective-permute-start(bf16[1,2,128,128]{3,2,1,0:T(8,128)(2,1)S(1)} %get-tuple-element.26), channel_id=1, source_target_pairs={{0,12},{12,0},{4,8},{8,4},{1,13},{13,1},{5,9},{9,5},{2,14},{14,2},... | collective-permute-start | bytes 196616 | tf_op jit(solution)/shard_map/ppermute | solution.py:322
  8.2 6.5 %collective-permute-start.3 = (bf16[1,2,128,128]{3,2,1,0:T(8,128)(2,1)S(1)}, bf16[1,2,128,128]{3,2,1,0:T(8,128)(2,1)S(1)}, u32[]{:S(2)}, u32[]{:S(2)}) collective-permute-start(bf16[1,2,128,128]{3,2,1,0:T(8,128)(2,1)S(1)} %get-tuple-element.25), channel_id=1, source_target_pairs={{4,8},{8,4},{0,0},{12,12},{5,9},{9,5},{1,1},{13,13},{6,10},{10,6},... | collective-permute-start | bytes 196616 | tf_op jit(solution)/shard_map/ppermute | solution.py:322
  9.0 2.4 %copy-start.1 = (s32[8]{0:T(128)S(1)}, s32[8]{0:T(128)}, u32[]{:S(2)}) copy-start(s32[8]{0:T(128)} %refs_0_.1) | copy-start | bytes 100
  9.0 6.2 %collective-permute-start.2 = (bf16[1,2,128,128]{3,2,1,0:T(8,128)(2,1)S(1)}, bf16[1,2,128,128]{3,2,1,0:T(8,128)(2,1)S(1)}, u32[]{:S(2)}, u32[]{:S(2)}) collective-permute-start(bf16[1,2,128,128]{3,2,1,0:T(8,128)(2,1)S(1)} %slice.14), channel_id=1, source_target_pairs={{0,4},{4,0},{8,12},{12,8},{1,5},{5,1},{9,13},{13,9},{2,6},{6,2},{1... | collective-permute-start | bytes 196616 | tf_op jit(solution)/shard_map/ppermute | solution.py:322

commit v6 on v5

--- a/solution.py
+++ b/solution.py
@@ -11,15 +11,14 @@
 ROUTE = (
     ("o1", "packed", ((0, 2), (3, 1), (1, 0), (2, 3))),
     ("o2", "packed", ((1, 3), (2, 0), (0, 1), (3, 2))),
-    ("x", "packed:0", ((0, 3), (3, 0), (1, 2), (2, 1))),
-    ("z", "o1:1", ((0, 1), (1, 0), (2, 3), (3, 2))),
-    ("y", "packed:1", ((1, 2), (2, 1), (0, 0), (3, 3))),
+    ("x", "keys", ((0, 3), (3, 0), (1, 2), (2, 1))),
+    ("z", "o1", ((0, 1), (1, 0), (2, 3), (3, 2))),
+    ("y", "values", ((1, 2), (2, 1), (0, 0), (3, 3))),
 )
-SOURCES = (
-    ((("o1",),), (0, 0, 0, 0)),
-    ((("o2",),), (0, 0, 0, 0)),
-    ((("x", "z"), ("x", "y")), (0, 1, 1, 0)),
-)
+WHOLE = ("o1", "o2")
+LAST_KEYS = "x"
+LAST_VALUES = ("z", "y")
+CHOICE = (0, 1, 1, 0)
 LOW = -1e30
 LOG2E = 1.4426950408889634
 
@@ -53,7 +52,7 @@
     return parts
 
 
-def weigh(parts, blocks, lanes, state):
+def soften(parts, lanes, state):
     groups, per_token = lanes
     lane = lax.broadcasted_iota(jnp.int32, parts[0].shape, 1)
     group = (lane % per_token) // (per_token // groups)
@@ -68,16 +67,25 @@
         rounded = weights.astype(jnp.bfloat16)
         nothing = jnp.zeros_like(rounded)
         spread += [jnp.where(group == g, rounded, nothing) for g in range(groups)]
-    product = lax.dot_general(
-        jnp.concatenate([value for _, value in blocks], axis=0),
-        jnp.concatenate(spread, axis=0),
-        (((0,), (0,)), ((), ())),
-        preferred_element_type=jnp.float32,
+    factor = None
+    if state is not None:
+        factor = jnp.exp2(state[0] - top)
+        total = state[1] * factor + total
+    return top, total, factor, jnp.concatenate(spread, axis=0)
+
+
+def multiply(value, spread):
+    return lax.dot_general(
+        value, spread, (((0,), (0,)), ((), ())), preferred_element_type=jnp.float32
     )
+
+
+def weigh(parts, blocks, lanes, state):
+    top, total, factor, spread = soften(parts, lanes, state)
+    product = multiply(jnp.concatenate([value for _, value in blocks], axis=0), spread)
     if state is None:
         return top, total, product
-    factor = jnp.exp2(state[0] - top)
-    return top, state[1] * factor + total, state[2] * factor + product
+    return top, total, state[2] * factor + product
 
 
 def attend(query, blocks, lanes, scale, state, diagonal):
@@ -132,35 +140,6 @@
     return codes[number : number + 1, 0:1][0, 0]
 
 
-def fetch(option, slot, which):
-    if len(option) == 1:
-        return option[0][slot, which]
-    if isinstance(slot, int):
-        return option[slot][0, which]
-    return jnp.where(slot == 0, option[0][0, which], option[1][0, which])
-
-
-def chooser(options, chosen):
-    def take(slot):
-        parts = []
-        for which in range(2):
-            value = fetch(options[0], slot, which)
-            for place in range(1, len(options)):
-                value = jnp.where(chosen == place, fetch(options[place], slot, which), value)
-            parts.append(value)
-        return tuple(parts)
-
-    return take
-
-
-def group(refs, shape):
-    options = []
-    for length in shape:
-        options.append(refs[:length])
-        refs = refs[length:]
-    return options
-
-
 def remote(lanes, scale, code, query, take, extra, refs, emit):
     late, source_late, before = split(code)
     early = 1 - late
@@ -183,8 +162,7 @@
         emit(late, attend(rows_of(query, late), blocks, lanes, scale, load(refs, late), False))
 
 
-def finish(state, staged, out, slot, done):
-    result = state[2] * (1.0 / state[1])
+def finish(result, staged, out, slot, done):
     staged[slot] = result.astype(staged.dtype).T
     half = staged.shape[1]
     rows = pl.ds(pl.multiple_of(slot * half, half), half)
@@ -198,31 +176,72 @@
         pltpu.make_async_copy(staged.at[slot], out.at[rows], done.at[slot]).wait()
 
 
-def stage_kernel(lanes, scale, number, shape, choose, first, codes, query, *rest):
+def block_of(packed):
+    return lambda slot: (packed[slot, 0], packed[slot, 1])
+
+
+def stage_kernel(number, lanes, scale, codes, query, *rest):
     blocks, before, after = rest[:-6], rest[-6:-3], rest[-3:]
-    extra = None
-    if first:
-        own, blocks = blocks[0], blocks[1:]
-
-        def extra(early):
-            return own[early, 0], own[early, 1]
-
-    take = chooser(group(blocks, shape), pick(choose, lax.axis_index("seq")))
+    extra = block_of(blocks[1]) if len(blocks) > 1 else None
 
     def emit(slot, state):
         store(after, slot, state)
 
-    remote(lanes, scale, code_of(codes, number), query, take, extra, before, emit)
-
-
-def last_kernel(lanes, scale, number, shape, choose, codes, query, *rest):
-    blocks, before, out, staged, done = rest[:-6], rest[-6:-3], rest[-3], rest[-2], rest[-1]
-    take = chooser(group(blocks, shape), pick(choose, lax.axis_index("seq")))
-
-    def emit(slot, state):
-        finish(state, staged, out, slot, done)
-
-    remote(lanes, scale, code_of(codes, number), query, take, None, before, emit)
+    code = code_of(codes, number)
+    remote(lanes, scale, code, query, block_of(blocks[0]), extra, before, emit)
+
+
+def weights_kernel(number, lanes, scale, codes, query, keys, top, total, acc, spread, share, base):
+    refs = (top, total, acc)
+    late, source_late, before = split(code_of(codes, number))
+    early = 1 - late
+
+    @pl.when(before == 1)
+    def _():
+        block = (keys[1 - source_late, 0], None)
+        parts = [score(rows_of(query, slot), [block], lanes, scale, False) for slot in range(2)]
+        for slot in range(2):
+            _, new_total, factor, weights = soften(parts[slot], lanes, load(refs, slot))
+            inverse = 1.0 / new_total
+            spread[slot] = weights
+            share[slot] = inverse
+            base[slot] = acc[slot] * (factor * inverse)
+
+    @pl.when(before == 0)
+    def _():
+        blocks = [(keys[slot, 0], None) for slot in range(2)]
+        parts = score(rows_of(query, late), blocks, lanes, scale, False)
+        _, new_total, factor, weights = soften(parts, lanes, load(refs, late))
+        inverse = 1.0 / new_total
+        half = weights.shape[0] // 2
+        spread[0] = weights[:half]
+        spread[1] = weights[half:]
+        share[late] = inverse
+        base[late] = acc[late] * (factor * inverse)
+        base[early] = acc[early] * (1.0 / total[early])
+
+
+def values_kernel(number, lanes, scale, codes, near, far, spread, share, base, out, staged, done):
+    chosen = pick(CHOICE, lax.axis_index("seq"))
+    late, source_late, before = split(code_of(codes, number))
+
+    def take(slot):
+        return jnp.where(chosen == 0, near[slot, 0], far[slot, 0])
+
+    @pl.when(before == 1)
+    def _():
+        value = take(1 - source_late)
+        products = [multiply(value, spread[slot]) for slot in range(2)]
+        for slot in range(2):
+            finish(base[slot] + products[slot] * share[slot], staged, out, slot, done)
+
+    @pl.when(before == 0)
+    def _():
+        finish(base[1 - late], staged, out, 1 - late, done)
+        value = jnp.concatenate([take(0), take(1)], axis=0)
+        product = multiply(value, jnp.concatenate([spread[0], spread[1]], axis=0))
+        finish(base[late] + product * share[late], staged, out, late, done)
+
     settle(staged, out, done)
 
 
@@ -241,13 +260,14 @@
 
     def step(index, carry):
         source = lax.rem(me + index, count)
-        take = chooser([[blocks.at[source]]], 0)
+        take = block_of(blocks.at[source])
         remote(lanes, scale, order_of(order, me, source), query, take, None, refs, emit)
         return carry
 
     lax.fori_loop(1, count, step, 0)
+    _, total, acc = refs
     for slot in range(2):
-        finish(load(refs, slot), staged, out, slot, done)
+        finish(acc[slot] * (1.0 / total[slot]), staged, out, slot, done)
     settle(staged, out, done)
 
 
@@ -265,7 +285,8 @@
         split = array.reshape(2, half, groups, width)
         return jnp.transpose(split, (0, 2, 1, 3)).reshape(2, 1, groups * half, width)
 
-    packed = jnp.concatenate([pack(keys), pack(values)], axis=1)
+    halves = {"keys": pack(keys), "values": pack(values)}
+    packed = jnp.concatenate([halves["keys"], halves["values"]], axis=1)
     shapes = [
         jax.ShapeDtypeStruct((2, 1, rows // 2), jnp.float32),
         jax.ShapeDtypeStruct((2, 1, rows // 2), jnp.float32),
@@ -304,44 +325,30 @@
         inputs = [block_order, query, packed]
         return call(kernel, 2, inputs, [anywhere], [*shapes, codes], [vmem] * 4, scratch)
 
-    if devices == len(ROUTE[0][2]):
-        held = {"packed": tuple(range(devices))}
+    if devices == len(CHOICE):
+        mine = tuple(range(devices))
+        held = {name: mine for name in ("packed", *halves)}
+        got = {"packed": packed, **halves}
         for name, sent, pairs in ROUTE:
             source = dict((target, origin) for origin, target in pairs)
-            held[name] = tuple(held[sent.partition(":")[0]][source[i]] for i in range(devices))
-        tables = [
-            tuple(held[options[choose[i]][0]][i] for i in range(devices))
-            for options, choose in SOURCES
-        ]
-        got = {"packed": packed}
-        for name, sent, pairs in ROUTE:
-            base, _, half_of = sent.partition(":")
-            value = got[base]
-            if half_of:
-                value = value[int(half_of) : int(half_of) + 1]
+            held[name] = tuple(held[sent][source[i]] for i in range(devices))
+            value = got[sent]
+            if name in LAST_VALUES and value.shape[1] > 1:
+                value = value[:, 1:]
             got[name] = lax.ppermute(value, "seq", pairs)
-        *state, codes = diagonal(tables)
-        final = len(SOURCES) - 1
-        for stage, (options, choose) in enumerate(SOURCES[:final]):
-            buffers = [got[name] for option in options for name in option]
-            if stage == 0:
-                buffers = [packed, *buffers]
-            form = (stage, tuple(map(len, options)), choose, stage == 0)
-
-            def kernel(lanes, scale, *refs, form=form):
-                stage_kernel(lanes, scale, *form, *refs)
-
-            inputs = [codes, query, *buffers, *state]
+        *state, codes = diagonal([held[name] for name in (*WHOLE, LAST_KEYS)])
+        for stage, name in enumerate(WHOLE):
+            blocks = [got[name]] if stage else [got[name], packed]
+            kernel = functools.partial(stage_kernel, stage)
+            inputs = [codes, query, *blocks, *state]
             state = call(kernel, 3, inputs, [], shapes, [vmem] * 3)
-
-        options, choose = SOURCES[final]
-        form = (final, tuple(map(len, options)), choose)
-
-        def kernel(lanes, scale, *refs):
-            last_kernel(lanes, scale, *form, *refs)
-
-        inputs = [codes, query, *[got[name] for option in options for name in option], *state]
-        out = call(kernel, 2, inputs, [], result, anywhere, staging)
+        kernel = functools.partial(weights_kernel, len(WHOLE))
+        spread = jax.ShapeDtypeStruct((2, groups * half, rows // 2), jnp.bfloat16)
+        inputs = [codes, query, got[LAST_KEYS], *state]
+        state = call(kernel, 1, inputs, [], [spread, *shapes[1:]], [vmem] * 3)
+        kernel = functools.partial(values_kernel, len(WHOLE))
+        inputs = [codes, *[got[name] for name in LAST_VALUES], *state]
+        out = call(kernel, 1, inputs, [], result, anywhere, staging)
     else:
         blocks = lax.all_gather(packed, "seq", axis=0, tiled=False)
         *state, _ = diagonal([])

time: 16.6 us -> 16.4 us (0.988)
  waiting for transfers between devices: 2.14 us -> 1.77 us
  Pallas kernels: 3.01 us -> 3.2 us
    ppermute x5, waiting for transfers between devices: 2.14 us -> 1.77 us  [on_device(): got[name] = lax.ppermute(value, 'seq', pairs)]
    pallas_call x4 -> x5, Pallas kernels: 3.01 us -> 3.2 us  [call(): pl.pallas_call(functools.partial(kernel, lanes, scale), out_shape=out_sha...]
  transfers between devices with their start and end apart: 5 -> 5, of which waited for: 4 -> 4; matrix products, arithmetic and copies ran while one was open for 0% -> 0% of each run, Pallas kernels for 11% -> 13%
where the time goes in v6:
time: 16.4 us; the launch traced here: 16.2 us
  starting transfers between devices  10.2 us (62%)
  Pallas kernels  3.2 us (20%)
  waiting for transfers between devices  1.77 us (11%)
  local copies, waits for them, and re-layouts  0.91 us (6%)
    ppermute x5, starting transfers between devices, on_device(): got[name] = lax.ppermute(value, 'seq', pairs)  10.2 us
    pallas_call x5, Pallas kernels, call(): pl.pallas_call(functools.partial(kernel, lanes, scale), out_shape=out_sha...  3.2 us
    ppermute x5, waiting for transfers between devices, on_device(): got[name] = lax.ppermute(value, 'seq', pairs)  1.77 us
    reshape x2, local copies, waits for them, and re-layouts, pack(): split = array.reshape(2, half, groups, width)  0.89 us
  transfers between devices with their start and end apart: 5, of which 4 were waited for; matrix products, arithmetic and copies ran while one was open for 0% of the time, Pallas kernels for 13%

profile of v6, /device:TPU:0, one launch (start us, length us, event | category | flops | bytes accessed | tf_op | source)
XLA Modules:
  0.0 16.2 jit_solution(8798852004035409921)
XLA Ops:
  0.0 0.0 copy-start.2
  0.0 0.9 %copy.5 = bf16[2,64,2,128]{3,1,2,0:T(8,128)(2,1)S(1)} copy(bf16[2,64,2,128]{3,2,1,0:T(2,128)(2,1)} %bitcast.18) | data formatting | bytes 131072 | tf_op jit(solution)/shard_map/reshape | solution.py:285
  0.9 0.0 copy-done.2
  0.9 0.0 copy-start
  1.0 4.1 %collective-permute-start = (bf16[2,2,128,128]{3,2,1,0:T(8,128)(2,1)S(1)}, bf16[2,2,128,128]{3,2,1,0:T(8,128)(2,1)S(1)}, u32[]{:S(2)}, u32[]{:S(2)}) collective-permute-start(bf16[2,2,128,128]{3,2,1,0:T(8,128)(2,1)S(1)} %pad_maximum_fusion.refs_2_.rest_1_), channel_id=1, source_target_pairs={{0,8},{12,4},{4,0},{8,12},{1,9},{13,5},{5,1},{9,13},{2,10},{14,6},... | collective-permute-start | bytes 393224 | tf_op jit(solution)/shard_map/ppermute | solution.py:338
  5.1 0.0 collective-permute-start.4
  5.1 3.0 %collective-permute-start.3 = (bf16[2,1,128,128]{3,2,1,0:T(8,128)(2,1)S(1)}, bf16[2,1,128,128]{3,2,1,0:T(8,128)(2,1)S(1)}, u32[]{:S(2)}, u32[]{:S(2)}) collective-permute-start(bf16[2,1,128,128]{3,2,1,0:T(8,128)(2,1)S(1)} %bitcast.17), channel_id=1, source_target_pairs={{0,12},{12,0},{4,8},{8,4},{1,13},{13,1},{5,9},{9,5},{2,14},{14,2},... | collective-permute-start | bytes 196616 | tf_op jit(solution)/shard_map/ppermute | solution.py:338
  8.1 0.7 %collective-permute-start.2 = (bf16[2,1,128,128]{3,2,1,0:T(8,128)(2,1)S(1)}, bf16[2,1,128,128]{3,2,1,0:T(8,128)(2,1)S(1)}, u32[]{:S(2)}, u32[]{:S(2)}) collective-permute-start(bf16[2,1,128,128]{3,2,1,0:T(8,128)(2,1)S(1)} %bitcast.15), channel_id=1, source_target_pairs={{4,8},{8,4},{0,0},{12,12},{5,9},{9,5},{1,1},{13,13},{6,10},{10,6},... | collective-permute-start | bytes 196616 | tf_op jit(solution)/shard_map/ppermute | solution.py:338
  8.8 0.2 %collective-permute-done.rest_0_ = bf16[2,2,128,128]{3,2,1,0:T(8,128)(2,1)S(1)} collective-permute-done((bf16[2,2,128,128]{3,2,1,0:T(8,128)(2,1)S(1)}, bf16[2,2,128,128]{3,2,1,0:T(8,128)(2,1)S(1)}, u32[]{:S(2)}, u32[]{:S(2)}) %collective-permute-start) | collective-permute-done | bytes 131104 | tf_op jit(solution)/shard_map/ppermute | solution.py:338
  9.0 0.0 copy-start.1
  9.0 2.4 %collective-permute-start.1 = (bf16[2,1,128,128]{3,2,1,0:T(8,128)(2,1)S(1)}, bf16[2,1,128,128]{3,2,1,0:T(8,128)(2,1)S(1)}, u32[]{:S(2)}, u32[]{:S(2)}) collective-permute-start(bf16[2,1,128,128]{3,2,1,0:T(8,128)(2,1)S(1)} %slice.4), channel_id=1, source_target_pairs={{0,4},{4,0},{8,12},{12,8},{1,5},{5,1},{9,13},{13,9},{2,6},{6,2},{1... | collective-permute-start | bytes 196616 | tf_op jit(solution)/shard_map/ppermute | solution.py:338
  11.4 0.0 copy-done
  11.4 0.0 copy-done.1
  11.4 0.6 %shard_map.46 = (f32[2,1,512]{2,1,0:T(1,128)S(1)}, f32[2,1,512]{2,1,0:T(1,128)S(1)}, f32[2,128,512]{2,1,0:T(8,128)S(1)}, s32[8,128]{1,0:T(8,128)S(1)}) custom-call(s32[8]{0:T(128)S(1)} %copy-done.1, bf16[1024,128]{1,0:T(8,128)(2,1)S(1)} %bitcast.10, bf16[2,2,128,128]{3,2,1,0:T(8,128)(2,1)S(1)} %pad_maximum_fusion.refs_2_.rest_1_), custom_call_target="tpu_custom_call" | custom-call | flops 67108864 | bytes 262144 | tf_op jit(solution)/shard_map/pallas_call | solution.py:305
  12.0 0.6 %shard_map.47 = (f32[2,1,512]{2,1,0:T(1,128)S(1)}, f32[2,1,512]{2,1,0:T(1,128)S(1)}, f32[2,128,512]{2,1,0:T(8,128)S(1)}) custom-call(s32[8,128]{1,0:T(8,128)S(1)} %get-tuple-element.18.codes, bf16[1024,128]{1,0:T(8,128)(2,1)S(1)} %bitcast.11, bf16[2,2,128,128]{3,2,1,0:T(8,128)(2,1)S(1)} %collective-permute-done.rest_0_, ...), custom_call_target="tpu_custom_call" | custom-call | flops 100663296 | bytes 262144 | tf_op jit(solution)/shard_map/pallas_call | solution.py:305
  12.6 1.3 %collective-permute-done.4.rest_0_ = bf16[2,2,128,128]{3,2,1,0:T(8,128)(2,1)S(1)} collective-permute-done((bf16[2,2,128,128]{3,2,1,0:T(8,128)(2,1)S(1)}, bf16[2,2,128,128]{3,2,1,0:T(8,128)(2,1)S(1)}, u32[]{:S(2)}, u32[]{:S(2)}) %collective-permute-start.4) | collective-permute-done | bytes 131104 | tf_op jit(solution)/shard_map/ppermute | solution.py:338
  13.9 0.5 %shard_map.48 = (f32[2,1,512]{2,1,0:T(1,128)S(1)}, f32[2,1,512]{2,1,0:T(1,128)S(1)}, f32[2,128,512]{2,1,0:T(8,128)S(1)}) custom-call(s32[8,128]{1,0:T(8,128)S(1)} %get-tuple-element.18.codes, bf16[1024,128]{1,0:T(8,128)(2,1)S(1)} %bitcast.12, bf16[2,2,128,128]{3,2,1,0:T(8,128)(2,1)S(1)} %collective-permute-done.4.rest_0_, ...), custom_call_target="tpu_custom_call" | custom-call | flops 100663296 | bytes 262144 | tf_op jit(solution)/shard_map/pallas_call | solution.py:305
  14.4 0.2 %collective-permute-done.3.keys = bf16[2,1,128,128]{3,2,1,0:T(8,128)(2,1)S(1)} collective-permute-done((bf16[2,1,128,128]{3,2,1,0:T(8,128)(2,1)S(1)}, bf16[2,1,128,128]{3,2,1,0:T(8,128)(2,1)S(1)}, u32[]{:S(2)}, u32[]{:S(2)}) %collective-permute-start.3) | collective-permute-done | bytes 65568 | tf_op jit(solution)/shard_map/ppermute | solution.py:338
  14.6 0.4 %shard_map.49 = (bf16[2,128,512]{2,1,0:T(8,128)(2,1)S(1)}, f32[2,1,512]{2,1,0:T(1,128)S(1)}, f32[2,128,512]{2,1,0:T(8,128)S(1)}) custom-call(s32[8,128]{1,0:T(8,128)S(1)} %get-tuple-element.18.codes, bf16[1024,128]{1,0:T(8,128)(2,1)S(1)} %bitcast.13, bf16[2,1,128,128]{3,2,1,0:T(8,128)(2,1)S(1)} %collective-permute-done.3.keys, ...), custom_call_target="tpu_custom_call" | custom-call | flops 33554432 | bytes 262144 | tf_op jit(solution)/shard_map/pallas_call | solution.py:305
  15.0 0.0 collective-permute-done.2.far
  15.1 0.1 collective-permute-done.1.near
  15.2 1.1 %shard_map.50 = bf16[1024,128]{1,0:T(8,128)(2,1)} custom-call(s32[8,128]{1,0:T(8,128)S(1)} %get-tuple-element.18.codes, bf16[2,1,128,128]{3,2,1,0:T(8,128)(2,1)S(1)} %collective-permute-done.1.near, bf16[2,1,128,128]{3,2,1,0:T(8,128)(2,1)S(1)} %collective-permute-done.2.far, bf16[2,128,512]{2,1,0:T(8,128)(2,1)S(1)} %get-tuple-element.28.spread, ...), custom_call_target="tpu_custom_call" | custom-call | flops 33554432 | bytes 262144 | tf_op jit(solution)/shard_map/pallas_call | solution.py:305
  (3 shorter events, 0.0 us)
Async XLA Ops:
  0.0 0.9 %copy-start.2 = (bf16[128,2,128]{2,1,0:T(2,128)(2,1)S(1)}, bf16[128,2,128]{2,1,0:T(2,128)(2,1)}, u32[]{:S(2)}) copy-start(bf16[128,2,128]{2,1,0:T(2,128)(2,1)} %param.6) | copy-start | bytes 196612
  0.9 10.5 %copy-start = (bf16[128,8,128]{2,1,0:T(8,128)(2,1)S(1)}, bf16[128,8,128]{2,1,0:T(8,128)(2,1)}, u32[]{:S(2)}) copy-start(bf16[128,8,128]{2,1,0:T(8,128)(2,1)} %param.4) | copy-start | bytes 786436
  1.0 8.0 %collective-permute-start = (bf16[2,2,128,128]{3,2,1,0:T(8,128)(2,1)S(1)}, bf16[2,2,128,128]{3,2,1,0:T(8,128)(2,1)S(1)}, u32[]{:S(2)}, u32[]{:S(2)}) collective-permute-start(bf16[2,2,128,128]{3,2,1,0:T(8,128)(2,1)S(1)} %pad_maximum_fusion.refs_2_.rest_1_), channel_id=1, source_target_pairs={{0,8},{12,4},{4,0},{8,12},{1,9},{13,5},{5,1},{9,13},{2,10},{14,6},... | collective-permute-start | bytes 393224 | tf_op jit(solution)/shard_map/ppermute | solution.py:338
  5.1 8.8 %collective-permute-start.4 = (bf16[2,2,128,128]{3,2,1,0:T(8,128)(2,1)S(1)}, bf16[2,2,128,128]{3,2,1,0:T(8,128)(2,1)S(1)}, u32[]{:S(2)}, u32[]{:S(2)}) collective-permute-start(bf16[2,2,128,128]{3,2,1,0:T(8,128)(2,1)S(1)} %pad_maximum_fusion.refs_2_.rest_1_), channel_id=1, source_target_pairs={{4,12},{8,0},{0,4},{12,8},{5,13},{9,1},{1,5},{13,9},{6,14},{10,2},... | collective-permute-start | bytes 393224 | tf_op jit(solution)/shard_map/ppermute | solution.py:338
  5.1 9.6 %collective-permute-start.3 = (bf16[2,1,128,128]{3,2,1,0:T(8,128)(2,1)S(1)}, bf16[2,1,128,128]{3,2,1,0:T(8,128)(2,1)S(1)}, u32[]{:S(2)}, u32[]{:S(2)}) collective-permute-start(bf16[2,1,128,128]{3,2,1,0:T(8,128)(2,1)S(1)} %bitcast.17), channel_id=1, source_target_pairs={{0,12},{12,0},{4,8},{8,4},{1,13},{13,1},{5,9},{9,5},{2,14},{14,2},... | collective-permute-start | bytes 196616 | tf_op jit(solution)/shard_map/ppermute | solution.py:338
  8.1 6.9 %collective-permute-start.2 = (bf16[2,1,128,128]{3,2,1,0:T(8,128)(2,1)S(1)}, bf16[2,1,128,128]{3,2,1,0:T(8,128)(2,1)S(1)}, u32[]{:S(2)}, u32[]{:S(2)}) collective-permute-start(bf16[2,1,128,128]{3,2,1,0:T(8,128)(2,1)S(1)} %bitcast.15), channel_id=1, source_target_pairs={{4,8},{8,4},{0,0},{12,12},{5,9},{9,5},{1,1},{13,13},{6,10},{10,6},... | collective-permute-start | bytes 196616 | tf_op jit(solution)/shard_map/ppermute | solution.py:338
  9.0 2.4 %copy-start.1 = (s32[8]{0:T(128)S(1)}, s32[8]{0:T(128)}, u32[]{:S(2)}) copy-start(s32[8]{0:T(128)} %refs_0_.1) | copy-start | bytes 100
  9.0 6.2 %collective-permute-start.1 = (bf16[2,1,128,128]{3,2,1,0:T(8,128)(2,1)S(1)}, bf16[2,1,128,128]{3,2,1,0:T(8,128)(2,1)S(1)}, u32[]{:S(2)}, u32[]{:S(2)}) collective-permute-start(bf16[2,1,128,128]{3,2,1,0:T(8,128)(2,1)S(1)} %slice.4), channel_id=1, source_target_pairs={{0,4},{4,0},{8,12},{12,8},{1,5},{5,1},{9,13},{13,9},{2,6},{6,2},{1... | collective-permute-start | bytes 196616 | tf_op jit(solution)/shard_map/ppermute | solution.py:338

commit v7 on v6

--- a/solution.py
+++ b/solution.py
@@ -52,25 +52,28 @@
     return parts
 
 
-def soften(parts, lanes, state):
+def soften(parts, lanes, state, divide=False):
     groups, per_token = lanes
     lane = lax.broadcasted_iota(jnp.int32, parts[0].shape, 1)
     group = (lane % per_token) // (per_token // groups)
     top = functools.reduce(jnp.maximum, [jnp.max(part, axis=0, keepdims=True) for part in parts])
     if state is not None:
         top = jnp.maximum(top, state[0])
-    total = 0.0
-    spread = []
-    for part in parts:
-        weights = jnp.exp2(part - top)
-        total = total + jnp.sum(weights, axis=0, keepdims=True)
-        rounded = weights.astype(jnp.bfloat16)
-        nothing = jnp.zeros_like(rounded)
-        spread += [jnp.where(group == g, rounded, nothing) for g in range(groups)]
+    parts = [jnp.exp2(part - top) for part in parts]
+    total = sum(jnp.sum(weights, axis=0, keepdims=True) for weights in parts)
     factor = None
     if state is not None:
         factor = jnp.exp2(state[0] - top)
         total = state[1] * factor + total
+    if divide:
+        inverse = 1.0 / total
+        factor = factor * inverse
+        parts = [weights * inverse for weights in parts]
+    spread = []
+    for weights in parts:
+        rounded = weights.astype(jnp.bfloat16)
+        nothing = jnp.zeros_like(rounded)
+        spread += [jnp.where(group == g, rounded, nothing) for g in range(groups)]
     return top, total, factor, jnp.concatenate(spread, axis=0)
 
 
@@ -163,7 +166,7 @@
 
 
 def finish(result, staged, out, slot, done):
-    staged[slot] = result.astype(staged.dtype).T
+    staged[slot] = result.astype(staged.dtype)
     half = staged.shape[1]
     rows = pl.ds(pl.multiple_of(slot * half, half), half)
     pltpu.make_async_copy(staged.at[slot], out.at[rows], done.at[slot]).start()
@@ -191,7 +194,7 @@
     remote(lanes, scale, code, query, block_of(blocks[0]), extra, before, emit)
 
 
-def weights_kernel(number, lanes, scale, codes, query, keys, top, total, acc, spread, share, base):
+def weights_kernel(number, lanes, scale, codes, query, keys, top, total, acc, spread, base):
     refs = (top, total, acc)
     late, source_late, before = split(code_of(codes, number))
     early = 1 - late
@@ -201,46 +204,39 @@
         block = (keys[1 - source_late, 0], None)
         parts = [score(rows_of(query, slot), [block], lanes, scale, False) for slot in range(2)]
         for slot in range(2):
-            _, new_total, factor, weights = soften(parts[slot], lanes, load(refs, slot))
-            inverse = 1.0 / new_total
-            spread[slot] = weights
-            share[slot] = inverse
-            base[slot] = acc[slot] * (factor * inverse)
+            _, _, factor, weights = soften(parts[slot], lanes, load(refs, slot), True)
+            spread[slot] = weights.T
+            base[slot] = (acc[slot] * factor).T
 
     @pl.when(before == 0)
     def _():
         blocks = [(keys[slot, 0], None) for slot in range(2)]
         parts = score(rows_of(query, late), blocks, lanes, scale, False)
-        _, new_total, factor, weights = soften(parts, lanes, load(refs, late))
-        inverse = 1.0 / new_total
+        _, _, factor, weights = soften(parts, lanes, load(refs, late), True)
         half = weights.shape[0] // 2
-        spread[0] = weights[:half]
-        spread[1] = weights[half:]
-        share[late] = inverse
-        base[late] = acc[late] * (factor * inverse)
-        base[early] = acc[early] * (1.0 / total[early])
-
-
-def values_kernel(number, lanes, scale, codes, near, far, spread, share, base, out, staged, done):
+        spread[0] = weights[:half].T
+        spread[1] = weights[half:].T
+        base[late] = (acc[late] * factor).T
+        base[early] = (acc[early] * (1.0 / total[early])).T
+
+
+def values_kernel(number, lanes, scale, codes, near, far, spread, base, out, staged, done):
     chosen = pick(CHOICE, lax.axis_index("seq"))
     late, source_late, before = split(code_of(codes, number))
 
-    def take(slot):
-        return jnp.where(chosen == 0, near[slot, 0], far[slot, 0])
+    def times(slot, source_slot):
+        value = jnp.where(chosen == 0, near[source_slot, 0], far[source_slot, 0])
+        return jnp.dot(spread[slot], value, preferred_element_type=jnp.float32)
 
     @pl.when(before == 1)
     def _():
-        value = take(1 - source_late)
-        products = [multiply(value, spread[slot]) for slot in range(2)]
         for slot in range(2):
-            finish(base[slot] + products[slot] * share[slot], staged, out, slot, done)
+            finish(base[slot] + times(slot, 1 - source_late), staged, out, slot, done)
 
     @pl.when(before == 0)
     def _():
         finish(base[1 - late], staged, out, 1 - late, done)
-        value = jnp.concatenate([take(0), take(1)], axis=0)
-        product = multiply(value, jnp.concatenate([spread[0], spread[1]], axis=0))
-        finish(base[late] + product * share[late], staged, out, late, done)
+        finish(base[late] + times(0, 0) + times(1, 1), staged, out, late, done)
 
     settle(staged, out, done)
 
@@ -267,7 +263,7 @@
     lax.fori_loop(1, count, step, 0)
     _, total, acc = refs
     for slot in range(2):
-        finish(acc[slot] * (1.0 / total[slot]), staged, out, slot, done)
+        finish((acc[slot] * (1.0 / total[slot])).T, staged, out, slot, done)
     settle(staged, out, done)
 
 
@@ -343,9 +339,10 @@
             inputs = [codes, query, *blocks, *state]
             state = call(kernel, 3, inputs, [], shapes, [vmem] * 3)
         kernel = functools.partial(weights_kernel, len(WHOLE))
-        spread = jax.ShapeDtypeStruct((2, groups * half, rows // 2), jnp.bfloat16)
+        spread = jax.ShapeDtypeStruct((2, rows // 2, groups * half), jnp.bfloat16)
+        base = jax.ShapeDtypeStruct((2, rows // 2, width), jnp.float32)
         inputs = [codes, query, got[LAST_KEYS], *state]
-        state = call(kernel, 1, inputs, [], [spread, *shapes[1:]], [vmem] * 3)
+        state = call(kernel, 1, inputs, [], [spread, base], [vmem] * 2)
         kernel = functools.partial(values_kernel, len(WHOLE))
         inputs = [codes, *[got[name] for name in LAST_VALUES], *state]
         out = call(kernel, 1, inputs, [], result, anywhere, staging)

time: 16.4 us -> 16.4 us (level)
  transfers between devices with their start and end apart: 5 -> 5, of which waited for: 4 -> 3; matrix products, arithmetic and copies ran while one was open for 0% -> 0% of each run, Pallas kernels for 13% -> 14%
where the time goes in v7:
time: 16.4 us; the launch traced here: 16.3 us
  starting transfers between devices  10.2 us (62%)
  Pallas kernels  3.32 us (20%)
  waiting for transfers between devices  1.68 us (10%)
  local copies, waits for them, and re-layouts  0.91 us (6%)
    ppermute x5, starting transfers between devices, on_device(): got[name] = lax.ppermute(value, 'seq', pairs)  10.2 us
    pallas_call x5, Pallas kernels, call(): pl.pallas_call(functools.partial(kernel, lanes, scale), out_shape=out_sha...  3.32 us
    ppermute x5, waiting for transfers between devices, on_device(): got[name] = lax.ppermute(value, 'seq', pairs)  1.68 us
    reshape x2, local copies, waits for them, and re-layouts, pack(): split = array.reshape(2, half, groups, width)  0.89 us
  transfers between devices with their start and end apart: 5, of which 3 were waited for; matrix products, arithmetic and copies ran while one was open for 0% of the time, Pallas kernels for 14%

profile of v7, /device:TPU:0, one launch (start us, length us, event | category | flops | bytes accessed | tf_op | source)
XLA Modules:
  0.0 16.3 jit_solution(9585459907265900737)
XLA Ops:
  0.0 0.0 copy-start.2
  0.0 0.9 %copy.5 = bf16[2,64,2,128]{3,1,2,0:T(8,128)(2,1)S(1)} copy(bf16[2,64,2,128]{3,2,1,0:T(2,128)(2,1)} %bitcast.18) | data formatting | bytes 131072 | tf_op jit(solution)/shard_map/reshape | solution.py:281
  0.9 0.0 copy-done.2
  0.9 0.0 copy-start
  1.0 4.1 %collective-permute-start = (bf16[2,2,128,128]{3,2,1,0:T(8,128)(2,1)S(1)}, bf16[2,2,128,128]{3,2,1,0:T(8,128)(2,1)S(1)}, u32[]{:S(2)}, u32[]{:S(2)}) collective-permute-start(bf16[2,2,128,128]{3,2,1,0:T(8,128)(2,1)S(1)} %pad_maximum_fusion.refs_2_.rest_1_), channel_id=1, source_target_pairs={{0,8},{12,4},{4,0},{8,12},{1,9},{13,5},{5,1},{9,13},{2,10},{14,6},... | collective-permute-start | bytes 393224 | tf_op jit(solution)/shard_map/ppermute | solution.py:334
  5.1 0.0 collective-permute-start.4
  5.1 3.0 %collective-permute-start.3 = (bf16[2,1,128,128]{3,2,1,0:T(8,128)(2,1)S(1)}, bf16[2,1,128,128]{3,2,1,0:T(8,128)(2,1)S(1)}, u32[]{:S(2)}, u32[]{:S(2)}) collective-permute-start(bf16[2,1,128,128]{3,2,1,0:T(8,128)(2,1)S(1)} %bitcast.17), channel_id=1, source_target_pairs={{0,12},{12,0},{4,8},{8,4},{1,13},{13,1},{5,9},{9,5},{2,14},{14,2},... | collective-permute-start | bytes 196616 | tf_op jit(solution)/shard_map/ppermute | solution.py:334
  8.1 0.7 %collective-permute-start.2 = (bf16[2,1,128,128]{3,2,1,0:T(8,128)(2,1)S(1)}, bf16[2,1,128,128]{3,2,1,0:T(8,128)(2,1)S(1)}, u32[]{:S(2)}, u32[]{:S(2)}) collective-permute-start(bf16[2,1,128,128]{3,2,1,0:T(8,128)(2,1)S(1)} %bitcast.15), channel_id=1, source_target_pairs={{4,8},{8,4},{0,0},{12,12},{5,9},{9,5},{1,1},{13,13},{6,10},{10,6},... | collective-permute-start | bytes 196616 | tf_op jit(solution)/shard_map/ppermute | solution.py:334
  8.8 0.2 %collective-permute-done.rest_0_ = bf16[2,2,128,128]{3,2,1,0:T(8,128)(2,1)S(1)} collective-permute-done((bf16[2,2,128,128]{3,2,1,0:T(8,128)(2,1)S(1)}, bf16[2,2,128,128]{3,2,1,0:T(8,128)(2,1)S(1)}, u32[]{:S(2)}, u32[]{:S(2)}) %collective-permute-start) | collective-permute-done | bytes 131104 | tf_op jit(solution)/shard_map/ppermute | solution.py:334
  9.0 0.0 copy-start.1
  9.0 2.4 %collective-permute-start.1 = (bf16[2,1,128,128]{3,2,1,0:T(8,128)(2,1)S(1)}, bf16[2,1,128,128]{3,2,1,0:T(8,128)(2,1)S(1)}, u32[]{:S(2)}, u32[]{:S(2)}) collective-permute-start(bf16[2,1,128,128]{3,2,1,0:T(8,128)(2,1)S(1)} %slice.4), channel_id=1, source_target_pairs={{0,4},{4,0},{8,12},{12,8},{1,5},{5,1},{9,13},{13,9},{2,6},{6,2},{1... | collective-permute-start | bytes 196616 | tf_op jit(solution)/shard_map/ppermute | solution.py:334
  11.4 0.0 copy-done
  11.4 0.0 copy-done.1
  11.4 0.6 %shard_map.46 = (f32[2,1,512]{2,1,0:T(1,128)S(1)}, f32[2,1,512]{2,1,0:T(1,128)S(1)}, f32[2,128,512]{2,1,0:T(8,128)S(1)}, s32[8,128]{1,0:T(8,128)S(1)}) custom-call(s32[8]{0:T(128)S(1)} %copy-done.1, bf16[1024,128]{1,0:T(8,128)(2,1)S(1)} %bitcast.10, bf16[2,2,128,128]{3,2,1,0:T(8,128)(2,1)S(1)} %pad_maximum_fusion.refs_2_.rest_1_), custom_call_target="tpu_custom_call" | custom-call | flops 67108864 | bytes 262144 | tf_op jit(solution)/shard_map/pallas_call | solution.py:301
  12.0 0.6 %shard_map.47 = (f32[2,1,512]{2,1,0:T(1,128)S(1)}, f32[2,1,512]{2,1,0:T(1,128)S(1)}, f32[2,128,512]{2,1,0:T(8,128)S(1)}) custom-call(s32[8,128]{1,0:T(8,128)S(1)} %get-tuple-element.17.codes, bf16[1024,128]{1,0:T(8,128)(2,1)S(1)} %bitcast.11, bf16[2,2,128,128]{3,2,1,0:T(8,128)(2,1)S(1)} %collective-permute-done.rest_0_, ...), custom_call_target="tpu_custom_call" | custom-call | flops 100663296 | bytes 262144 | tf_op jit(solution)/shard_map/pallas_call | solution.py:301
  12.6 1.3 %collective-permute-done.4.rest_0_ = bf16[2,2,128,128]{3,2,1,0:T(8,128)(2,1)S(1)} collective-permute-done((bf16[2,2,128,128]{3,2,1,0:T(8,128)(2,1)S(1)}, bf16[2,2,128,128]{3,2,1,0:T(8,128)(2,1)S(1)}, u32[]{:S(2)}, u32[]{:S(2)}) %collective-permute-start.4) | collective-permute-done | bytes 131104 | tf_op jit(solution)/shard_map/ppermute | solution.py:334
  13.9 0.5 %shard_map.48 = (f32[2,1,512]{2,1,0:T(1,128)S(1)}, f32[2,1,512]{2,1,0:T(1,128)S(1)}, f32[2,128,512]{2,1,0:T(8,128)S(1)}) custom-call(s32[8,128]{1,0:T(8,128)S(1)} %get-tuple-element.17.codes, bf16[1024,128]{1,0:T(8,128)(2,1)S(1)} %bitcast.12, bf16[2,2,128,128]{3,2,1,0:T(8,128)(2,1)S(1)} %collective-permute-done.4.rest_0_, ...), custom_call_target="tpu_custom_call" | custom-call | flops 100663296 | bytes 262144 | tf_op jit(solution)/shard_map/pallas_call | solution.py:301
  14.4 0.2 %collective-permute-done.3.keys = bf16[2,1,128,128]{3,2,1,0:T(8,128)(2,1)S(1)} collective-permute-done((bf16[2,1,128,128]{3,2,1,0:T(8,128)(2,1)S(1)}, bf16[2,1,128,128]{3,2,1,0:T(8,128)(2,1)S(1)}, u32[]{:S(2)}, u32[]{:S(2)}) %collective-permute-start.3) | collective-permute-done | bytes 65568 | tf_op jit(solution)/shard_map/ppermute | solution.py:334
  14.6 0.6 %shard_map.49 = (bf16[2,512,128]{2,1,0:T(8,128)(2,1)S(1)}, f32[2,512,128]{2,1,0:T(8,128)S(1)}) custom-call(s32[8,128]{1,0:T(8,128)S(1)} %get-tuple-element.17.codes, bf16[1024,128]{1,0:T(8,128)(2,1)S(1)} %bitcast.13, bf16[2,1,128,128]{3,2,1,0:T(8,128)(2,1)S(1)} %collective-permute-done.3.keys, f32[2,1,512]{2,1,0:T(1,128)S(1)} %get-tuple-element.24.top, ...), custom_call_target="tpu_custom_call" | custom-call | flops 33554432 | bytes 262144 | tf_op jit(solution)/shard_map/pallas_call | solution.py:301
  15.3 0.0 collective-permute-done.2.far
  15.3 0.0 collective-permute-done.1.near
  15.3 1.0 %shard_map.50 = bf16[1024,128]{1,0:T(8,128)(2,1)} custom-call(s32[8,128]{1,0:T(8,128)S(1)} %get-tuple-element.17.codes, bf16[2,1,128,128]{3,2,1,0:T(8,128)(2,1)S(1)} %collective-permute-done.1.near, bf16[2,1,128,128]{3,2,1,0:T(8,128)(2,1)S(1)} %collective-permute-done.2.far, bf16[2,512,128]{2,1,0:T(8,128)(2,1)S(1)} %get-tuple-element.27.spread, ...), custom_call_target="tpu_custom_call" | custom-call | flops 33554432 | bytes 262144 | tf_op jit(solution)/shard_map/pallas_call | solution.py:301
  (3 shorter events, 0.0 us)
Async XLA Ops:
  0.0 0.9 %copy-start.2 = (bf16[128,2,128]{2,1,0:T(2,128)(2,1)S(1)}, bf16[128,2,128]{2,1,0:T(2,128)(2,1)}, u32[]{:S(2)}) copy-start(bf16[128,2,128]{2,1,0:T(2,128)(2,1)} %param.6) | copy-start | bytes 196612
  0.9 10.5 %copy-start = (bf16[128,8,128]{2,1,0:T(8,128)(2,1)S(1)}, bf16[128,8,128]{2,1,0:T(8,128)(2,1)}, u32[]{:S(2)}) copy-start(bf16[128,8,128]{2,1,0:T(8,128)(2,1)} %param.4) | copy-start | bytes 786436
  1.0 8.0 %collective-permute-start = (bf16[2,2,128,128]{3,2,1,0:T(8,128)(2,1)S(1)}, bf16[2,2,128,128]{3,2,1,0:T(8,128)(2,1)S(1)}, u32[]{:S(2)}, u32[]{:S(2)}) collective-permute-start(bf16[2,2,128,128]{3,2,1,0:T(8,128)(2,1)S(1)} %pad_maximum_fusion.refs_2_.rest_1_), channel_id=1, source_target_pairs={{0,8},{12,4},{4,0},{8,12},{1,9},{13,5},{5,1},{9,13},{2,10},{14,6},... | collective-permute-start | bytes 393224 | tf_op jit(solution)/shard_map/ppermute | solution.py:334
  5.1 8.8 %collective-permute-start.4 = (bf16[2,2,128,128]{3,2,1,0:T(8,128)(2,1)S(1)}, bf16[2,2,128,128]{3,2,1,0:T(8,128)(2,1)S(1)}, u32[]{:S(2)}, u32[]{:S(2)}) collective-permute-start(bf16[2,2,128,128]{3,2,1,0:T(8,128)(2,1)S(1)} %pad_maximum_fusion.refs_2_.rest_1_), channel_id=1, source_target_pairs={{4,12},{8,0},{0,4},{12,8},{5,13},{9,1},{1,5},{13,9},{6,14},{10,2},... | collective-permute-start | bytes 393224 | tf_op jit(solution)/shard_map/ppermute | solution.py:334
  5.1 9.6 %collective-permute-start.3 = (bf16[2,1,128,128]{3,2,1,0:T(8,128)(2,1)S(1)}, bf16[2,1,128,128]{3,2,1,0:T(8,128)(2,1)S(1)}, u32[]{:S(2)}, u32[]{:S(2)}) collective-permute-start(bf16[2,1,128,128]{3,2,1,0:T(8,128)(2,1)S(1)} %bitcast.17), channel_id=1, source_target_pairs={{0,12},{12,0},{4,8},{8,4},{1,13},{13,1},{5,9},{9,5},{2,14},{14,2},... | collective-permute-start | bytes 196616 | tf_op jit(solution)/shard_map/ppermute | solution.py:334
  8.1 7.2 %collective-permute-start.2 = (bf16[2,1,128,128]{3,2,1,0:T(8,128)(2,1)S(1)}, bf16[2,1,128,128]{3,2,1,0:T(8,128)(2,1)S(1)}, u32[]{:S(2)}, u32[]{:S(2)}) collective-permute-start(bf16[2,1,128,128]{3,2,1,0:T(8,128)(2,1)S(1)} %bitcast.15), channel_id=1, source_target_pairs={{4,8},{8,4},{0,0},{12,12},{5,9},{9,5},{1,1},{13,13},{6,10},{10,6},... | collective-permute-start | bytes 196616 | tf_op jit(solution)/shard_map/ppermute | solution.py:334
  9.0 2.4 %copy-start.1 = (s32[8]{0:T(128)S(1)}, s32[8]{0:T(128)}, u32[]{:S(2)}) copy-start(s32[8]{0:T(128)} %refs_0_.1) | copy-start | bytes 100
  9.0 6.3 %collective-permute-start.1 = (bf16[2,1,128,128]{3,2,1,0:T(8,128)(2,1)S(1)}, bf16[2,1,128,128]{3,2,1,0:T(8,128)(2,1)S(1)}, u32[]{:S(2)}, u32[]{:S(2)}) collective-permute-start(bf16[2,1,128,128]{3,2,1,0:T(8,128)(2,1)S(1)} %slice.4), channel_id=1, source_target_pairs={{0,4},{4,0},{8,12},{12,8},{1,5},{5,1},{9,13},{13,9},{2,6},{6,2},{1... | collective-permute-start | bytes 196616 | tf_op jit(solution)/shard_map/ppermute | solution.py:334

commit v8 on v7

--- a/solution.py
+++ b/solution.py
@@ -206,7 +206,7 @@
         for slot in range(2):
             _, _, factor, weights = soften(parts[slot], lanes, load(refs, slot), True)
             spread[slot] = weights.T
-            base[slot] = (acc[slot] * factor).T
+            base[slot] = acc[slot] * factor
 
     @pl.when(before == 0)
     def _():
@@ -216,8 +216,8 @@
         half = weights.shape[0] // 2
         spread[0] = weights[:half].T
         spread[1] = weights[half:].T
-        base[late] = (acc[late] * factor).T
-        base[early] = (acc[early] * (1.0 / total[early])).T
+        base[late] = acc[late] * factor
+        base[early] = acc[early] * (1.0 / total[early])
 
 
 def values_kernel(number, lanes, scale, codes, near, far, spread, base, out, staged, done):
@@ -231,12 +231,12 @@
     @pl.when(before == 1)
     def _():
         for slot in range(2):
-            finish(base[slot] + times(slot, 1 - source_late), staged, out, slot, done)
+            finish(base[slot].T + times(slot, 1 - source_late), staged, out, slot, done)
 
     @pl.when(before == 0)
     def _():
-        finish(base[1 - late], staged, out, 1 - late, done)
-        finish(base[late] + times(0, 0) + times(1, 1), staged, out, late, done)
+        finish(base[1 - late].T, staged, out, 1 - late, done)
+        finish(base[late].T + times(0, 0) + times(1, 1), staged, out, late, done)
 
     settle(staged, out, done)
 
@@ -340,9 +340,8 @@
             state = call(kernel, 3, inputs, [], shapes, [vmem] * 3)
         kernel = functools.partial(weights_kernel, len(WHOLE))
         spread = jax.ShapeDtypeStruct((2, rows // 2, groups * half), jnp.bfloat16)
-        base = jax.ShapeDtypeStruct((2, rows // 2, width), jnp.float32)
         inputs = [codes, query, got[LAST_KEYS], *state]
-        state = call(kernel, 1, inputs, [], [spread, base], [vmem] * 2)
+        state = call(kernel, 1, inputs, [], [spread, shapes[2]], [vmem] * 2)
         kernel = functools.partial(values_kernel, len(WHOLE))
         inputs = [codes, *[got[name] for name in LAST_VALUES], *state]
         out = call(kernel, 1, inputs, [], result, anywhere, staging)

time: 16.4 us -> 16.3 us (level)
  no operation moved by 1% of the time
where the time goes in v8:
time: 16.3 us; the launch traced here: 16.2 us
  starting transfers between devices  10.2 us (63%)
  Pallas kernels  3.19 us (20%)
  waiting for transfers between devices  1.71 us (10%)
  local copies, waits for them, and re-layouts  0.91 us (6%)
    ppermute x5, starting transfers between devices, on_device(): got[name] = lax.ppermute(value, 'seq', pairs)  10.2 us
    pallas_call x5, Pallas kernels, call(): pl.pallas_call(functools.partial(kernel, lanes, scale), out_shape=out_sha...  3.19 us
    ppermute x5, waiting for transfers between devices, on_device(): got[name] = lax.ppermute(value, 'seq', pairs)  1.71 us
    reshape x2, local copies, waits for them, and re-layouts, pack(): split = array.reshape(2, half, groups, width)  0.89 us
  transfers between devices with their start and end apart: 5, of which 3 were waited for; matrix products, arithmetic and copies ran while one was open for 0% of the time, Pallas kernels for 14%

profile of v8, /device:TPU:0, one launch (start us, length us, event | category | flops | bytes accessed | tf_op | source)
XLA Modules:
  0.0 16.2 jit_solution(6664133785970793648)
XLA Ops:
  0.0 0.0 copy-start.2
  0.0 0.9 %copy.5 = bf16[2,64,2,128]{3,1,2,0:T(8,128)(2,1)S(1)} copy(bf16[2,64,2,128]{3,2,1,0:T(2,128)(2,1)} %bitcast.18) | data formatting | bytes 131072 | tf_op jit(solution)/shard_map/reshape | solution.py:281
  0.9 0.0 copy-done.2
  0.9 0.0 copy-start
  1.0 4.1 %collective-permute-start = (bf16[2,2,128,128]{3,2,1,0:T(8,128)(2,1)S(1)}, bf16[2,2,128,128]{3,2,1,0:T(8,128)(2,1)S(1)}, u32[]{:S(2)}, u32[]{:S(2)}) collective-permute-start(bf16[2,2,128,128]{3,2,1,0:T(8,128)(2,1)S(1)} %pad_maximum_fusion.refs_2_.rest_1_), channel_id=1, source_target_pairs={{0,8},{12,4},{4,0},{8,12},{1,9},{13,5},{5,1},{9,13},{2,10},{14,6},... | collective-permute-start | bytes 393224 | tf_op jit(solution)/shard_map/ppermute | solution.py:334
  5.1 0.0 collective-permute-start.4
  5.1 3.0 %collective-permute-start.3 = (bf16[2,1,128,128]{3,2,1,0:T(8,128)(2,1)S(1)}, bf16[2,1,128,128]{3,2,1,0:T(8,128)(2,1)S(1)}, u32[]{:S(2)}, u32[]{:S(2)}) collective-permute-start(bf16[2,1,128,128]{3,2,1,0:T(8,128)(2,1)S(1)} %bitcast.17), channel_id=1, source_target_pairs={{0,12},{12,0},{4,8},{8,4},{1,13},{13,1},{5,9},{9,5},{2,14},{14,2},... | collective-permute-start | bytes 196616 | tf_op jit(solution)/shard_map/ppermute | solution.py:334
  8.1 0.7 %collective-permute-start.2 = (bf16[2,1,128,128]{3,2,1,0:T(8,128)(2,1)S(1)}, bf16[2,1,128,128]{3,2,1,0:T(8,128)(2,1)S(1)}, u32[]{:S(2)}, u32[]{:S(2)}) collective-permute-start(bf16[2,1,128,128]{3,2,1,0:T(8,128)(2,1)S(1)} %bitcast.15), channel_id=1, source_target_pairs={{4,8},{8,4},{0,0},{12,12},{5,9},{9,5},{1,1},{13,13},{6,10},{10,6},... | collective-permute-start | bytes 196616 | tf_op jit(solution)/shard_map/ppermute | solution.py:334
  8.8 0.2 %collective-permute-done.rest_0_ = bf16[2,2,128,128]{3,2,1,0:T(8,128)(2,1)S(1)} collective-permute-done((bf16[2,2,128,128]{3,2,1,0:T(8,128)(2,1)S(1)}, bf16[2,2,128,128]{3,2,1,0:T(8,128)(2,1)S(1)}, u32[]{:S(2)}, u32[]{:S(2)}) %collective-permute-start) | collective-permute-done | bytes 131104 | tf_op jit(solution)/shard_map/ppermute | solution.py:334
  9.0 0.0 copy-start.1
  9.0 2.4 %collective-permute-start.1 = (bf16[2,1,128,128]{3,2,1,0:T(8,128)(2,1)S(1)}, bf16[2,1,128,128]{3,2,1,0:T(8,128)(2,1)S(1)}, u32[]{:S(2)}, u32[]{:S(2)}) collective-permute-start(bf16[2,1,128,128]{3,2,1,0:T(8,128)(2,1)S(1)} %slice.4), channel_id=1, source_target_pairs={{0,4},{4,0},{8,12},{12,8},{1,5},{5,1},{9,13},{13,9},{2,6},{6,2},{1... | collective-permute-start | bytes 196616 | tf_op jit(solution)/shard_map/ppermute | solution.py:334
  11.4 0.0 copy-done
  11.4 0.0 copy-done.1
  11.4 0.6 %shard_map.46 = (f32[2,1,512]{2,1,0:T(1,128)S(1)}, f32[2,1,512]{2,1,0:T(1,128)S(1)}, f32[2,128,512]{2,1,0:T(8,128)S(1)}, s32[8,128]{1,0:T(8,128)S(1)}) custom-call(s32[8]{0:T(128)S(1)} %copy-done.1, bf16[1024,128]{1,0:T(8,128)(2,1)S(1)} %bitcast.10, bf16[2,2,128,128]{3,2,1,0:T(8,128)(2,1)S(1)} %pad_maximum_fusion.refs_2_.rest_1_), custom_call_target="tpu_custom_call" | custom-call | flops 67108864 | bytes 262144 | tf_op jit(solution)/shard_map/pallas_call | solution.py:301
  12.0 0.6 %shard_map.47 = (f32[2,1,512]{2,1,0:T(1,128)S(1)}, f32[2,1,512]{2,1,0:T(1,128)S(1)}, f32[2,128,512]{2,1,0:T(8,128)S(1)}) custom-call(s32[8,128]{1,0:T(8,128)S(1)} %get-tuple-element.17.codes, bf16[1024,128]{1,0:T(8,128)(2,1)S(1)} %bitcast.11, bf16[2,2,128,128]{3,2,1,0:T(8,128)(2,1)S(1)} %collective-permute-done.rest_0_, ...), custom_call_target="tpu_custom_call" | custom-call | flops 100663296 | bytes 262144 | tf_op jit(solution)/shard_map/pallas_call | solution.py:301
  12.6 1.3 %collective-permute-done.4.rest_0_ = bf16[2,2,128,128]{3,2,1,0:T(8,128)(2,1)S(1)} collective-permute-done((bf16[2,2,128,128]{3,2,1,0:T(8,128)(2,1)S(1)}, bf16[2,2,128,128]{3,2,1,0:T(8,128)(2,1)S(1)}, u32[]{:S(2)}, u32[]{:S(2)}) %collective-permute-start.4) | collective-permute-done | bytes 131104 | tf_op jit(solution)/shard_map/ppermute | solution.py:334
  13.9 0.5 %shard_map.48 = (f32[2,1,512]{2,1,0:T(1,128)S(1)}, f32[2,1,512]{2,1,0:T(1,128)S(1)}, f32[2,128,512]{2,1,0:T(8,128)S(1)}) custom-call(s32[8,128]{1,0:T(8,128)S(1)} %get-tuple-element.17.codes, bf16[1024,128]{1,0:T(8,128)(2,1)S(1)} %bitcast.12, bf16[2,2,128,128]{3,2,1,0:T(8,128)(2,1)S(1)} %collective-permute-done.4.rest_0_, ...), custom_call_target="tpu_custom_call" | custom-call | flops 100663296 | bytes 262144 | tf_op jit(solution)/shard_map/pallas_call | solution.py:301
  14.4 0.2 %collective-permute-done.3.keys = bf16[2,1,128,128]{3,2,1,0:T(8,128)(2,1)S(1)} collective-permute-done((bf16[2,1,128,128]{3,2,1,0:T(8,128)(2,1)S(1)}, bf16[2,1,128,128]{3,2,1,0:T(8,128)(2,1)S(1)}, u32[]{:S(2)}, u32[]{:S(2)}) %collective-permute-start.3) | collective-permute-done | bytes 65568 | tf_op jit(solution)/shard_map/ppermute | solution.py:334
  14.6 0.5 %shard_map.49 = (bf16[2,512,128]{2,1,0:T(8,128)(2,1)S(1)}, f32[2,128,512]{2,1,0:T(8,128)S(1)}) custom-call(s32[8,128]{1,0:T(8,128)S(1)} %get-tuple-element.17.codes, bf16[1024,128]{1,0:T(8,128)(2,1)S(1)} %bitcast.13, bf16[2,1,128,128]{3,2,1,0:T(8,128)(2,1)S(1)} %collective-permute-done.3.keys, f32[2,1,512]{2,1,0:T(1,128)S(1)} %get-tuple-element.24.top, ...), custom_call_target="tpu_custom_call" | custom-call | flops 33554432 | bytes 262144 | tf_op jit(solution)/shard_map/pallas_call | solution.py:301
  15.1 0.0 collective-permute-done.2.far
  15.1 0.0 collective-permute-done.1.near
  15.2 1.0 %shard_map.50 = bf16[1024,128]{1,0:T(8,128)(2,1)} custom-call(s32[8,128]{1,0:T(8,128)S(1)} %get-tuple-element.17.codes, bf16[2,1,128,128]{3,2,1,0:T(8,128)(2,1)S(1)} %collective-permute-done.1.near, bf16[2,1,128,128]{3,2,1,0:T(8,128)(2,1)S(1)} %collective-permute-done.2.far, bf16[2,512,128]{2,1,0:T(8,128)(2,1)S(1)} %get-tuple-element.27.spread, ...), custom_call_target="tpu_custom_call" | custom-call | flops 33554432 | bytes 262144 | tf_op jit(solution)/shard_map/pallas_call | solution.py:301
  (3 shorter events, 0.0 us)
Async XLA Ops:
  0.0 0.9 %copy-start.2 = (bf16[128,2,128]{2,1,0:T(2,128)(2,1)S(1)}, bf16[128,2,128]{2,1,0:T(2,128)(2,1)}, u32[]{:S(2)}) copy-start(bf16[128,2,128]{2,1,0:T(2,128)(2,1)} %param.6) | copy-start | bytes 196612
  0.9 10.5 %copy-start = (bf16[128,8,128]{2,1,0:T(8,128)(2,1)S(1)}, bf16[128,8,128]{2,1,0:T(8,128)(2,1)}, u32[]{:S(2)}) copy-start(bf16[128,8,128]{2,1,0:T(8,128)(2,1)} %param.4) | copy-start | bytes 786436
  1.0 8.0 %collective-permute-start = (bf16[2,2,128,128]{3,2,1,0:T(8,128)(2,1)S(1)}, bf16[2,2,128,128]{3,2,1,0:T(8,128)(2,1)S(1)}, u32[]{:S(2)}, u32[]{:S(2)}) collective-permute-start(bf16[2,2,128,128]{3,2,1,0:T(8,128)(2,1)S(1)} %pad_maximum_fusion.refs_2_.rest_1_), channel_id=1, source_target_pairs={{0,8},{12,4},{4,0},{8,12},{1,9},{13,5},{5,1},{9,13},{2,10},{14,6},... | collective-permute-start | bytes 393224 | tf_op jit(solution)/shard_map/ppermute | solution.py:334
  5.1 8.8 %collective-permute-start.4 = (bf16[2,2,128,128]{3,2,1,0:T(8,128)(2,1)S(1)}, bf16[2,2,128,128]{3,2,1,0:T(8,128)(2,1)S(1)}, u32[]{:S(2)}, u32[]{:S(2)}) collective-permute-start(bf16[2,2,128,128]{3,2,1,0:T(8,128)(2,1)S(1)} %pad_maximum_fusion.refs_2_.rest_1_), channel_id=1, source_target_pairs={{4,12},{8,0},{0,4},{12,8},{5,13},{9,1},{1,5},{13,9},{6,14},{10,2},... | collective-permute-start | bytes 393224 | tf_op jit(solution)/shard_map/ppermute | solution.py:334
  5.1 9.6 %collective-permute-start.3 = (bf16[2,1,128,128]{3,2,1,0:T(8,128)(2,1)S(1)}, bf16[2,1,128,128]{3,2,1,0:T(8,128)(2,1)S(1)}, u32[]{:S(2)}, u32[]{:S(2)}) collective-permute-start(bf16[2,1,128,128]{3,2,1,0:T(8,128)(2,1)S(1)} %bitcast.17), channel_id=1, source_target_pairs={{0,12},{12,0},{4,8},{8,4},{1,13},{13,1},{5,9},{9,5},{2,14},{14,2},... | collective-permute-start | bytes 196616 | tf_op jit(solution)/shard_map/ppermute | solution.py:334
  8.1 7.0 %collective-permute-start.2 = (bf16[2,1,128,128]{3,2,1,0:T(8,128)(2,1)S(1)}, bf16[2,1,128,128]{3,2,1,0:T(8,128)(2,1)S(1)}, u32[]{:S(2)}, u32[]{:S(2)}) collective-permute-start(bf16[2,1,128,128]{3,2,1,0:T(8,128)(2,1)S(1)} %bitcast.15), channel_id=1, source_target_pairs={{4,8},{8,4},{0,0},{12,12},{5,9},{9,5},{1,1},{13,13},{6,10},{10,6},... | collective-permute-start | bytes 196616 | tf_op jit(solution)/shard_map/ppermute | solution.py:334
  9.0 2.4 %copy-start.1 = (s32[8]{0:T(128)S(1)}, s32[8]{0:T(128)}, u32[]{:S(2)}) copy-start(s32[8]{0:T(128)} %refs_0_.1) | copy-start | bytes 100
  9.0 6.2 %collective-permute-start.1 = (bf16[2,1,128,128]{3,2,1,0:T(8,128)(2,1)S(1)}, bf16[2,1,128,128]{3,2,1,0:T(8,128)(2,1)S(1)}, u32[]{:S(2)}, u32[]{:S(2)}) collective-permute-start(bf16[2,1,128,128]{3,2,1,0:T(8,128)(2,1)S(1)} %slice.4), channel_id=1, source_target_pairs={{0,4},{4,0},{8,12},{12,8},{1,5},{5,1},{9,13},{13,9},{2,6},{6,2},{1... | collective-permute-start | bytes 196616 | tf_op jit(solution)/shard_map/ppermute | solution.py:334

commit v9 on v6

--- a/solution.py
+++ b/solution.py
@@ -271,6 +271,30 @@
     settle(staged, out, done)
 
 
+def together_kernel(keys, values, out, done):
+    copies = []
+    for which, source in enumerate((keys, values)):
+        copies.append(pltpu.make_async_copy(source, out.at[which], done.at[which]))
+        copies[-1].start()
+    for copy in copies:
+        copy.wait()
+
+
+def together(keys, values):
+    hbm = pl.BlockSpec(memory_space=pltpu.HBM)
+    return pl.pallas_call(
+        together_kernel,
+        out_shape=jax.ShapeDtypeStruct((2, *keys.shape), keys.dtype),
+        in_specs=[hbm, hbm],
+        out_specs=pl.BlockSpec(memory_space=pltpu.VMEM),
+        scratch_shapes=[pltpu.SemaphoreType.DMA((2,))],
+        compiler_params=pltpu.CompilerParams(vmem_limit_bytes=16 * 2**20),
+    )(
+        pltpu.with_memory_space_constraint(keys, pltpu.HBM),
+        pltpu.with_memory_space_constraint(values, pltpu.HBM),
+    )
+
+
 def on_device(queries, keys, values, block_order):
     tokens, heads, width = queries.shape
     groups = keys.shape[1]
@@ -281,12 +305,14 @@
     rows = tokens * heads
     query = queries.reshape(rows, width)
 
-    def pack(array):
-        split = array.reshape(2, half, groups, width)
-        return jnp.transpose(split, (0, 2, 1, 3)).reshape(2, 1, groups * half, width)
-
-    halves = {"keys": pack(keys), "values": pack(values)}
-    packed = jnp.concatenate([halves["keys"], halves["values"]], axis=1)
+    raw = together(keys, values)
+
+    def arrange(array):
+        split = array.reshape(array.shape[0], 2, half, groups, width)
+        turned = jnp.transpose(split, (1, 0, 3, 2, 4))
+        return turned.reshape(2, array.shape[0], groups * half, width)
+
+    packed = arrange(raw)
     shapes = [
         jax.ShapeDtypeStruct((2, 1, rows // 2), jnp.float32),
         jax.ShapeDtypeStruct((2, 1, rows // 2), jnp.float32),
@@ -322,32 +348,42 @@
 
         codes = jax.ShapeDtypeStruct((8, 128), jnp.int32)
         scratch = [pltpu.SMEM(block_order.shape, jnp.int32), pltpu.SemaphoreType.DMA]
-        inputs = [block_order, query, packed]
+        order = pltpu.with_memory_space_constraint(block_order, pltpu.HBM)
+        inputs = [order, query, packed]
         return call(kernel, 2, inputs, [anywhere], [*shapes, codes], [vmem] * 4, scratch)
 
     if devices == len(CHOICE):
         mine = tuple(range(devices))
-        held = {name: mine for name in ("packed", *halves)}
-        got = {"packed": packed, **halves}
+        got = {"packed": raw, "keys": raw[:1], "values": raw[1:]}
+        held = {name: mine for name in got}
         for name, sent, pairs in ROUTE:
             source = dict((target, origin) for origin, target in pairs)
             held[name] = tuple(held[sent][source[i]] for i in range(devices))
             value = got[sent]
-            if name in LAST_VALUES and value.shape[1] > 1:
-                value = value[:, 1:]
+            if name in LAST_VALUES and value.shape[0] > 1:
+                value = value[1:]
             got[name] = lax.ppermute(value, "seq", pairs)
+
+        def when(name, state):
+            value, state = lax.optimization_barrier((got[name], state))
+            return arrange(value), state
+
         *state, codes = diagonal([held[name] for name in (*WHOLE, LAST_KEYS)])
         for stage, name in enumerate(WHOLE):
-            blocks = [got[name]] if stage else [got[name], packed]
+            block, state = when(name, state)
+            blocks = [block] if stage else [block, packed]
             kernel = functools.partial(stage_kernel, stage)
             inputs = [codes, query, *blocks, *state]
             state = call(kernel, 3, inputs, [], shapes, [vmem] * 3)
         kernel = functools.partial(weights_kernel, len(WHOLE))
         spread = jax.ShapeDtypeStruct((2, groups * half, rows // 2), jnp.bfloat16)
-        inputs = [codes, query, got[LAST_KEYS], *state]
+        block, state = when(LAST_KEYS, state)
+        inputs = [codes, query, block, *state]
         state = call(kernel, 1, inputs, [], [spread, *shapes[1:]], [vmem] * 3)
         kernel = functools.partial(values_kernel, len(WHOLE))
-        inputs = [codes, *[got[name] for name in LAST_VALUES], *state]
+        near, state = when(LAST_VALUES[0], state)
+        far, state = when(LAST_VALUES[1], state)
+        inputs = [codes, near, far, *state]
         out = call(kernel, 1, inputs, [], result, anywhere, staging)
     else:
         blocks = lax.all_gather(packed, "seq", axis=0, tiled=False)

time: 16.4 us -> 16.3 us (level)
  Pallas kernels: 3.2 us -> 4.21 us
  local copies, waits for them, and re-layouts: 0.91 us -> 0.24 us
  waiting for transfers between devices: 1.77 us -> 1.25 us
    pallas_call x0 -> x1, Pallas kernels: none -> 0.89 us  [together(): pl.pallas_call(together_kernel, out_shape=jax.ShapeDtypeStruct((2, *keys....]
    reshape x2 -> x6, local copies, waits for them, and re-layouts: 0.89 us -> 0.09 us  [arrange(): split = array.reshape(array.shape[0], 2, half, groups, width)]
    ppermute x5, waiting for transfers between devices: 1.77 us -> 1.25 us  [on_device(): got[name] = lax.ppermute(value, 'seq', pairs)]
  transfers between devices with their start and end apart: 5 -> 5, of which waited for: 4 -> 3; matrix products, arithmetic and copies ran while one was open for 0% -> 1% of each run, Pallas kernels for 13% -> 14%
where the time goes in v9:
time: 16.3 us; the launch traced here: 16.1 us
  starting transfers between devices  10.3 us (63%)
  Pallas kernels  4.21 us (26%)
  waiting for transfers between devices  1.25 us (8%)
  local copies, waits for them, and re-layouts  0.24 us (1%)
    ppermute x5, starting transfers between devices, on_device(): got[name] = lax.ppermute(value, 'seq', pairs)  10.3 us
    pallas_call x5, Pallas kernels, call(): pl.pallas_call(functools.partial(kernel, lanes, scale), out_shape=out_sha...  3.33 us
    ppermute x5, waiting for transfers between devices, on_device(): got[name] = lax.ppermute(value, 'seq', pairs)  1.25 us
    pallas_call x1, Pallas kernels, together(): pl.pallas_call(together_kernel, out_shape=jax.ShapeDtypeStruct((2, *keys....  0.89 us
  transfers between devices with their start and end apart: 5, of which 3 were waited for; matrix products, arithmetic and copies ran while one was open for 1% of the time, Pallas kernels for 14%

profile of v9, /device:TPU:0, one launch (start us, length us, event | category | flops | bytes accessed | tf_op | source)
XLA Modules:
  0.0 16.1 jit_solution(6370280260557484522)
XLA Ops:
  0.0 0.9 %shard_map.46 = bf16[2,128,2,128]{3,2,1,0:T(2,128)(2,1)S(1)} custom-call(bf16[128,2,128]{2,1,0:T(2,128)(2,1)} %keys.1, bf16[128,2,128]{2,1,0:T(2,128)(2,1)} %values.1), custom_call_target="tpu_custom_call" | custom-call | tf_op jit(solution)/shard_map/pallas_call | solution.py:285
  0.9 4.1 %collective-permute-start = (bf16[2,128,2,128]{3,2,1,0:T(2,128)(2,1)S(1)}, bf16[2,128,2,128]{3,2,1,0:T(2,128)(2,1)S(1)}, u32[]{:S(2)}, u32[]{:S(2)}) collective-permute-start(bf16[2,128,2,128]{3,2,1,0:T(2,128)(2,1)S(1)} %shard_map.46), channel_id=1, source_target_pairs={{0,8},{12,4},{4,0},{8,12},{1,9},{13,5},{5,1},{9,13},{2,10},{14,6},... | collective-permute-start | bytes 393224 | tf_op jit(solution)/shard_map/ppermute | solution.py:365
  5.0 0.0 collective-permute-start.3
  5.0 0.1 fusion
  5.1 0.0 copy-start
  5.1 3.1 %collective-permute-start.2 = (bf16[1,128,2,128]{3,2,1,0:T(2,128)(2,1)S(1)}, bf16[1,128,2,128]{3,2,1,0:T(2,128)(2,1)S(1)}, u32[]{:S(2)}, u32[]{:S(2)}) collective-permute-start(bf16[1,128,2,128]{3,2,1,0:T(2,128)(2,1)S(1)} %get-tuple-element.72), channel_id=1, source_target_pairs={{0,12},{12,0},{4,8},{8,4},{1,13},{13,1},{5,9},{9,5},{2,14},{14,2},... | collective-permute-start | bytes 196616 | tf_op jit(solution)/shard_map/ppermute | solution.py:365
  8.2 0.7 %collective-permute-done = bf16[2,128,2,128]{3,2,1,0:T(2,128)(2,1)S(1)} collective-permute-done((bf16[2,128,2,128]{3,2,1,0:T(2,128)(2,1)S(1)}, bf16[2,128,2,128]{3,2,1,0:T(2,128)(2,1)S(1)}, u32[]{:S(2)}, u32[]{:S(2)}) %collective-permute-start) | collective-permute-done | bytes 131104 | tf_op jit(solution)/shard_map/ppermute | solution.py:365
  8.9 2.4 %collective-permute-start.1 = (bf16[1,128,2,128]{3,2,1,0:T(2,128)(2,1)S(1)}, bf16[1,128,2,128]{3,2,1,0:T(2,128)(2,1)S(1)}, u32[]{:S(2)}, u32[]{:S(2)}) collective-permute-start(bf16[1,128,2,128]{3,2,1,0:T(2,128)(2,1)S(1)} %slice.12), channel_id=1, source_target_pairs={{0,4},{4,0},{8,12},{12,8},{1,5},{5,1},{9,13},{13,9},{2,6},{6,2},{1... | collective-permute-start | bytes 196616 | tf_op jit(solution)/shard_map/ppermute | solution.py:365
  11.4 0.7 %collective-permute-start.4 = (bf16[1,128,2,128]{3,2,1,0:T(2,128)(2,1)S(1)}, bf16[1,128,2,128]{3,2,1,0:T(2,128)(2,1)S(1)}, u32[]{:S(2)}, u32[]{:S(2)}) collective-permute-start(bf16[1,128,2,128]{3,2,1,0:T(2,128)(2,1)S(1)} %get-tuple-element.71), channel_id=1, source_target_pairs={{4,8},{8,4},{0,0},{12,12},{5,9},{9,5},{1,1},{13,13},{6,10},{10,6},... | collective-permute-start | bytes 196616 | tf_op jit(solution)/shard_map/ppermute | solution.py:365
  12.1 0.0 copy-done
  12.1 0.7 %shard_map.47 = (f32[2,1,512]{2,1,0:T(1,128)S(1)}, f32[2,1,512]{2,1,0:T(1,128)S(1)}, f32[2,128,512]{2,1,0:T(8,128)S(1)}, s32[8,128]{1,0:T(8,128)S(1)}) custom-call(s32[8]{0:T(128)} %refs_0_.1, bf16[1024,128]{1,0:T(8,128)(2,1)S(1)} %bitcast.26, bf16[2,2,128,128]{3,2,1,0:T(8,128)(2,1)S(1)} %bitcast.31), custom_call_target="tpu_custom_call" | custom-call | flops 67108864 | bytes 262144 | tf_op jit(solution)/shard_map/pallas_call | solution.py:331
  12.8 0.6 %shard_map.48 = (f32[2,1,512]{2,1,0:T(1,128)S(1)}, f32[2,1,512]{2,1,0:T(1,128)S(1)}, f32[2,128,512]{2,1,0:T(8,128)S(1)}) custom-call(s32[8,128]{1,0:T(8,128)S(1)} %get-tuple-element.38.codes, bf16[1024,128]{1,0:T(8,128)(2,1)S(1)} %bitcast.27, bf16[2,2,128,128]{3,2,1,0:T(8,128)(2,1)S(1)} %bitcast.34, bf16[2,2,128,128]{3,2,1,0:T(8,128)(2,1)S(1)} %bitcast.32, ...), custom_call_target="tpu_custom_call" | custom-call | flops 100663296 | bytes 262144 | tf_op jit(solution)/shard_map/pallas_call | solution.py:331
  13.5 0.3 %collective-permute-done.3 = bf16[2,128,2,128]{3,2,1,0:T(2,128)(2,1)S(1)} collective-permute-done((bf16[2,128,2,128]{3,2,1,0:T(2,128)(2,1)S(1)}, bf16[2,128,2,128]{3,2,1,0:T(2,128)(2,1)S(1)}, u32[]{:S(2)}, u32[]{:S(2)}) %collective-permute-start.3) | collective-permute-done | bytes 131104 | tf_op jit(solution)/shard_map/ppermute | solution.py:365
  13.8 0.5 %shard_map.49 = (f32[2,1,512]{2,1,0:T(1,128)S(1)}, f32[2,1,512]{2,1,0:T(1,128)S(1)}, f32[2,128,512]{2,1,0:T(8,128)S(1)}) custom-call(s32[8,128]{1,0:T(8,128)S(1)} %get-tuple-element.38.codes, bf16[1024,128]{1,0:T(8,128)(2,1)S(1)} %bitcast.28, bf16[2,2,128,128]{3,2,1,0:T(8,128)(2,1)S(1)} %bitcast.33, f32[2,1,512]{2,1,0:T(1,128)S(1)} %get-tuple-element.50.rest_1_, ...), custom_call_target="tpu_custom_call" | custom-call | flops 100663296 | bytes 262144 | tf_op jit(solution)/shard_map/pallas_call | solution.py:331
  14.3 0.3 %collective-permute-done.2 = bf16[1,128,2,128]{3,2,1,0:T(2,128)(2,1)S(1)} collective-permute-done((bf16[1,128,2,128]{3,2,1,0:T(2,128)(2,1)S(1)}, bf16[1,128,2,128]{3,2,1,0:T(2,128)(2,1)S(1)}, u32[]{:S(2)}, u32[]{:S(2)}) %collective-permute-start.2) | collective-permute-done | bytes 65568 | tf_op jit(solution)/shard_map/ppermute | solution.py:365
  14.6 0.4 %shard_map.50 = (bf16[2,128,512]{2,1,0:T(8,128)(2,1)S(1)}, f32[2,1,512]{2,1,0:T(1,128)S(1)}, f32[2,128,512]{2,1,0:T(8,128)S(1)}) custom-call(s32[8,128]{1,0:T(8,128)S(1)} %get-tuple-element.38.codes, bf16[1024,128]{1,0:T(8,128)(2,1)S(1)} %bitcast.29, bf16[2,1,128,128]{3,2,1,0:T(8,128)(2,1)S(1)} %bitcast.37, f32[2,1,512]{2,1,0:T(1,128)S(1)} %get-tuple-element.57.top, ...), custom_call_target="tpu_custom_call" | custom-call | flops 33554432 | bytes 262144 | tf_op jit(solution)/shard_map/pallas_call | solution.py:331
  15.0 0.0 collective-permute-done.1
  15.0 0.0 collective-permute-done.4
  15.1 1.1 %shard_map.51 = bf16[1024,128]{1,0:T(8,128)(2,1)} custom-call(s32[8,128]{1,0:T(8,128)S(1)} %get-tuple-element.38.codes, bf16[2,1,128,128]{3,2,1,0:T(8,128)(2,1)S(1)} %bitcast.36, bf16[2,1,128,128]{3,2,1,0:T(8,128)(2,1)S(1)} %bitcast.35, bf16[2,128,512]{2,1,0:T(8,128)(2,1)S(1)} %get-tuple-element.68.spread, f32[2,1,512]{2,1,0:T(1,128)S(1)} %get-tuple-element.69.share, ...), custom_call_target="tpu_custom_call" | custom-call | flops 33554432 | bytes 262144 | tf_op jit(solution)/shard_map/pallas_call | solution.py:331
  (7 shorter events, 0.1 us)
Async XLA Ops:
  0.9 8.0 %collective-permute-start = (bf16[2,128,2,128]{3,2,1,0:T(2,128)(2,1)S(1)}, bf16[2,128,2,128]{3,2,1,0:T(2,128)(2,1)S(1)}, u32[]{:S(2)}, u32[]{:S(2)}) collective-permute-start(bf16[2,128,2,128]{3,2,1,0:T(2,128)(2,1)S(1)} %shard_map.46), channel_id=1, source_target_pairs={{0,8},{12,4},{4,0},{8,12},{1,9},{13,5},{5,1},{9,13},{2,10},{14,6},... | collective-permute-start | bytes 393224 | tf_op jit(solution)/shard_map/ppermute | solution.py:365
  5.0 8.8 %collective-permute-start.3 = (bf16[2,128,2,128]{3,2,1,0:T(2,128)(2,1)S(1)}, bf16[2,128,2,128]{3,2,1,0:T(2,128)(2,1)S(1)}, u32[]{:S(2)}, u32[]{:S(2)}) collective-permute-start(bf16[2,128,2,128]{3,2,1,0:T(2,128)(2,1)S(1)} %shard_map.46), channel_id=1, source_target_pairs={{4,12},{8,0},{0,4},{12,8},{5,13},{9,1},{1,5},{13,9},{6,14},{10,2},... | collective-permute-start | bytes 393224 | tf_op jit(solution)/shard_map/ppermute | solution.py:365
  5.1 7.0 %copy-start = (bf16[128,8,128]{2,1,0:T(8,128)(2,1)S(1)}, bf16[128,8,128]{2,1,0:T(8,128)(2,1)}, u32[]{:S(2)}) copy-start(bf16[128,8,128]{2,1,0:T(8,128)(2,1)} %param.4) | copy-start | bytes 786436
  5.1 9.5 %collective-permute-start.2 = (bf16[1,128,2,128]{3,2,1,0:T(2,128)(2,1)S(1)}, bf16[1,128,2,128]{3,2,1,0:T(2,128)(2,1)S(1)}, u32[]{:S(2)}, u32[]{:S(2)}) collective-permute-start(bf16[1,128,2,128]{3,2,1,0:T(2,128)(2,1)S(1)} %get-tuple-element.72), channel_id=1, source_target_pairs={{0,12},{12,0},{4,8},{8,4},{1,13},{13,1},{5,9},{9,5},{2,14},{14,2},... | collective-permute-start | bytes 196616 | tf_op jit(solution)/shard_map/ppermute | solution.py:365
  8.9 6.1 %collective-permute-start.1 = (bf16[1,128,2,128]{3,2,1,0:T(2,128)(2,1)S(1)}, bf16[1,128,2,128]{3,2,1,0:T(2,128)(2,1)S(1)}, u32[]{:S(2)}, u32[]{:S(2)}) collective-permute-start(bf16[1,128,2,128]{3,2,1,0:T(2,128)(2,1)S(1)} %slice.12), channel_id=1, source_target_pairs={{0,4},{4,0},{8,12},{12,8},{1,5},{5,1},{9,13},{13,9},{2,6},{6,2},{1... | collective-permute-start | bytes 196616 | tf_op jit(solution)/shard_map/ppermute | solution.py:365
  11.4 3.6 %collective-permute-start.4 = (bf16[1,128,2,128]{3,2,1,0:T(2,128)(2,1)S(1)}, bf16[1,128,2,128]{3,2,1,0:T(2,128)(2,1)S(1)}, u32[]{:S(2)}, u32[]{:S(2)}) collective-permute-start(bf16[1,128,2,128]{3,2,1,0:T(2,128)(2,1)S(1)} %get-tuple-element.71), channel_id=1, source_target_pairs={{4,8},{8,4},{0,0},{12,12},{5,9},{9,5},{1,1},{13,13},{6,10},{10,6},... | collective-permute-start | bytes 196616 | tf_op jit(solution)/shard_map/ppermute | solution.py:365

commit v10 on v9

--- a/solution.py
+++ b/solution.py
@@ -271,10 +271,11 @@
     settle(staged, out, done)
 
 
-def together_kernel(keys, values, out, done):
+def together_kernel(keys, values, out, first, second, done):
     copies = []
-    for which, source in enumerate((keys, values)):
-        copies.append(pltpu.make_async_copy(source, out.at[which], done.at[which]))
+    pairs = ((keys, out.at[0]), (values, out.at[1]), (keys, first.at[0]), (values, second.at[0]))
+    for which, (source, target) in enumerate(pairs):
+        copies.append(pltpu.make_async_copy(source, target, done.at[which]))
         copies[-1].start()
     for copy in copies:
         copy.wait()
@@ -284,10 +285,10 @@
     hbm = pl.BlockSpec(memory_space=pltpu.HBM)
     return pl.pallas_call(
         together_kernel,
-        out_shape=jax.ShapeDtypeStruct((2, *keys.shape), keys.dtype),
+        out_shape=[jax.ShapeDtypeStruct((n, *keys.shape), keys.dtype) for n in (2, 1, 1)],
         in_specs=[hbm, hbm],
-        out_specs=pl.BlockSpec(memory_space=pltpu.VMEM),
-        scratch_shapes=[pltpu.SemaphoreType.DMA((2,))],
+        out_specs=[pl.BlockSpec(memory_space=pltpu.VMEM)] * 3,
+        scratch_shapes=[pltpu.SemaphoreType.DMA((4,))],
         compiler_params=pltpu.CompilerParams(vmem_limit_bytes=16 * 2**20),
     )(
         pltpu.with_memory_space_constraint(keys, pltpu.HBM),
@@ -305,7 +306,7 @@
     rows = tokens * heads
     query = queries.reshape(rows, width)
 
-    raw = together(keys, values)
+    raw, raw_keys, raw_values = together(keys, values)
 
     def arrange(array):
         split = array.reshape(array.shape[0], 2, half, groups, width)
@@ -354,7 +355,7 @@
 
     if devices == len(CHOICE):
         mine = tuple(range(devices))
-        got = {"packed": raw, "keys": raw[:1], "values": raw[1:]}
+        got = {"packed": raw, "keys": raw_keys, "values": raw_values}
         held = {name: mine for name in got}
         for name, sent, pairs in ROUTE:
             source = dict((target, origin) for origin, target in pairs)

time: 16.3 us -> 16.4 us (level)
  waiting for transfers between devices: 1.25 us -> 1.42 us
    ppermute x5, waiting for transfers between devices: 1.25 us -> 1.42 us  [on_device(): got[name] = lax.ppermute(value, 'seq', pairs)]
where the time goes in v10:
time: 16.4 us; the launch traced here: 16.3 us
  starting transfers between devices  10.2 us (62%)
  Pallas kernels  4.33 us (26%)
  waiting for transfers between devices  1.42 us (9%)
    ppermute x5, starting transfers between devices, on_device(): got[name] = lax.ppermute(value, 'seq', pairs)  10.2 us
    pallas_call x5, Pallas kernels, call(): pl.pallas_call(functools.partial(kernel, lanes, scale), out_shape=out_sha...  3.32 us
    ppermute x5, waiting for transfers between devices, on_device(): got[name] = lax.ppermute(value, 'seq', pairs)  1.42 us
    pallas_call x1, Pallas kernels, together(): pl.pallas_call(together_kernel, out_shape=[jax.ShapeDtypeStruct((n, *keys...  1.01 us
  transfers between devices with their start and end apart: 5, of which 3 were waited for; matrix products, arithmetic and copies ran while one was open for 1% of the time, Pallas kernels for 14%

profile of v10, /device:TPU:0, one launch (start us, length us, event | category | flops | bytes accessed | tf_op | source)
XLA Modules:
  0.0 16.3 jit_solution(17672389749334703399)
XLA Ops:
  0.0 0.0 copy-start
  0.0 1.0 %shard_map.46 = (bf16[2,128,2,128]{3,2,1,0:T(2,128)(2,1)S(1)}, bf16[1,128,2,128]{3,2,1,0:T(2,128)(2,1)S(1)}, bf16[1,128,2,128]{3,2,1,0:T(2,128)(2,1)S(1)}) custom-call(bf16[128,2,128]{2,1,0:T(2,128)(2,1)} %keys.1, bf16[128,2,128]{2,1,0:T(2,128)(2,1)} %values.1), custom_call_target="tpu_custom_call" | custom-call | tf_op jit(solution)/shard_map/pallas_call | solution.py:286
  1.0 4.1 %collective-permute-start = (bf16[2,128,2,128]{3,2,1,0:T(2,128)(2,1)S(1)}, bf16[2,128,2,128]{3,2,1,0:T(2,128)(2,1)S(1)}, u32[]{:S(2)}, u32[]{:S(2)}) collective-permute-start(bf16[2,128,2,128]{3,2,1,0:T(2,128)(2,1)S(1)} %get-tuple-element.41), channel_id=1, source_target_pairs={{0,8},{12,4},{4,0},{8,12},{1,9},{13,5},{5,1},{9,13},{2,10},{14,6},... | collective-permute-start | bytes 393224 | tf_op jit(solution)/shard_map/ppermute | solution.py:366
  5.1 0.0 collective-permute-start.3
  5.1 3.0 %collective-permute-start.2 = (bf16[1,128,2,128]{3,2,1,0:T(2,128)(2,1)S(1)}, bf16[1,128,2,128]{3,2,1,0:T(2,128)(2,1)S(1)}, u32[]{:S(2)}, u32[]{:S(2)}) collective-permute-start(bf16[1,128,2,128]{3,2,1,0:T(2,128)(2,1)S(1)} %get-tuple-element.43), channel_id=1, source_target_pairs={{0,12},{12,0},{4,8},{8,4},{1,13},{13,1},{5,9},{9,5},{2,14},{14,2},... | collective-permute-start | bytes 196616 | tf_op jit(solution)/shard_map/ppermute | solution.py:366
  8.2 0.8 %collective-permute-done = bf16[2,128,2,128]{3,2,1,0:T(2,128)(2,1)S(1)} collective-permute-done((bf16[2,128,2,128]{3,2,1,0:T(2,128)(2,1)S(1)}, bf16[2,128,2,128]{3,2,1,0:T(2,128)(2,1)S(1)}, u32[]{:S(2)}, u32[]{:S(2)}) %collective-permute-start) | collective-permute-done | bytes 131104 | tf_op jit(solution)/shard_map/ppermute | solution.py:366
  9.1 2.4 %collective-permute-start.1 = (bf16[1,128,2,128]{3,2,1,0:T(2,128)(2,1)S(1)}, bf16[1,128,2,128]{3,2,1,0:T(2,128)(2,1)S(1)}, u32[]{:S(2)}, u32[]{:S(2)}) collective-permute-start(bf16[1,128,2,128]{3,2,1,0:T(2,128)(2,1)S(1)} %slice.4), channel_id=1, source_target_pairs={{0,4},{4,0},{8,12},{12,8},{1,5},{5,1},{9,13},{13,9},{2,6},{6,2},{1... | collective-permute-start | bytes 196616 | tf_op jit(solution)/shard_map/ppermute | solution.py:366
  11.5 0.7 %collective-permute-start.4 = (bf16[1,128,2,128]{3,2,1,0:T(2,128)(2,1)S(1)}, bf16[1,128,2,128]{3,2,1,0:T(2,128)(2,1)S(1)}, u32[]{:S(2)}, u32[]{:S(2)}) collective-permute-start(bf16[1,128,2,128]{3,2,1,0:T(2,128)(2,1)S(1)} %get-tuple-element.69), channel_id=1, source_target_pairs={{4,8},{8,4},{0,0},{12,12},{5,9},{9,5},{1,1},{13,13},{6,10},{10,6},... | collective-permute-start | bytes 196616 | tf_op jit(solution)/shard_map/ppermute | solution.py:366
  12.2 0.0 copy-done
  12.2 0.7 %shard_map.47 = (f32[2,1,512]{2,1,0:T(1,128)S(1)}, f32[2,1,512]{2,1,0:T(1,128)S(1)}, f32[2,128,512]{2,1,0:T(8,128)S(1)}, s32[8,128]{1,0:T(8,128)S(1)}) custom-call(s32[8]{0:T(128)} %refs_0_.1, bf16[1024,128]{1,0:T(8,128)(2,1)S(1)} %bitcast.26, bf16[2,2,128,128]{3,2,1,0:T(8,128)(2,1)S(1)} %bitcast.30), custom_call_target="tpu_custom_call" | custom-call | flops 67108864 | bytes 262144 | tf_op jit(solution)/shard_map/pallas_call | solution.py:332
  13.0 0.6 %shard_map.48 = (f32[2,1,512]{2,1,0:T(1,128)S(1)}, f32[2,1,512]{2,1,0:T(1,128)S(1)}, f32[2,128,512]{2,1,0:T(8,128)S(1)}) custom-call(s32[8,128]{1,0:T(8,128)S(1)} %get-tuple-element.42.codes, bf16[1024,128]{1,0:T(8,128)(2,1)S(1)} %bitcast.27, bf16[2,2,128,128]{3,2,1,0:T(8,128)(2,1)S(1)} %bitcast.33, bf16[2,2,128,128]{3,2,1,0:T(8,128)(2,1)S(1)} %bitcast.31, ...), custom_call_target="tpu_custom_call" | custom-call | flops 100663296 | bytes 262144 | tf_op jit(solution)/shard_map/pallas_call | solution.py:332
  13.6 0.3 %collective-permute-done.3 = bf16[2,128,2,128]{3,2,1,0:T(2,128)(2,1)S(1)} collective-permute-done((bf16[2,128,2,128]{3,2,1,0:T(2,128)(2,1)S(1)}, bf16[2,128,2,128]{3,2,1,0:T(2,128)(2,1)S(1)}, u32[]{:S(2)}, u32[]{:S(2)}) %collective-permute-start.3) | collective-permute-done | bytes 131104 | tf_op jit(solution)/shard_map/ppermute | solution.py:366
  13.9 0.5 %shard_map.49 = (f32[2,1,512]{2,1,0:T(1,128)S(1)}, f32[2,1,512]{2,1,0:T(1,128)S(1)}, f32[2,128,512]{2,1,0:T(8,128)S(1)}) custom-call(s32[8,128]{1,0:T(8,128)S(1)} %get-tuple-element.42.codes, bf16[1024,128]{1,0:T(8,128)(2,1)S(1)} %bitcast.28, bf16[2,2,128,128]{3,2,1,0:T(8,128)(2,1)S(1)} %bitcast.32, f32[2,1,512]{2,1,0:T(1,128)S(1)} %get-tuple-element.55.rest_1_, ...), custom_call_target="tpu_custom_call" | custom-call | flops 100663296 | bytes 262144 | tf_op jit(solution)/shard_map/pallas_call | solution.py:332
  14.5 0.3 %collective-permute-done.2 = bf16[1,128,2,128]{3,2,1,0:T(2,128)(2,1)S(1)} collective-permute-done((bf16[1,128,2,128]{3,2,1,0:T(2,128)(2,1)S(1)}, bf16[1,128,2,128]{3,2,1,0:T(2,128)(2,1)S(1)}, u32[]{:S(2)}, u32[]{:S(2)}) %collective-permute-start.2) | collective-permute-done | bytes 65568 | tf_op jit(solution)/shard_map/ppermute | solution.py:366
  14.7 0.4 %shard_map.50 = (bf16[2,128,512]{2,1,0:T(8,128)(2,1)S(1)}, f32[2,1,512]{2,1,0:T(1,128)S(1)}, f32[2,128,512]{2,1,0:T(8,128)S(1)}) custom-call(s32[8,128]{1,0:T(8,128)S(1)} %get-tuple-element.42.codes, bf16[1024,128]{1,0:T(8,128)(2,1)S(1)} %bitcast.29, bf16[2,1,128,128]{3,2,1,0:T(8,128)(2,1)S(1)} %bitcast.36, f32[2,1,512]{2,1,0:T(1,128)S(1)} %get-tuple-element.62.top, ...), custom_call_target="tpu_custom_call" | custom-call | flops 33554432 | bytes 262144 | tf_op jit(solution)/shard_map/pallas_call | solution.py:332
  15.1 0.0 collective-permute-done.1
  15.2 0.0 collective-permute-done.4
  15.2 1.1 %shard_map.51 = bf16[1024,128]{1,0:T(8,128)(2,1)} custom-call(s32[8,128]{1,0:T(8,128)S(1)} %get-tuple-element.42.codes, bf16[2,1,128,128]{3,2,1,0:T(8,128)(2,1)S(1)} %bitcast.34, bf16[2,1,128,128]{3,2,1,0:T(8,128)(2,1)S(1)} %bitcast.35, bf16[2,128,512]{2,1,0:T(8,128)(2,1)S(1)} %get-tuple-element.74.spread, f32[2,1,512]{2,1,0:T(1,128)S(1)} %get-tuple-element.75.share, ...), custom_call_target="tpu_custom_call" | custom-call | flops 33554432 | bytes 262144 | tf_op jit(solution)/shard_map/pallas_call | solution.py:332
  (7 shorter events, 0.1 us)
Async XLA Ops:
  0.0 12.2 %copy-start = (bf16[128,8,128]{2,1,0:T(8,128)(2,1)S(1)}, bf16[128,8,128]{2,1,0:T(8,128)(2,1)}, u32[]{:S(2)}) copy-start(bf16[128,8,128]{2,1,0:T(8,128)(2,1)} %param.4) | copy-start | bytes 786436
  1.0 8.0 %collective-permute-start = (bf16[2,128,2,128]{3,2,1,0:T(2,128)(2,1)S(1)}, bf16[2,128,2,128]{3,2,1,0:T(2,128)(2,1)S(1)}, u32[]{:S(2)}, u32[]{:S(2)}) collective-permute-start(bf16[2,128,2,128]{3,2,1,0:T(2,128)(2,1)S(1)} %get-tuple-element.41), channel_id=1, source_target_pairs={{0,8},{12,4},{4,0},{8,12},{1,9},{13,5},{5,1},{9,13},{2,10},{14,6},... | collective-permute-start | bytes 393224 | tf_op jit(solution)/shard_map/ppermute | solution.py:366
  5.1 8.8 %collective-permute-start.3 = (bf16[2,128,2,128]{3,2,1,0:T(2,128)(2,1)S(1)}, bf16[2,128,2,128]{3,2,1,0:T(2,128)(2,1)S(1)}, u32[]{:S(2)}, u32[]{:S(2)}) collective-permute-start(bf16[2,128,2,128]{3,2,1,0:T(2,128)(2,1)S(1)} %get-tuple-element.41), channel_id=1, source_target_pairs={{4,12},{8,0},{0,4},{12,8},{5,13},{9,1},{1,5},{13,9},{6,14},{10,2},... | collective-permute-start | bytes 393224 | tf_op jit(solution)/shard_map/ppermute | solution.py:366
  5.1 9.6 %collective-permute-start.2 = (bf16[1,128,2,128]{3,2,1,0:T(2,128)(2,1)S(1)}, bf16[1,128,2,128]{3,2,1,0:T(2,128)(2,1)S(1)}, u32[]{:S(2)}, u32[]{:S(2)}) collective-permute-start(bf16[1,128,2,128]{3,2,1,0:T(2,128)(2,1)S(1)} %get-tuple-element.43), channel_id=1, source_target_pairs={{0,12},{12,0},{4,8},{8,4},{1,13},{13,1},{5,9},{9,5},{2,14},{14,2},... | collective-permute-start | bytes 196616 | tf_op jit(solution)/shard_map/ppermute | solution.py:366
  9.1 6.1 %collective-permute-start.1 = (bf16[1,128,2,128]{3,2,1,0:T(2,128)(2,1)S(1)}, bf16[1,128,2,128]{3,2,1,0:T(2,128)(2,1)S(1)}, u32[]{:S(2)}, u32[]{:S(2)}) collective-permute-start(bf16[1,128,2,128]{3,2,1,0:T(2,128)(2,1)S(1)} %slice.4), channel_id=1, source_target_pairs={{0,4},{4,0},{8,12},{12,8},{1,5},{5,1},{9,13},{13,9},{2,6},{6,2},{1... | collective-permute-start | bytes 196616 | tf_op jit(solution)/shard_map/ppermute | solution.py:366
  11.5 3.7 %collective-permute-start.4 = (bf16[1,128,2,128]{3,2,1,0:T(2,128)(2,1)S(1)}, bf16[1,128,2,128]{3,2,1,0:T(2,128)(2,1)S(1)}, u32[]{:S(2)}, u32[]{:S(2)}) collective-permute-start(bf16[1,128,2,128]{3,2,1,0:T(2,128)(2,1)S(1)} %get-tuple-element.69), channel_id=1, source_target_pairs={{4,8},{8,4},{0,0},{12,12},{5,9},{9,5},{1,1},{13,13},{6,10},{10,6},... | collective-permute-start | bytes 196616 | tf_op jit(solution)/shard_map/ppermute | solution.py:366
